TPU v7x, 512 devices: a whole 4x8x8 slice. The times are simulated.
512 devices in a mesh: pop: 16 (over y, core), shard: 32 (over z, x).
Axes of the slice: x: 4, y: 8, z: 8, core: 2. Of those that a mesh axis runs over, the one named last changes fastest.
Arguments:
- tokens: bfloat16 [4096, 2048], P('shard'), may hold values from -6 to 6
- targets: bfloat16 [4096, 2048], P('shard'), may hold values from -6 to 6
- norm_gain: float32 [2048], replicated, may hold values from 0.5 to 1.5
- weights: float32 [16, 2, 2048, 256], P('pop', None, 'shard'), may hold values from -6 to 6
- first_moment: float32 [16, 2, 2048, 256], P('pop', None, 'shard'), may hold values from -4 to 4
- second_moment: float32 [16, 2, 2048, 256], P('pop', None, 'shard'), may hold values from 0.05 to 2
- learned_params: float32 [192], replicated, may hold values from -4 to 4
- perturbation: float32 [8, 192], replicated, may hold values from -0.75 to 0.75
- accumulated: float32 [8, 192], replicated, may hold values from -3 to 3
Outputs:
- new_weights: float32 [16, 2, 2048, 256], P('pop', None, 'shard')
- new_first: float32 [16, 2, 2048, 256], P('pop', None, 'shard')
- new_second: float32 [16, 2, 2048, 256], P('pop', None, 'shard')
- unroll_loss: float32 [16], P('pop')
- outer_grad: float32 [192], replicated
All inputs are finite; a program needn't handle non-finite values.
Results may differ from a plain program's by a relative error of at most 0.004.
Values may be sent and summed in bfloat16 or wider, within the bound.
No kernel may reach another device: no remote copies, remote signals or barrier semaphores. Data moves between devices by JAX's collectives and lax.ppermute only.
A program may use at most 64 MiB of HBM per device.

v0:
```python
import jax
import jax.numpy as jnp
from jax import lax
from jax.sharding import PartitionSpec as P

D = 2048
RANK = 256


step_size = 0.1
beta_one = 0.9
beta_two = 0.99
norm_eps = 1e-05
grad_eps = 1e-06


def from_everyone(array, axis):
    copies = jnp.broadcast_to(array, (lax.axis_size(axis), *array.shape))
    return lax.all_to_all(copies, axis, split_axis=0, concat_axis=0, tiled=True)


def joined_along(tiles, dim):
    lengths = list(tiles.shape[1:])
    lengths[dim] *= tiles.shape[0]
    return jnp.moveaxis(tiles, 0, dim).reshape(lengths)


def gather_directly(array, axis, dim):
    tiles = from_everyone(array, axis)
    return joined_along(tiles, dim)


def over_copies(array, axis):
    everything = from_everyone(array, axis)
    return jnp.sum(everything, axis=0)


def in_blocks(array, dim, count):
    before, after = (array.shape[:dim], array.shape[dim + 1 :])
    return jnp.moveaxis(array.reshape(*before, count, -1, *after), dim, 0)


def sum_at_owner(array, axis, dim):
    count = lax.axis_size(axis)
    tiles = lax.all_to_all(in_blocks(array, dim, count), axis, 0, 0, tiled=True)
    return jnp.sum(tiles.astype(jnp.float32), axis=0)


def learned_update(weights, first_state, second_state, gradient, mean_square, learned):
    hidden_units = learned.shape[0] // 6
    scaled = gradient * lax.rsqrt(mean_square + grad_eps)[:, None, None]
    first_new = beta_one * first_state + (1.0 - beta_one) * scaled
    second_new = beta_two * second_state + (1.0 - beta_two) * scaled * scaled
    inverse = lax.rsqrt(second_new)
    momentum = (first_new * inverse).reshape(-1)
    features = jnp.stack([(scaled * inverse).reshape(-1), momentum, weights.reshape(-1)])
    in_map = learned[: 3 * hidden_units].reshape(3, hidden_units)
    in_bias = learned[3 * hidden_units : 4 * hidden_units]
    out_map = learned[4 * hidden_units :].reshape(2, hidden_units)
    hidden_act = jnp.tanh(jnp.dot(in_map.T, features) + in_bias[:, None])
    outputs = jnp.dot(out_map, hidden_act)
    change = -step_size * (momentum + outputs[0]) * jnp.exp(jnp.tanh(outputs[1]))
    return (weights + change.reshape(weights.shape), first_new, second_new)


def normalize(tokens, norm_gain):
    values = tokens.astype(jnp.float32)
    inverse = lax.rsqrt(jnp.mean(values * values, axis=-1, keepdims=True) + norm_eps)
    return (values * inverse * norm_gain).astype(jnp.bfloat16)


def local(
    tokens,
    targets,
    norm_gain,
    weights,
    first_moment,
    second_moment,
    learned_params,
    perturbation,
    accumulated,
):
    normed = normalize(tokens, norm_gain)
    tokens_wide = tokens.astype(jnp.float32)
    target_wide = targets.astype(jnp.float32)
    down_scale = D ** (-0.5)
    up_scale = RANK ** (-0.5)
    token_rows = tokens.shape[0]
    total_tokens = token_rows * lax.axis_size("shard")
    pop_index = lax.axis_index("pop")
    polarity = (1 - 2 * (pop_index % 2)).astype(jnp.float32)
    pair_index = pop_index // 2
    learned = learned_params + polarity * lax.dynamic_index_in_dim(
        perturbation, pair_index, 0, keepdims=False
    )
    current = weights[0]
    first_state = first_moment[0]
    second_state = second_moment[0]
    rounded = current.astype(jnp.bfloat16)
    gathered = gather_directly(rounded, "shard", 1)
    branch_input = jnp.dot(normed, gathered[0], preferred_element_type=jnp.float32) * down_scale
    active = jax.nn.silu(branch_input).astype(jnp.bfloat16)
    branch = (
        lax.dot_general(
            active, gathered[1], (((1,), (1,)), ((), ())), preferred_element_type=jnp.float32
        )
        * up_scale
    )
    residual = tokens_wide + branch - target_wide
    partial_value = jnp.sum(residual * residual)
    partial_value = over_copies(partial_value, "shard")
    step_losses = [partial_value]
    upstream = (2.0 * residual).astype(jnp.bfloat16)
    back_act = jnp.dot(upstream, gathered[1], preferred_element_type=jnp.float32) * up_scale
    logistic = jax.nn.sigmoid(branch_input)
    back = (back_act * logistic * (1.0 + branch_input * (1.0 - logistic))).astype(jnp.bfloat16)
    down_term = (
        lax.dot_general(normed, back, (((0,), (0,)), ((), ())), preferred_element_type=jnp.float32)
        * down_scale
    )
    up_term = (
        lax.dot_general(
            upstream, active, (((0,), (0,)), ((), ())), preferred_element_type=jnp.float32
        )
        * up_scale
    )
    summed = sum_at_owner(
        jnp.concatenate([down_term, up_term], axis=1).astype(jnp.bfloat16), "shard", 0
    )
    gradient = jnp.stack([summed[:, :RANK], summed[:, RANK:]])
    squares = over_copies(jnp.sum(gradient * gradient, axis=(1, 2)), "shard")
    mean_square = squares / (D * RANK)
    current, first_state, second_state = learned_update(
        current, first_state, second_state, gradient, mean_square, learned
    )
    local_total = jnp.sum(jnp.stack(step_losses)) / (total_tokens * D)
    direction = lax.dynamic_index_in_dim(accumulated + perturbation, pair_index, 0, keepdims=False)
    pair_norm = 2.0 * (lax.axis_size("pop") // 2)
    outer_grad = over_copies(polarity * local_total * direction / pair_norm, "pop")
    return (current[None], first_state[None], second_state[None], local_total[None], outer_grad)


def solution(mesh):
    return jax.shard_map(
        local,
        mesh=mesh,
        in_specs=(
            P("shard", None),
            P("shard", None),
            P(),
            P("pop", None, "shard", None),
            P("pop", None, "shard", None),
            P("pop", None, "shard", None),
            P(),
            P(),
            P(),
        ),
        out_specs=(
            P("pop", None, "shard", None),
            P("pop", None, "shard", None),
            P("pop", None, "shard", None),
            P("pop"),
            P(),
        ),
        check_vma=False,
    )
```

profile of v0, /device:TPU:1, one launch (start us, length us, event | category | flops | bytes accessed | tf_op | source)
XLA Modules:
  0.0 176.8 jit_solution(1798192167490026070)
XLA Ops:
  0.6 0.9 convert_bitcast_fusion
  1.5 1.6 broadcast_in_dim.10
  3.1 13.8 %all-to-all-start = ((bf16[32,2,64,256]{3,2,1,0:T(8,128)(2,1)}), bf16[32,2,64,256]{3,2,1,0:T(8,128)(2,1)S(1)}, u32[]{:S(2)}, u32[]{:S(2)}) async-start(bf16[32,2,64,256]{3,2,1,0:T(8,128)(2,1)} %broadcast_in_dim.10), calls=%async_computation | async-start | bytes 4194304 | tf_op jit(solution)/shard_map/all_to_all | solution.py:19
  17.0 0.0 copy-done
  17.0 0.2 fusion.10
  17.2 48.3 %all-to-all-done = bf16[32,2,64,256]{3,2,1,0:T(8,128)(2,1)S(1)} async-done(((bf16[32,2,64,256]{3,2,1,0:T(8,128)(2,1)}), bf16[32,2,64,256]{3,2,1,0:T(8,128)(2,1)S(1)}, u32[]{:S(2)}, u32[]{:S(2)}) %all-to-all-start) | async-done | bytes 2097184 | tf_op jit(solution)/shard_map/all_to_all | solution.py:19
  65.5 0.2 fusion.47
  65.7 0.8 copy-done.1
  66.5 0.0 copy-done.9
  66.5 0.4 convolution_multiply_fusion.4
  66.9 0.0 copy-start.2
  66.9 0.0 copy-done.7
  66.9 1.1 multiply_reduce_fusion
  68.0 0.0 copy-done.2
  68.0 2.0 %fusion.1 = bf16[2048,256]{1,0:T(8,128)(2,1)} fusion(bf16[2048,256]{1,0:T(8,128)(2,1)S(1)} %bitcast.35, f32[128,2048]{1,0:T(8,128)S(1)} %get-tuple-element.21, bf16[128,2048]{1,0:T(8,128)(2,1)S(1)} %copy-done.2, f32[2048]{0:T(1024)S(1)} %copy-done.9, f32[128]{0:T(128)S(1)} %add_rsqrt_fusion.1, f32[128,256]{1,0:T(8,128)S(1)} %convolution_multiply_fusion.4), kind=kOutput, calls=%fused_computation.5 | convolution fusion | flops 271384576 | bytes 3809792 | tf_op jit(solution)/shard_map/dot_general | solution.py:118
  70.0 0.5 fusion.2
  70.5 1.3 broadcast_in_dim.24
  71.8 6.7 %all-to-all-start.3 = ((f32[32,1,1]{2,1,0:T(1,128)}), f32[32,1,1]{2,1,0:T(1,128)S(1)}, u32[]{:S(2)}, u32[]{:S(2)}) async-start(f32[32,1,1]{2,1,0:T(1,128)} %broadcast_in_dim.24), calls=%async_computation.3 | async-start | bytes 32768 | tf_op jit(solution)/shard_map/all_to_all | solution.py:19
  78.4 0.0 copy-done.4
  78.4 1.5 pad_maximum_fusion
  80.0 7.0 %all-to-all-done.3 = f32[32,1,1]{2,1,0:T(1,128)S(1)} async-done(((f32[32,1,1]{2,1,0:T(1,128)}), f32[32,1,1]{2,1,0:T(1,128)S(1)}, u32[]{:S(2)}, u32[]{:S(2)}) %all-to-all-start.3) | async-done | bytes 160 | tf_op jit(solution)/shard_map/all_to_all | solution.py:19
  87.0 4.0 %all-to-all-start.1 = ((bf16[32,64,512]{2,1,0:T(8,128)(2,1)}), bf16[32,64,512]{2,1,0:T(8,128)(2,1)S(1)}, u32[]{:S(2)}, u32[]{:S(2)}) async-start(bf16[32,64,512]{2,1,0:T(8,128)(2,1)} %pad_maximum_fusion), calls=%async_computation.1 | async-start | bytes 4194304 | tf_op jit(solution)/shard_map/all_to_all | solution.py:45
  91.0 0.0 copy-start.8
  91.1 0.1 copy.20
  91.2 0.1 copy.21
  91.4 0.1 copy.22
  91.5 0.6 reduce_sum.72
  92.8 0.7 fusion.37
  93.6 43.7 %all-to-all-done.1 = bf16[32,64,512]{2,1,0:T(8,128)(2,1)S(1)} async-done(((bf16[32,64,512]{2,1,0:T(8,128)(2,1)}), bf16[32,64,512]{2,1,0:T(8,128)(2,1)S(1)}, u32[]{:S(2)}, u32[]{:S(2)}) %all-to-all-start.1) | async-done | bytes 2097184 | tf_op jit(solution)/shard_map/all_to_all | solution.py:45
  137.3 0.6 broadcast_in_dim.26
  137.9 11.9 %all-to-all-start.4 = ((f32[16,1,192]{2,1,0:T(1,128)}), f32[16,1,192]{2,1,0:T(1,128)S(1)}, u32[]{:S(2)}, u32[]{:S(2)}) async-start(f32[16,1,192]{2,1,0:T(1,128)} %broadcast_in_dim.26), calls=%async_computation.4 | async-start | bytes 32768 | tf_op jit(solution)/shard_map/all_to_all | solution.py:19
  149.8 0.3 convert_reduce_fusion
  150.1 0.1 multiply_reduce_fusion.1
  150.2 6.9 %all-to-all-done.4 = f32[16,1,192]{2,1,0:T(1,128)S(1)} async-done(((f32[16,1,192]{2,1,0:T(1,128)}), f32[16,1,192]{2,1,0:T(1,128)S(1)}, u32[]{:S(2)}, u32[]{:S(2)}) %all-to-all-start.4) | async-done | bytes 12320 | tf_op jit(solution)/shard_map/all_to_all | solution.py:19
  157.2 0.6 broadcast_in_dim.11
  157.8 5.7 %all-to-all-start.2 = ((f32[32,1,2]{2,1,0:T(1,128)}), f32[32,1,2]{2,1,0:T(1,128)S(1)}, u32[]{:S(2)}, u32[]{:S(2)}) async-start(f32[32,1,2]{2,1,0:T(1,128)} %broadcast_in_dim.11), calls=%async_computation.2 | async-start | bytes 32768 | tf_op jit(solution)/shard_map/all_to_all | solution.py:19
  163.5 0.1 slice.58
  163.6 0.1 slice.57
  163.6 0.1 slice.55
  163.7 0.6 reduce_sum.73
  164.3 7.7 %all-to-all-done.2 = f32[32,1,2]{2,1,0:T(1,128)S(1)} async-done(((f32[32,1,2]{2,1,0:T(1,128)}), f32[32,1,2]{2,1,0:T(1,128)S(1)}, u32[]{:S(2)}, u32[]{:S(2)}) %all-to-all-start.2) | async-done | bytes 288 | tf_op jit(solution)/shard_map/all_to_all | solution.py:19
  172.0 0.1 reduce_sum.70
  172.0 0.1 fusion.33
  172.1 0.1 mul.342
  172.3 0.4 fusion.45
  172.6 1.4 fusion.5
  174.0 0.8 slice_reduce_fusion
  174.9 0.8 multiply_add_fusion
  (22 shorter events, 0.2 us)
Async XLA Ops:
  3.1 13.8 %copy-start = (bf16[128,2048]{1,0:T(8,128)(2,1)S(1)}, bf16[128,2048]{1,0:T(8,128)(2,1)}, u32[]{:S(2)}) copy-start(bf16[128,2048]{1,0:T(8,128)(2,1)} %param.9) | copy-start | bytes 1572868
  3.1 62.3 %all-to-all-start = ((bf16[32,2,64,256]{3,2,1,0:T(8,128)(2,1)}), bf16[32,2,64,256]{3,2,1,0:T(8,128)(2,1)S(1)}, u32[]{:S(2)}, u32[]{:S(2)}) async-start(bf16[32,2,64,256]{3,2,1,0:T(8,128)(2,1)} %broadcast_in_dim.10), calls=%async_computation | async-start | bytes 4194304 | tf_op jit(solution)/shard_map/all_to_all | solution.py:19
  65.5 1.0 copy-start.1
  65.5 1.0 copy-start.9
  65.5 1.4 copy-start.7
  66.9 1.2 copy-start.2
  70.0 8.4 %copy-start.4 = (bf16[2048,256]{1,0:T(8,128)(2,1)S(1)}, bf16[2048,256]{1,0:T(8,128)(2,1)}, u32[]{:S(2)}) copy-start(bf16[2048,256]{1,0:T(8,128)(2,1)} %fusion.1) | copy-start | bytes 3145732
  71.8 15.2 %all-to-all-start.3 = ((f32[32,1,1]{2,1,0:T(1,128)}), f32[32,1,1]{2,1,0:T(1,128)S(1)}, u32[]{:S(2)}, u32[]{:S(2)}) async-start(f32[32,1,1]{2,1,0:T(1,128)} %broadcast_in_dim.24), calls=%async_computation.3 | async-start | bytes 32768 | tf_op jit(solution)/shard_map/all_to_all | solution.py:19
  80.0 11.0 %copy-start.5 = (f32[1,2,64,256]{3,2,1,0:T(8,128)S(1)}, f32[1,2,64,256]{3,2,1,0:T(8,128)}, u32[]{:S(2)}) copy-start(f32[1,2,64,256]{3,2,1,0:T(8,128)} %param.14) | copy-start | bytes 393220
  80.0 11.2 %copy-start.6 = (f32[1,2,64,256]{3,2,1,0:T(8,128)S(1)}, f32[1,2,64,256]{3,2,1,0:T(8,128)}, u32[]{:S(2)}) copy-start(f32[1,2,64,256]{3,2,1,0:T(8,128)} %param.13) | copy-start | bytes 393220
  80.0 11.4 %copy-start.3 = (f32[1,2,64,256]{3,2,1,0:T(8,128)S(1)}, f32[1,2,64,256]{3,2,1,0:T(8,128)}, u32[]{:S(2)}) copy-start(f32[1,2,64,256]{3,2,1,0:T(8,128)} %param.12) | copy-start | bytes 393220
  87.0 50.3 %all-to-all-start.1 = ((bf16[32,64,512]{2,1,0:T(8,128)(2,1)}), bf16[32,64,512]{2,1,0:T(8,128)(2,1)S(1)}, u32[]{:S(2)}, u32[]{:S(2)}) async-start(bf16[32,64,512]{2,1,0:T(8,128)(2,1)} %pad_maximum_fusion), calls=%async_computation.1 | async-start | bytes 4194304 | tf_op jit(solution)/shard_map/all_to_all | solution.py:45
  91.0 72.4 %copy-start.8 = (f32[192]{0:T(256)S(1)}, f32[192]{0:T(256)}, u32[]{:S(2)}) copy-start(f32[192]{0:T(256)} %param.15) | copy-start | bytes 2308
  137.9 19.2 %all-to-all-start.4 = ((f32[16,1,192]{2,1,0:T(1,128)}), f32[16,1,192]{2,1,0:T(1,128)S(1)}, u32[]{:S(2)}, u32[]{:S(2)}) async-start(f32[16,1,192]{2,1,0:T(1,128)} %broadcast_in_dim.26), calls=%async_computation.4 | async-start | bytes 32768 | tf_op jit(solution)/shard_map/all_to_all | solution.py:19
  157.8 14.2 %all-to-all-start.2 = ((f32[32,1,2]{2,1,0:T(1,128)}), f32[32,1,2]{2,1,0:T(1,128)S(1)}, u32[]{:S(2)}, u32[]{:S(2)}) async-start(f32[32,1,2]{2,1,0:T(1,128)} %broadcast_in_dim.11), calls=%async_computation.2 | async-start | bytes 32768 | tf_op jit(solution)/shard_map/all_to_all | solution.py:19
where the time goes:
time: 177 us
  waiting for transfers between devices  114 us (64%)
  starting transfers between devices  42.1 us (24%)
  local copies, waits for them, and re-layouts  6.81 us (4%)
  other arithmetic  6.38 us (4%)
  matrix products  5.3 us (3%)
  between operations  2.7 us (2%)
    all_to_all x4, waiting for transfers between devices, from_everyone(): return lax.all_to_all(copies, axis, split_axis=0, concat_axis=0, tiled=True)  69.8 us
    all_to_all x1, waiting for transfers between devices, sum_at_owner(): tiles = lax.all_to_all(in_blocks(array, dim, count), axis, 0, 0, tiled=True)  43.7 us
    all_to_all x4, starting transfers between devices, from_everyone(): return lax.all_to_all(copies, axis, split_axis=0, concat_axis=0, tiled=True)  38.1 us
    broadcast_in_dim x4, local copies, waits for them, and re-layouts, from_everyone(): copies = jnp.broadcast_to(array, (lax.axis_size(axis), *array.shape))  4.09 us
    all_to_all x1, starting transfers between devices, sum_at_owner(): tiles = lax.all_to_all(in_blocks(array, dim, count), axis, 0, 0, tiled=True)  4.01 us
  transfers between devices with their start and end apart: 5, of which 5 were waited for; matrix products, arithmetic and copies ran while one was open for 3% of the time, Pallas kernels for 0%

commit v1 on v0

v1 whole, which is shorter than its diff:
```python
import jax
import jax.numpy as jnp
from jax import lax
from jax.sharding import Mesh, PartitionSpec as P

D = 2048
RANK = 256

step_size = 0.1
beta_one = 0.9
beta_two = 0.99
norm_eps = 1e-05
grad_eps = 1e-06
f32 = jnp.float32
bf16 = jnp.bfloat16


def from_everyone(array, axis):
    copies = jnp.broadcast_to(array, (lax.axis_size(axis), *array.shape))
    return lax.all_to_all(copies, axis, split_axis=0, concat_axis=0, tiled=True)


def learned_update(weights, first_state, second_state, gradient, mean_square, learned):
    hidden_units = learned.shape[0] // 6
    scaled = gradient * lax.rsqrt(mean_square + grad_eps)[:, None, None]
    first_new = beta_one * first_state + (1.0 - beta_one) * scaled
    second_new = beta_two * second_state + (1.0 - beta_two) * scaled * scaled
    inverse = lax.rsqrt(second_new)
    momentum = (first_new * inverse).reshape(-1)
    features = jnp.stack([(scaled * inverse).reshape(-1), momentum, weights.reshape(-1)])
    in_map = learned[: 3 * hidden_units].reshape(3, hidden_units)
    in_bias = learned[3 * hidden_units : 4 * hidden_units]
    out_map = learned[4 * hidden_units :].reshape(2, hidden_units)
    hidden_act = jnp.tanh(jnp.dot(in_map.T, features) + in_bias[:, None])
    outputs = jnp.dot(out_map, hidden_act)
    change = -step_size * (momentum + outputs[0]) * jnp.exp(jnp.tanh(outputs[1]))
    return (weights + change.reshape(weights.shape), first_new, second_new)


def normalize(tokens, norm_gain):
    values = tokens.astype(f32)
    inverse = lax.rsqrt(jnp.mean(values * values, axis=-1, keepdims=True) + norm_eps)
    return (values * inverse * norm_gain).astype(bf16)


def shift(array, axis, step):
    count = lax.axis_size(axis)
    return lax.ppermute(array, axis, [(i, (i + step) % count) for i in range(count)])


def swap(array, axis, mask):
    return lax.ppermute(array, axis, [(i, i ^ mask) for i in range(lax.axis_size(axis))])


def local(
    tokens,
    targets,
    norm_gain,
    weights,
    first_moment,
    second_moment,
    learned_params,
    perturbation,
    accumulated,
):
    nz, nx = lax.axis_size("z"), lax.axis_size("x")
    particles = lax.axis_size("y") * lax.axis_size("core")
    my_x = lax.axis_index("x")
    rows = weights.shape[2]
    block = tokens.shape[0]
    width = nz * rows
    total_tokens = block * nz * nx
    down_scale = D ** (-0.5)
    up_scale = RANK ** (-0.5)
    particle = lax.axis_index("y") * lax.axis_size("core") + lax.axis_index("core")
    polarity = (1 - 2 * (particle % 2)).astype(f32)
    pair_index = particle // 2
    learned = learned_params + polarity * lax.dynamic_index_in_dim(
        perturbation, pair_index, 0, keepdims=False
    )

    gathered = from_everyone(weights[0].astype(bf16), "z")
    down_w = gathered[:, 0].reshape(width, RANK)
    up_w = gathered[:, 1].reshape(width, RANK)

    normed = normalize(tokens, norm_gain)
    cut = jnp.stack([normed, tokens, targets]).reshape(3, block, nz, nx, rows)
    cut = jnp.transpose(cut, (3, 0, 1, 2, 4)).reshape(nx, 3, block, width)

    def slot(array, step):
        return lax.dynamic_index_in_dim(array, (my_x + step) % nx, 0, keepdims=False)

    parts = [slot(cut, 0)] + [shift(slot(cut, k), "x", k) for k in range(1, nx)]
    normed_x, tokens_x, targets_x = (
        jnp.concatenate([p[i] for p in parts], axis=0) for i in range(3)
    )

    def summed_over_x(partial):
        blocks = partial.astype(bf16)
        total = partial
        for k in range(1, nx):
            turned = jnp.roll(blocks, k * block, axis=0)
            total = total + shift(turned, "x", k).astype(f32)
        return total

    branch_input = summed_over_x(
        jnp.dot(normed_x, down_w, preferred_element_type=f32) * down_scale
    )
    active = jax.nn.silu(branch_input).astype(bf16)
    branch = (
        lax.dot_general(active, up_w, (((1,), (1,)), ((), ())), preferred_element_type=f32)
        * up_scale
    )
    residual = tokens_x.astype(f32) + branch - targets_x.astype(f32)
    loss_part = jnp.sum(residual * residual)
    upstream = (2.0 * residual).astype(bf16)
    back_act = summed_over_x(jnp.dot(upstream, up_w, preferred_element_type=f32) * up_scale)
    logistic = jax.nn.sigmoid(branch_input)
    back = (back_act * logistic * (1.0 + branch_input * (1.0 - logistic))).astype(bf16)
    down_term = (
        lax.dot_general(normed_x, back, (((0,), (0,)), ((), ())), preferred_element_type=f32)
        * down_scale
    )
    up_term = (
        lax.dot_general(upstream, active, (((0,), (0,)), ((), ())), preferred_element_type=f32)
        * up_scale
    )
    terms = jnp.stack(
        [
            down_term.astype(bf16).reshape(nz, rows, RANK),
            up_term.astype(bf16).reshape(nz, rows, RANK),
        ],
        axis=1,
    )
    gradient = jnp.sum(
        lax.all_to_all(terms, "z", 0, 0, tiled=True).astype(f32), axis=0
    )

    losses = jnp.where(jnp.arange(particles) == particle, loss_part, 0.0)
    losses = losses + swap(losses, "core", 1)
    for mask in (1, 2, 4):
        losses = losses + swap(losses, "y", mask)
    squares = jnp.sum(gradient * gradient, axis=(1, 2))
    sums = jnp.sum(from_everyone(jnp.concatenate([squares, losses]), ("z", "x")), axis=0)
    mean_square = sums[:2] / (D * RANK)
    all_losses = sums[2:] / (total_tokens * D)

    current, first_state, second_state = learned_update(
        weights[0], first_moment[0], second_moment[0], gradient, mean_square, learned
    )
    own_loss = lax.dynamic_index_in_dim(all_losses, particle, 0, keepdims=True)
    pair_diff = all_losses[0::2] - all_losses[1::2]
    outer_grad = jnp.sum(pair_diff[:, None] * (accumulated + perturbation), axis=0) / particles
    return (current[None], first_state[None], second_state[None], own_loss, outer_grad)


def solution(mesh):
    grid = Mesh(mesh.devices.reshape(8, 2, 8, 4), ("y", "core", "z", "x"))
    pop, shard = ("y", "core"), ("z", "x")
    return jax.shard_map(
        local,
        mesh=grid,
        in_specs=(
            P(shard, None),
            P(shard, None),
            P(),
            P(pop, None, shard, None),
            P(pop, None, shard, None),
            P(pop, None, shard, None),
            P(),
            P(),
            P(),
        ),
        out_specs=(
            P(pop, None, shard, None),
            P(pop, None, shard, None),
            P(pop, None, shard, None),
            P(pop),
            P(),
        ),
        check_vma=False,
    )
```

time: 177 us -> 145 us (0.82)
  the two profiles are of different devices: /device:TPU:1 before, /device:TPU:40 now
where the time goes in v1:
time: 145 us; the launch traced here: 144 us
  starting transfers between devices  61.9 us (43%)
  waiting for transfers between devices  57.2 us (39%)
  local copies, waits for them, and re-layouts  13.5 us (9%)
  other arithmetic  6.34 us (4%)
  matrix products  4.05 us (3%)
  between operations  1.47 us (1%)
    ppermute x9, waiting for transfers between devices, shift(): lax.ppermute(array, axis, [(i, (i + step) % count) for i in range(count)])  34.9 us
    ppermute x9, starting transfers between devices, shift(): lax.ppermute(array, axis, [(i, (i + step) % count) for i in range(count)])  26.3 us
    all_to_all x2, starting transfers between devices, from_everyone(): return lax.all_to_all(copies, axis, split_axis=0, concat_axis=0, tiled=True)  17.9 us
    ppermute x4, waiting for transfers between devices, swap(): lax.ppermute(array, axis, [(i, i ^ mask) for i in range(lax.axis_size(axi...  13.4 us
    ppermute x4, starting transfers between devices, swap(): lax.ppermute(array, axis, [(i, i ^ mask) for i in range(lax.axis_size(axi...  10.8 us
    all_to_all x2, waiting for transfers between devices, from_everyone(): return lax.all_to_all(copies, axis, split_axis=0, concat_axis=0, tiled=True)  8.94 us
    all_to_all x1, starting transfers between devices, local(): lax.all_to_all(terms, 'z', 0, 0, tiled=True).astype(f32)  6.92 us
    unnamed x42, local copies, waits for them, and re-layouts  3.47 us
  transfers between devices with their start and end apart: 16, of which 13 were waited for; matrix products, arithmetic and copies ran while one was open for 7% of the time, Pallas kernels for 0%

profile of v1, /device:TPU:40, one launch (start us, length us, event | category | flops | bytes accessed | tf_op | source)
XLA Modules:
  0.0 144.5 jit_solution(10056938881692193386)
XLA Ops:
  0.7 1.3 copy.58
  2.0 1.3 copy.56
  4.4 0.9 copy.63
  5.4 4.7 %collective-permute-start.2 = (bf16[3,128,512]{2,1,0:T(8,128)(2,1)}, bf16[3,128,512]{2,1,0:T(8,128)(2,1)S(1)}, u32[]{:S(2)}, u32[]{:S(2)}) collective-permute-start(bf16[3,128,512]{2,1,0:T(8,128)(2,1)} %bitcast.10), channel_id=1, source_target_pairs={{0,3},{1,0},{2,1},{3,2},{4,7},{5,4},{6,5},{7,6},{8,11},{9,8},{10,9... | collective-permute-start | bytes 1179656 | tf_op jit(solution)/shard_map/ppermute | solution.py:48
  10.1 0.9 broadcast_in_dim.12
  10.9 10.3 %all-to-all-start = ((bf16[8,2,64,256]{3,2,1,0:T(8,128)(2,1)}), bf16[8,2,64,256]{3,2,1,0:T(8,128)(2,1)S(1)}, u32[]{:S(2)}, u32[]{:S(2)}) async-start(bf16[8,2,64,256]{3,2,1,0:T(8,128)(2,1)} %broadcast_in_dim.12), calls=%async_computation | async-start | bytes 1048576 | tf_op jit(solution)/shard_map/all_to_all | solution.py:20
  21.2 0.9 copy.62
  22.2 2.7 %collective-permute-start.1 = (bf16[3,128,512]{2,1,0:T(8,128)(2,1)}, bf16[3,128,512]{2,1,0:T(8,128)(2,1)}, u32[]{:S(2)}, u32[]{:S(2)}) collective-permute-start(bf16[3,128,512]{2,1,0:T(8,128)(2,1)} %bitcast.79), channel_id=1, source_target_pairs={{0,2},{1,3},{2,0},{3,1},{4,6},{5,7},{6,4},{7,5},{8,10},{9,11},{10,... | collective-permute-start | bytes 1179656 | tf_op jit(solution)/shard_map/ppermute | solution.py:48
  24.9 0.9 copy.61
  25.8 2.8 %collective-permute-start = (bf16[3,128,512]{2,1,0:T(8,128)(2,1)}, bf16[3,128,512]{2,1,0:T(8,128)(2,1)S(1)}, u32[]{:S(2)}, u32[]{:S(2)}) collective-permute-start(bf16[3,128,512]{2,1,0:T(8,128)(2,1)} %bitcast.78), channel_id=1, source_target_pairs={{0,1},{1,2},{2,3},{3,0},{4,5},{5,6},{6,7},{7,4},{8,9},{9,10},{10,1... | collective-permute-start | bytes 1179656 | tf_op jit(solution)/shard_map/ppermute | solution.py:48
  28.8 0.7 slice_bitcast_fusion
  29.6 8.4 %collective-permute-done.1 = bf16[3,128,512]{2,1,0:T(8,128)(2,1)} collective-permute-done((bf16[3,128,512]{2,1,0:T(8,128)(2,1)}, bf16[3,128,512]{2,1,0:T(8,128)(2,1)}, u32[]{:S(2)}, u32[]{:S(2)}) %collective-permute-start.1) | collective-permute-done | bytes 393248 | tf_op jit(solution)/shard_map/ppermute | solution.py:48
  37.9 1.8 %slice_bitcast_fusion.1 = (bf16[128,512]{1,0:T(8,128)(2,1)}, bf16[128,512]{1,0:T(8,128)(2,1)}, bf16[128,512]{1,0:T(8,128)(2,1)S(1)}) fusion(bf16[3,128,512]{2,1,0:T(8,128)(2,1)} %collective-permute-done.1), kind=kLoop, calls=%fused_computation.47 | loop fusion | bytes 786432 | tf_op jit(solution)/shard_map/squeeze | solution.py:95
  39.7 4.8 %collective-permute-done = bf16[3,128,512]{2,1,0:T(8,128)(2,1)S(1)} collective-permute-done((bf16[3,128,512]{2,1,0:T(8,128)(2,1)}, bf16[3,128,512]{2,1,0:T(8,128)(2,1)S(1)}, u32[]{:S(2)}, u32[]{:S(2)}) %collective-permute-start) | collective-permute-done | bytes 393248 | tf_op jit(solution)/shard_map/ppermute | solution.py:48
  44.5 0.8 slice_bitcast_fusion.2
  45.7 2.5 %collective-permute-start.5 = (bf16[512,256]{1,0:T(8,128)(2,1)S(1)}, bf16[512,256]{1,0:T(8,128)(2,1)S(1)}, u32[]{:S(2)}, u32[]{:S(2)}) collective-permute-start(bf16[512,256]{1,0:T(8,128)(2,1)S(1)} %pad_maximum_fusion.4), channel_id=1, source_target_pairs={{0,3},{1,0},{2,1},{3,2},{4,7},{5,4},{6,5},{7,6},{8,11},{9,8},{10,9... | collective-permute-start | bytes 786440 | tf_op jit(solution)/shard_map/ppermute | solution.py:48
  48.3 2.8 %collective-permute-start.4 = (bf16[512,256]{1,0:T(8,128)(2,1)S(1)}, bf16[512,256]{1,0:T(8,128)(2,1)S(1)}, u32[]{:S(2)}, u32[]{:S(2)}) collective-permute-start(bf16[512,256]{1,0:T(8,128)(2,1)S(1)} %pad_maximum_fusion.3), channel_id=1, source_target_pairs={{0,2},{1,3},{2,0},{3,1},{4,6},{5,7},{6,4},{7,5},{8,10},{9,11},{10,... | collective-permute-start | bytes 786440 | tf_op jit(solution)/shard_map/ppermute | solution.py:48
  51.2 2.7 %collective-permute-start.3 = (bf16[512,256]{1,0:T(8,128)(2,1)S(1)}, bf16[512,256]{1,0:T(8,128)(2,1)S(1)}, u32[]{:S(2)}, u32[]{:S(2)}) collective-permute-start(bf16[512,256]{1,0:T(8,128)(2,1)S(1)} %pad_maximum_fusion.2), channel_id=1, source_target_pairs={{0,1},{1,2},{2,3},{3,0},{4,5},{5,6},{6,7},{7,4},{8,9},{9,10},{10,1... | collective-permute-start | bytes 786440 | tf_op jit(solution)/shard_map/ppermute | solution.py:48
  54.2 2.6 %collective-permute-done.5 = bf16[512,256]{1,0:T(8,128)(2,1)S(1)} collective-permute-done((bf16[512,256]{1,0:T(8,128)(2,1)S(1)}, bf16[512,256]{1,0:T(8,128)(2,1)S(1)}, u32[]{:S(2)}, u32[]{:S(2)}) %collective-permute-start.5) | collective-permute-done | bytes 262176 | tf_op jit(solution)/shard_map/ppermute | solution.py:48
  56.8 4.2 %collective-permute-done.4 = bf16[512,256]{1,0:T(8,128)(2,1)S(1)} collective-permute-done((bf16[512,256]{1,0:T(8,128)(2,1)S(1)}, bf16[512,256]{1,0:T(8,128)(2,1)S(1)}, u32[]{:S(2)}, u32[]{:S(2)}) %collective-permute-start.4) | collective-permute-done | bytes 262176 | tf_op jit(solution)/shard_map/ppermute | solution.py:48
  61.0 4.1 %collective-permute-done.3 = bf16[512,256]{1,0:T(8,128)(2,1)S(1)} collective-permute-done((bf16[512,256]{1,0:T(8,128)(2,1)S(1)}, bf16[512,256]{1,0:T(8,128)(2,1)S(1)}, u32[]{:S(2)}, u32[]{:S(2)}) %collective-permute-start.3) | collective-permute-done | bytes 262176 | tf_op jit(solution)/shard_map/ppermute | solution.py:48
  65.4 1.1 multiply_reduce_fusion
  66.9 2.6 %collective-permute-start.8 = (bf16[512,256]{1,0:T(8,128)(2,1)S(1)}, bf16[512,256]{1,0:T(8,128)(2,1)S(1)}, u32[]{:S(2)}, u32[]{:S(2)}) collective-permute-start(bf16[512,256]{1,0:T(8,128)(2,1)S(1)} %pad_maximum_fusion.7), channel_id=1, source_target_pairs={{0,3},{1,0},{2,1},{3,2},{4,7},{5,4},{6,5},{7,6},{8,11},{9,8},{10,9... | collective-permute-start | bytes 786440 | tf_op jit(solution)/shard_map/ppermute | solution.py:48
  69.5 2.7 %collective-permute-start.7 = (bf16[512,256]{1,0:T(8,128)(2,1)S(1)}, bf16[512,256]{1,0:T(8,128)(2,1)S(1)}, u32[]{:S(2)}, u32[]{:S(2)}) collective-permute-start(bf16[512,256]{1,0:T(8,128)(2,1)S(1)} %pad_maximum_fusion.6), channel_id=1, source_target_pairs={{0,2},{1,3},{2,0},{3,1},{4,6},{5,7},{6,4},{7,5},{8,10},{9,11},{10,... | collective-permute-start | bytes 786440 | tf_op jit(solution)/shard_map/ppermute | solution.py:48
  72.3 2.8 %collective-permute-start.6 = (bf16[512,256]{1,0:T(8,128)(2,1)S(1)}, bf16[512,256]{1,0:T(8,128)(2,1)S(1)}, u32[]{:S(2)}, u32[]{:S(2)}) collective-permute-start(bf16[512,256]{1,0:T(8,128)(2,1)S(1)} %pad_maximum_fusion.5), channel_id=1, source_target_pairs={{0,1},{1,2},{2,3},{3,0},{4,5},{5,6},{6,7},{7,4},{8,9},{9,10},{10,1... | collective-permute-start | bytes 786440 | tf_op jit(solution)/shard_map/ppermute | solution.py:48
  75.4 2.7 %collective-permute-done.8 = bf16[512,256]{1,0:T(8,128)(2,1)S(1)} collective-permute-done((bf16[512,256]{1,0:T(8,128)(2,1)S(1)}, bf16[512,256]{1,0:T(8,128)(2,1)S(1)}, u32[]{:S(2)}, u32[]{:S(2)}) %collective-permute-start.8) | collective-permute-done | bytes 262176 | tf_op jit(solution)/shard_map/ppermute | solution.py:48
  78.1 4.0 %collective-permute-done.7 = bf16[512,256]{1,0:T(8,128)(2,1)S(1)} collective-permute-done((bf16[512,256]{1,0:T(8,128)(2,1)S(1)}, bf16[512,256]{1,0:T(8,128)(2,1)S(1)}, u32[]{:S(2)}, u32[]{:S(2)}) %collective-permute-start.7) | collective-permute-done | bytes 262176 | tf_op jit(solution)/shard_map/ppermute | solution.py:48
  82.1 4.1 %collective-permute-done.6 = bf16[512,256]{1,0:T(8,128)(2,1)S(1)} collective-permute-done((bf16[512,256]{1,0:T(8,128)(2,1)S(1)}, bf16[512,256]{1,0:T(8,128)(2,1)S(1)}, u32[]{:S(2)}, u32[]{:S(2)}) %collective-permute-start.6) | collective-permute-done | bytes 262176 | tf_op jit(solution)/shard_map/ppermute | solution.py:48
  86.2 0.7 fusion.3
  86.9 0.9 pad_maximum_fusion.1
  87.8 6.9 %all-to-all-start.1 = ((bf16[8,2,64,256]{3,2,1,0:T(8,128)(2,1)}), bf16[8,2,64,256]{3,2,1,0:T(8,128)(2,1)S(1)}, u32[]{:S(2)}, u32[]{:S(2)}) async-start(bf16[8,2,64,256]{3,2,1,0:T(8,128)(2,1)} %pad_maximum_fusion.1), calls=%async_computation.1 | async-start | bytes 1048576 | tf_op jit(solution)/shard_map/all_to_all | solution.py:136
  94.8 0.7 compare_select_fusion
  95.5 1.9 %collective-permute-start.9 = (f32[16]{0:T(128)S(1)}, f32[16]{0:T(128)S(1)}, u32[]{:S(2)}, u32[]{:S(2)}) collective-permute-start(f32[16]{0:T(128)S(1)} %compare_select_fusion), channel_id=1, source_target_pairs={{0,32},{32,0},{1,33},{33,1},{2,34},{34,2},{3,35},{35,3},{4,36},{36... | collective-permute-start | bytes 200 | tf_op jit(solution)/shard_map/ppermute | solution.py:52
  97.4 1.1 collective-permute-done.9
  98.5 0.6 fusion.49
  99.2 3.3 %collective-permute-start.10 = (f32[16]{0:T(128)S(1)}, f32[16]{0:T(128)S(1)}, u32[]{:S(2)}, u32[]{:S(2)}) collective-permute-start(f32[16]{0:T(128)S(1)} %fusion.49), channel_id=1, source_target_pairs={{0,64},{64,0},{128,192},{192,128},{256,320},{320,256},{384,448},{4... | collective-permute-start | bytes 200 | tf_op jit(solution)/shard_map/ppermute | solution.py:52
  102.4 2.2 %collective-permute-done.10 = f32[16]{0:T(128)S(1)} collective-permute-done((f32[16]{0:T(128)S(1)}, f32[16]{0:T(128)S(1)}, u32[]{:S(2)}, u32[]{:S(2)}) %collective-permute-start.10) | collective-permute-done | bytes 96 | tf_op jit(solution)/shard_map/ppermute | solution.py:52
  104.6 0.6 fusion.50
  105.3 2.7 %collective-permute-start.11 = (f32[16]{0:T(128)S(1)}, f32[16]{0:T(128)S(1)}, u32[]{:S(2)}, u32[]{:S(2)}) collective-permute-start(f32[16]{0:T(128)S(1)} %fusion.50), channel_id=1, source_target_pairs={{0,128},{64,192},{128,0},{192,64},{256,384},{320,448},{384,256},{4... | collective-permute-start | bytes 200 | tf_op jit(solution)/shard_map/ppermute | solution.py:52
  108.0 3.6 %collective-permute-done.11 = f32[16]{0:T(128)S(1)} collective-permute-done((f32[16]{0:T(128)S(1)}, f32[16]{0:T(128)S(1)}, u32[]{:S(2)}, u32[]{:S(2)}) %collective-permute-start.11) | collective-permute-done | bytes 96 | tf_op jit(solution)/shard_map/ppermute | solution.py:52
  111.7 2.9 %collective-permute-start.12 = (f32[16]{0:T(128)S(1)}, f32[16]{0:T(128)S(1)}, u32[]{:S(2)}, u32[]{:S(2)}) collective-permute-start(f32[16]{0:T(128)S(1)} %add.189), channel_id=1, source_target_pairs={{0,256},{64,320},{128,384},{192,448},{256,0},{320,64},{384,128},{4... | collective-permute-start | bytes 200 | tf_op jit(solution)/shard_map/ppermute | solution.py:52
  114.6 6.4 %collective-permute-done.12 = f32[16]{0:T(128)S(1)} collective-permute-done((f32[16]{0:T(128)S(1)}, f32[16]{0:T(128)S(1)}, u32[]{:S(2)}, u32[]{:S(2)}) %collective-permute-start.12) | collective-permute-done | bytes 96 | tf_op jit(solution)/shard_map/ppermute | solution.py:52
  121.3 0.6 broadcast_in_dim.25
  121.9 7.6 %all-to-all-start.2 = ((f32[32,1,18]{2,1,0:T(1,128)}), f32[32,1,18]{2,1,0:T(1,128)S(1)}, u32[]{:S(2)}, u32[]{:S(2)}) async-start(f32[32,1,18]{2,1,0:T(1,128)} %broadcast_in_dim.25), calls=%async_computation.2 | async-start | bytes 32768 | tf_op jit(solution)/shard_map/all_to_all | solution.py:20
  130.3 8.9 %all-to-all-done.2 = f32[32,1,18]{2,1,0:T(1,128)S(1)} async-done(((f32[32,1,18]{2,1,0:T(1,128)}), f32[32,1,18]{2,1,0:T(1,128)S(1)}, u32[]{:S(2)}, u32[]{:S(2)}) %all-to-all-start.2) | async-done | bytes 2336 | tf_op jit(solution)/shard_map/all_to_all | solution.py:20
  140.1 1.4 fusion.1
  141.5 0.8 slice_reduce_fusion
  143.6 0.8 multiply_add_fusion
  (96 shorter events, 6.2 us)
Async XLA Ops:
  0.6 3.0 %copy-start.14 = (f32[2048]{0:T(1024)S(1)}, f32[2048]{0:T(1024)}, u32[]{:S(2)}) copy-start(f32[2048]{0:T(1024)} %param.11) | copy-start | bytes 24580
  4.3 5.7 %copy-start = (f32[1,2,64,256]{3,2,1,0:T(8,128)S(1)}, f32[1,2,64,256]{3,2,1,0:T(8,128)}, u32[]{:S(2)}) copy-start(f32[1,2,64,256]{3,2,1,0:T(8,128)} %param.12) | copy-start | bytes 393220
  5.4 23.5 %collective-permute-start.2 = (bf16[3,128,512]{2,1,0:T(8,128)(2,1)}, bf16[3,128,512]{2,1,0:T(8,128)(2,1)S(1)}, u32[]{:S(2)}, u32[]{:S(2)}) collective-permute-start(bf16[3,128,512]{2,1,0:T(8,128)(2,1)} %bitcast.10), channel_id=1, source_target_pairs={{0,3},{1,0},{2,1},{3,2},{4,7},{5,4},{6,5},{7,6},{8,11},{9,8},{10,9... | collective-permute-start | bytes 1179656 | tf_op jit(solution)/shard_map/ppermute | solution.py:48
  10.9 34.3 %all-to-all-start = ((bf16[8,2,64,256]{3,2,1,0:T(8,128)(2,1)}), bf16[8,2,64,256]{3,2,1,0:T(8,128)(2,1)S(1)}, u32[]{:S(2)}, u32[]{:S(2)}) async-start(bf16[8,2,64,256]{3,2,1,0:T(8,128)(2,1)} %broadcast_in_dim.12), calls=%async_computation | async-start | bytes 1048576 | tf_op jit(solution)/shard_map/all_to_all | solution.py:20
  22.2 15.7 %collective-permute-start.1 = (bf16[3,128,512]{2,1,0:T(8,128)(2,1)}, bf16[3,128,512]{2,1,0:T(8,128)(2,1)}, u32[]{:S(2)}, u32[]{:S(2)}) collective-permute-start(bf16[3,128,512]{2,1,0:T(8,128)(2,1)} %bitcast.79), channel_id=1, source_target_pairs={{0,2},{1,3},{2,0},{3,1},{4,6},{5,7},{6,4},{7,5},{8,10},{9,11},{10,... | collective-permute-start | bytes 1179656 | tf_op jit(solution)/shard_map/ppermute | solution.py:48
  25.8 18.7 %collective-permute-start = (bf16[3,128,512]{2,1,0:T(8,128)(2,1)}, bf16[3,128,512]{2,1,0:T(8,128)(2,1)S(1)}, u32[]{:S(2)}, u32[]{:S(2)}) collective-permute-start(bf16[3,128,512]{2,1,0:T(8,128)(2,1)} %bitcast.78), channel_id=1, source_target_pairs={{0,1},{1,2},{2,3},{3,0},{4,5},{5,6},{6,7},{7,4},{8,9},{9,10},{10,1... | collective-permute-start | bytes 1179656 | tf_op jit(solution)/shard_map/ppermute | solution.py:48
  28.8 16.5 %copy-start.3 = (bf16[1,1,128,512]{3,2,1,0:T(8,128)(2,1)}, bf16[1,1,128,512]{3,2,1,0:T(8,128)(2,1)S(1)}, u32[]{:S(2)}) copy-start(bf16[1,1,128,512]{3,2,1,0:T(8,128)(2,1)S(1)} %copy.69) | copy-start | bytes 393220
  29.6 16.1 %copy-start.5 = (bf16[128,512]{1,0:T(8,128)(2,1)}, bf16[128,512]{1,0:T(8,128)(2,1)S(1)}, u32[]{:S(2)}) copy-start(bf16[128,512]{1,0:T(8,128)(2,1)S(1)} %get-tuple-element.26) | copy-start | bytes 393220
  45.7 11.1 %collective-permute-start.5 = (bf16[512,256]{1,0:T(8,128)(2,1)S(1)}, bf16[512,256]{1,0:T(8,128)(2,1)S(1)}, u32[]{:S(2)}, u32[]{:S(2)}) collective-permute-start(bf16[512,256]{1,0:T(8,128)(2,1)S(1)} %pad_maximum_fusion.4), channel_id=1, source_target_pairs={{0,3},{1,0},{2,1},{3,2},{4,7},{5,4},{6,5},{7,6},{8,11},{9,8},{10,9... | collective-permute-start | bytes 786440 | tf_op jit(solution)/shard_map/ppermute | solution.py:48
  48.3 17.1 %copy-start.7 = (bf16[128,512]{1,0:T(8,128)(2,1)S(1)}, bf16[128,512]{1,0:T(8,128)(2,1)}, u32[]{:S(2)}) copy-start(bf16[128,512]{1,0:T(8,128)(2,1)} %get-tuple-element.24) | copy-start | bytes 393220
  48.3 17.1 %copy-start.8 = (bf16[128,512]{1,0:T(8,128)(2,1)S(1)}, bf16[128,512]{1,0:T(8,128)(2,1)}, u32[]{:S(2)}) copy-start(bf16[128,512]{1,0:T(8,128)(2,1)} %get-tuple-element.25) | copy-start | bytes 393220
  48.3 17.1 %copy-start.9 = (bf16[128,512]{1,0:T(8,128)(2,1)S(1)}, bf16[128,512]{1,0:T(8,128)(2,1)}, u32[]{:S(2)}) copy-start(bf16[128,512]{1,0:T(8,128)(2,1)} %get-tuple-element.21) | copy-start | bytes 393220
  48.3 12.7 %collective-permute-start.4 = (bf16[512,256]{1,0:T(8,128)(2,1)S(1)}, bf16[512,256]{1,0:T(8,128)(2,1)S(1)}, u32[]{:S(2)}, u32[]{:S(2)}) collective-permute-start(bf16[512,256]{1,0:T(8,128)(2,1)S(1)} %pad_maximum_fusion.3), channel_id=1, source_target_pairs={{0,2},{1,3},{2,0},{3,1},{4,6},{5,7},{6,4},{7,5},{8,10},{9,11},{10,... | collective-permute-start | bytes 786440 | tf_op jit(solution)/shard_map/ppermute | solution.py:48
  51.2 13.9 %collective-permute-start.3 = (bf16[512,256]{1,0:T(8,128)(2,1)S(1)}, bf16[512,256]{1,0:T(8,128)(2,1)S(1)}, u32[]{:S(2)}, u32[]{:S(2)}) collective-permute-start(bf16[512,256]{1,0:T(8,128)(2,1)S(1)} %pad_maximum_fusion.2), channel_id=1, source_target_pairs={{0,1},{1,2},{2,3},{3,0},{4,5},{5,6},{6,7},{7,4},{8,9},{9,10},{10,1... | collective-permute-start | bytes 786440 | tf_op jit(solution)/shard_map/ppermute | solution.py:48
  54.2 11.2 %copy-start.10 = (bf16[128,512]{1,0:T(8,128)(2,1)S(1)}, bf16[128,512]{1,0:T(8,128)(2,1)}, u32[]{:S(2)}) copy-start(bf16[128,512]{1,0:T(8,128)(2,1)} %get-tuple-element.22) | copy-start | bytes 393220
  54.2 11.1 %copy-start.11 = (bf16[128,512]{1,0:T(8,128)(2,1)S(1)}, bf16[128,512]{1,0:T(8,128)(2,1)}, u32[]{:S(2)}) copy-start(bf16[128,512]{1,0:T(8,128)(2,1)} %get-tuple-element.18) | copy-start | bytes 393220
  54.2 11.1 %copy-start.12 = (bf16[128,512]{1,0:T(8,128)(2,1)S(1)}, bf16[128,512]{1,0:T(8,128)(2,1)}, u32[]{:S(2)}) copy-start(bf16[128,512]{1,0:T(8,128)(2,1)} %get-tuple-element.19) | copy-start | bytes 393220
  66.8 19.4 %copy-start.4 = (bf16[1,1,128,512]{3,2,1,0:T(8,128)(2,1)S(1)}, bf16[1,1,128,512]{3,2,1,0:T(8,128)(2,1)}, u32[]{:S(2)}) copy-start(bf16[1,1,128,512]{3,2,1,0:T(8,128)(2,1)} %copy-done.3) | copy-start | bytes 393220
  66.9 19.4 %copy-start.6 = (bf16[128,512]{1,0:T(8,128)(2,1)S(1)}, bf16[128,512]{1,0:T(8,128)(2,1)}, u32[]{:S(2)}) copy-start(bf16[128,512]{1,0:T(8,128)(2,1)} %copy-done.5) | copy-start | bytes 393220
  66.9 11.2 %collective-permute-start.8 = (bf16[512,256]{1,0:T(8,128)(2,1)S(1)}, bf16[512,256]{1,0:T(8,128)(2,1)S(1)}, u32[]{:S(2)}, u32[]{:S(2)}) collective-permute-start(bf16[512,256]{1,0:T(8,128)(2,1)S(1)} %pad_maximum_fusion.7), channel_id=1, source_target_pairs={{0,3},{1,0},{2,1},{3,2},{4,7},{5,4},{6,5},{7,6},{8,11},{9,8},{10,9... | collective-permute-start | bytes 786440 | tf_op jit(solution)/shard_map/ppermute | solution.py:48
  69.5 12.6 %collective-permute-start.7 = (bf16[512,256]{1,0:T(8,128)(2,1)S(1)}, bf16[512,256]{1,0:T(8,128)(2,1)S(1)}, u32[]{:S(2)}, u32[]{:S(2)}) collective-permute-start(bf16[512,256]{1,0:T(8,128)(2,1)S(1)} %pad_maximum_fusion.6), channel_id=1, source_target_pairs={{0,2},{1,3},{2,0},{3,1},{4,6},{5,7},{6,4},{7,5},{8,10},{9,11},{10,... | collective-permute-start | bytes 786440 | tf_op jit(solution)/shard_map/ppermute | solution.py:48
  72.3 13.9 %collective-permute-start.6 = (bf16[512,256]{1,0:T(8,128)(2,1)S(1)}, bf16[512,256]{1,0:T(8,128)(2,1)S(1)}, u32[]{:S(2)}, u32[]{:S(2)}) collective-permute-start(bf16[512,256]{1,0:T(8,128)(2,1)S(1)} %pad_maximum_fusion.5), channel_id=1, source_target_pairs={{0,1},{1,2},{2,3},{3,0},{4,5},{5,6},{6,7},{7,4},{8,9},{9,10},{10,1... | collective-permute-start | bytes 786440 | tf_op jit(solution)/shard_map/ppermute | solution.py:48
  86.9 7.8 %copy-start.1 = (f32[1,2,64,256]{3,2,1,0:T(8,128)S(1)}, f32[1,2,64,256]{3,2,1,0:T(8,128)}, u32[]{:S(2)}) copy-start(f32[1,2,64,256]{3,2,1,0:T(8,128)} %param.14) | copy-start | bytes 393220
  86.9 7.9 %copy-start.2 = (f32[1,2,64,256]{3,2,1,0:T(8,128)S(1)}, f32[1,2,64,256]{3,2,1,0:T(8,128)}, u32[]{:S(2)}) copy-start(f32[1,2,64,256]{3,2,1,0:T(8,128)} %param.13) | copy-start | bytes 393220
  86.9 42.6 %copy-start.13 = (f32[8,192]{1,0:T(8,128)S(1)}, f32[8,192]{1,0:T(8,128)}, u32[]{:S(2)}) copy-start(f32[8,192]{1,0:T(8,128)} %param.16) | copy-start | bytes 18436
  86.9 42.6 %copy-start.16 = (f32[192]{0:T(256)S(1)}, f32[192]{0:T(256)}, u32[]{:S(2)}) copy-start(f32[192]{0:T(256)} %param.15) | copy-start | bytes 2308
  87.8 33.2 %all-to-all-start.1 = ((bf16[8,2,64,256]{3,2,1,0:T(8,128)(2,1)}), bf16[8,2,64,256]{3,2,1,0:T(8,128)(2,1)S(1)}, u32[]{:S(2)}, u32[]{:S(2)}) async-start(bf16[8,2,64,256]{3,2,1,0:T(8,128)(2,1)} %pad_maximum_fusion.1), calls=%async_computation.1 | async-start | bytes 1048576 | tf_op jit(solution)/shard_map/all_to_all | solution.py:136
  95.5 3.1 %collective-permute-start.9 = (f32[16]{0:T(128)S(1)}, f32[16]{0:T(128)S(1)}, u32[]{:S(2)}, u32[]{:S(2)}) collective-permute-start(f32[16]{0:T(128)S(1)} %compare_select_fusion), channel_id=1, source_target_pairs={{0,32},{32,0},{1,33},{33,1},{2,34},{34,2},{3,35},{35,3},{4,36},{36... | collective-permute-start | bytes 200 | tf_op jit(solution)/shard_map/ppermute | solution.py:52
  99.2 5.5 %collective-permute-start.10 = (f32[16]{0:T(128)S(1)}, f32[16]{0:T(128)S(1)}, u32[]{:S(2)}, u32[]{:S(2)}) collective-permute-start(f32[16]{0:T(128)S(1)} %fusion.49), channel_id=1, source_target_pairs={{0,64},{64,0},{128,192},{192,128},{256,320},{320,256},{384,448},{4... | collective-permute-start | bytes 200 | tf_op jit(solution)/shard_map/ppermute | solution.py:52
  105.3 6.4 %collective-permute-start.11 = (f32[16]{0:T(128)S(1)}, f32[16]{0:T(128)S(1)}, u32[]{:S(2)}, u32[]{:S(2)}) collective-permute-start(f32[16]{0:T(128)S(1)} %fusion.50), channel_id=1, source_target_pairs={{0,128},{64,192},{128,0},{192,64},{256,384},{320,448},{384,256},{4... | collective-permute-start | bytes 200 | tf_op jit(solution)/shard_map/ppermute | solution.py:52
  111.7 9.4 %collective-permute-start.12 = (f32[16]{0:T(128)S(1)}, f32[16]{0:T(128)S(1)}, u32[]{:S(2)}, u32[]{:S(2)}) collective-permute-start(f32[16]{0:T(128)S(1)} %add.189), channel_id=1, source_target_pairs={{0,256},{64,320},{128,384},{192,448},{256,0},{320,64},{384,128},{4... | collective-permute-start | bytes 200 | tf_op jit(solution)/shard_map/ppermute | solution.py:52
  121.9 17.3 %all-to-all-start.2 = ((f32[32,1,18]{2,1,0:T(1,128)}), f32[32,1,18]{2,1,0:T(1,128)S(1)}, u32[]{:S(2)}, u32[]{:S(2)}) async-start(f32[32,1,18]{2,1,0:T(1,128)} %broadcast_in_dim.25), calls=%async_computation.2 | async-start | bytes 32768 | tf_op jit(solution)/shard_map/all_to_all | solution.py:20
  140.1 2.8 %copy-start.15 = (f32[8,192]{1,0:T(8,128)S(1)}, f32[8,192]{1,0:T(8,128)}, u32[]{:S(2)}) copy-start(f32[8,192]{1,0:T(8,128)} %param.17) | copy-start | bytes 18436

commit v2 on v1

v2 whole, which is shorter than its diff:
```python
import jax
import jax.numpy as jnp
from jax import lax
from jax.experimental import pallas as pl
from jax.experimental.pallas import tpu as pltpu
from jax.sharding import Mesh, PartitionSpec as P

D = 2048
RANK = 256
HIDDEN = 32

step_size = 0.1
beta_one = 0.9
beta_two = 0.99
norm_eps = 1e-05
grad_eps = 1e-06
down_scale = D ** (-0.5)
up_scale = RANK ** (-0.5)
f32 = jnp.float32
bf16 = jnp.bfloat16
VMEM = pl.BlockSpec(memory_space=pltpu.VMEM)
SMEM = pl.BlockSpec(memory_space=pltpu.SMEM)


def call(kernel, outs, args, flops, name):
    scalars = [a.dtype == jnp.int32 or a.ndim == 1 for a in args]
    moved = sum(a.size * a.dtype.itemsize for a in args)
    return pl.pallas_call(
        kernel,
        out_shape=[jax.ShapeDtypeStruct(s, d) for s, d in outs],
        in_specs=[SMEM if s else VMEM for s in scalars],
        out_specs=[VMEM] * len(outs),
        compiler_params=pltpu.CompilerParams(vmem_limit_bytes=16 * 2**20),
        cost_estimate=pl.CostEstimate(flops=flops, bytes_accessed=moved, transcendentals=0),
        name=name,
    )(*args)


def cut_kernel(place, tokens, targets, gain, *outs):
    block, rows = tokens.shape[0], 64
    lanes = lax.broadcasted_iota(jnp.int32, (block, 128), 1) < rows
    values = tokens[...].astype(f32)
    inverse = lax.rsqrt(jnp.mean(values * values, axis=-1, keepdims=True) + norm_eps)
    for k in range(4):
        x = lax.rem(place[0] + k, 4)
        high, odd = x // 2, lax.rem(x, 2) == 1
        keep = jnp.logical_xor(lanes, odd)
        for q in range(4):
            spots = [pl.ds(pl.multiple_of((2 * q + j) * 256 + high * 128, 128), 128) for j in range(2)]

            def merged(pair):
                a, b = pair
                return jnp.where(
                    keep, jnp.where(odd, b, a), pltpu.roll(jnp.where(odd, a, b), rows, 1)
                )

            out = pl.ds(q * 128, 128)
            toks = [tokens[:, s].astype(f32) for s in spots]
            norms = [t * inverse * gain[:, s] for t, s in zip(toks, spots)]
            outs[k][:, out] = merged(norms).astype(bf16)
            outs[4 + k][0:block, out] = merged(toks).astype(bf16)
            outs[4 + k][block : 2 * block, out] = merged(
                [targets[:, s].astype(f32) for s in spots]
            ).astype(bf16)


def spread(parts, own, sends):
    count = len(parts)
    for i, part in enumerate(parts):
        height = part.shape[0]
        own[i * height : (i + 1) * height, :] = part
        small = part.astype(bf16)
        for k in range(1, count):
            j = (i + k) % count
            sends[k - 1][j * height : (j + 1) * height, :] = small


def first_kernel(n0, n1, n2, n3, gathered, own, s1, s2, s3):
    down_w = gathered[:, 0].reshape(-1, RANK)
    parts = [
        jnp.dot(n[...], down_w, preferred_element_type=f32) * down_scale for n in (n0, n1, n2, n3)
    ]
    spread(parts, own, (s1, s2, s3))


def middle_kernel(
    own, r1, r2, r3, t0, t1, t2, t3, gathered, slope, active_out, upstream_out, loss, back, s1, s2, s3
):
    up_w = gathered[:, 1].reshape(-1, RANK)
    parts, losses = [], 0.0
    for i, t in enumerate((t0, t1, t2, t3)):
        block = t.shape[0] // 2
        at = pl.ds(i * block, block)
        pre = (own[at, :] + r1[at, :].astype(f32)) + (r2[at, :].astype(f32) + r3[at, :].astype(f32))
        logistic = jax.nn.sigmoid(pre)
        slope[at, :] = logistic * (1.0 + pre * (1.0 - logistic))
        active = (pre * logistic).astype(bf16)
        active_out[at, :] = active
        branch = lax.dot_general(
            active, up_w, (((1,), (1,)), ((), ())), preferred_element_type=f32
        )
        residual = (
            t[0:block, :].astype(f32) + branch * up_scale - t[block : 2 * block, :].astype(f32)
        )
        losses = losses + jnp.sum(residual * residual, axis=0, keepdims=True)
        upstream = (2.0 * residual).astype(bf16)
        upstream_out[at, :] = upstream
        parts.append(jnp.dot(upstream, up_w, preferred_element_type=f32) * up_scale)
    loss[...] = losses
    spread(parts, back, (s1, s2, s3))


def last_kernel(own, r1, r2, r3, slope, n0, n1, n2, n3, upstream, active, terms):
    count, _, rows, _ = terms.shape
    total = (own[...] + r1[...].astype(f32)) + (r2[...].astype(f32) + r3[...].astype(f32))
    back = (total * slope[...]).astype(bf16)
    turned = (((0,), (0,)), ((), ()))
    up = lax.dot_general(upstream[...], active[...], turned, preferred_element_type=f32) * up_scale
    terms[:, 1] = up.astype(bf16).reshape(count, rows, RANK)
    down = 0.0
    for i, n in enumerate((n0, n1, n2, n3)):
        block = n.shape[0]
        down = down + lax.dot_general(
            n[...], back[i * block : (i + 1) * block], turned, preferred_element_type=f32
        )
    terms[:, 0] = (down * down_scale).astype(bf16).reshape(count, rows, RANK)


def update_kernel(
    number,
    learned,
    sums,
    gradient,
    weights,
    first,
    second,
    accumulated,
    perturbation,
    new_weights,
    new_first,
    new_second,
    own_loss,
    outer,
):
    total = jnp.sum(sums[...], axis=0, keepdims=True)
    lane = lax.broadcasted_iota(jnp.int32, total.shape, 1)
    elements = weights.shape[0] * weights.shape[1] * weights.shape[2] * sums.shape[0] // 2
    pairs = accumulated.shape[0]
    own_loss[...] = jnp.sum(jnp.where(lane == 2 + number[0], total, 0.0), axis=1, keepdims=True)
    row = lax.broadcasted_iota(jnp.int32, (pairs, total.shape[1]), 0)
    spot = lax.broadcasted_iota(jnp.int32, (pairs, total.shape[1]), 1)
    signs = jnp.where(spot == 2 + 2 * row, 1.0, 0.0) - jnp.where(spot == 3 + 2 * row, 1.0, 0.0)
    difference = jnp.sum(signs * total, axis=1, keepdims=True)
    outer[...] = jnp.sum(
        difference * (accumulated[...] + perturbation[...]), axis=0, keepdims=True
    ) / (2 * pairs)
    chunk = 32
    for half in range(2):
        square = jnp.sum(jnp.where(lane == half, total, 0.0), axis=1, keepdims=True)
        factor = lax.rsqrt(square / elements + grad_eps)
        for start in range(0, weights.shape[1], chunk):
            at = (half, pl.ds(start, chunk))
            weight = weights[at]
            scaled = gradient[at] * factor
            m = beta_one * first[at] + (1.0 - beta_one) * scaled
            v = beta_two * second[at] + (1.0 - beta_two) * scaled * scaled
            new_first[at] = m
            new_second[at] = v
            inverse = lax.rsqrt(v)
            momentum = m * inverse
            speed = scaled * inverse
            out_a = jnp.zeros_like(momentum)
            out_b = jnp.zeros_like(momentum)
            for h in range(HIDDEN):
                act = jnp.tanh(
                    speed * learned[h]
                    + momentum * learned[HIDDEN + h]
                    + weight * learned[2 * HIDDEN + h]
                    + learned[3 * HIDDEN + h]
                )
                out_a = out_a + act * learned[4 * HIDDEN + h]
                out_b = out_b + act * learned[5 * HIDDEN + h]
            new_weights[at] = weight - step_size * (momentum + out_a) * jnp.exp(jnp.tanh(out_b))


def from_everyone(array, axis):
    copies = jnp.broadcast_to(array, (lax.axis_size(axis), *array.shape))
    return lax.all_to_all(copies, axis, split_axis=0, concat_axis=0, tiled=True)


def shift(array, axis, step):
    count = lax.axis_size(axis)
    return lax.ppermute(array, axis, [(i, (i + step) % count) for i in range(count)])


def local(
    tokens,
    targets,
    norm_gain,
    weights,
    first_moment,
    second_moment,
    learned_params,
    perturbation,
    accumulated,
):
    nz, nx = lax.axis_size("z"), lax.axis_size("x")
    particles = lax.axis_size("y") * lax.axis_size("core")
    rows = weights.shape[2]
    block = tokens.shape[0]
    width = nz * rows
    tall = nx * block
    total_tokens = tall * nz
    particle = lax.axis_index("y") * lax.axis_size("core") + lax.axis_index("core")
    polarity = (1 - 2 * (particle % 2)).astype(f32)
    learned = learned_params + polarity * lax.dynamic_index_in_dim(
        perturbation, particle // 2, 0, keepdims=False
    )

    gathered = from_everyone(weights[0].astype(bf16), "z")
    place = lax.axis_index("x").astype(jnp.int32)[None]
    pieces = call(
        cut_kernel,
        [((block, width), bf16)] * 4 + [((2 * block, width), bf16)] * 4,
        (place, tokens, targets, norm_gain[None]),
        20 * block * D,
        "cut",
    )
    normed = [pieces[0]] + [shift(pieces[k], "x", k) for k in range(1, nx)]
    pairs = [pieces[4]] + [shift(pieces[4 + k], "x", k) for k in range(1, nx)]

    wide, thin = ((tall, RANK), f32), ((tall, RANK), bf16)
    product = 2 * tall * width * RANK
    pre, *sends = call(first_kernel, [wide] + [thin] * 3, (*normed, gathered), product, "first")
    sends = [shift(s, "x", k + 1) for k, s in enumerate(sends)]
    slope, active, upstream, loss, back, *sends = call(
        middle_kernel,
        [wide, thin, ((tall, width), bf16), ((1, width), f32), wide] + [thin] * 3,
        (pre, *sends, *pairs, gathered),
        2 * product,
        "middle",
    )
    sends = [shift(s, "x", k + 1) for k, s in enumerate(sends)]
    shares = from_everyone(jnp.sum(loss)[None, None], ("y", "core"))
    sends, shares = lax.optimization_barrier((sends, shares))
    (terms,) = call(
        last_kernel,
        [((nz, 2, rows, RANK), bf16)],
        (back, *sends, slope, *normed, upstream, active),
        2 * product,
        "last",
    )
    gradient = jnp.sum(lax.all_to_all(terms, "z", 0, 0, tiled=True).astype(f32), axis=0)
    squares = jnp.sum(gradient * gradient, axis=(1, 2))
    line = jnp.concatenate([squares, shares.reshape(-1) / (total_tokens * D)])
    line = jnp.pad(line, (0, 128 - line.shape[0]))
    sums = from_everyone(line, ("z", "x"))
    shape = (weights.shape[1], rows, RANK)
    new_w, new_m, new_v, own_loss, outer = call(
        update_kernel,
        [(shape, f32)] * 3 + [((1, 1), f32), ((1, learned.shape[0]), f32)],
        (
            particle.astype(jnp.int32)[None],
            learned,
            sums,
            gradient,
            weights[0],
            first_moment[0],
            second_moment[0],
            accumulated,
            perturbation,
        ),
        400 * weights.size,
        "update",
    )
    return (new_w[None], new_m[None], new_v[None], own_loss.reshape(1), outer.reshape(-1))


def solution(mesh):
    grid = Mesh(mesh.devices.reshape(8, 2, 8, 4), ("y", "core", "z", "x"))
    pop, shard = ("y", "core"), ("z", "x")
    return jax.shard_map(
        local,
        mesh=grid,
        in_specs=(
            P(shard, None),
            P(shard, None),
            P(),
            P(pop, None, shard, None),
            P(pop, None, shard, None),
            P(pop, None, shard, None),
            P(),
            P(),
            P(),
        ),
        out_specs=(
            P(pop, None, shard, None),
            P(pop, None, shard, None),
            P(pop, None, shard, None),
            P(pop),
            P(),
        ),
        check_vma=False,
    )
```

time: 145 us -> 130 us (0.90)
  the two profiles are of different devices: /device:TPU:40 before, /device:TPU:1 now
where the time goes in v2:
time: 130 us; the launch traced here: 129 us
  starting transfers between devices  61.2 us (47%)
  waiting for transfers between devices  34 us (26%)
  blocking collectives  16.5 us (13%)
  Pallas kernels  8.52 us (7%)
  local copies, waits for them, and re-layouts  6.11 us (5%)
  other arithmetic  2 us (2%)
    ppermute x12, starting transfers between devices, shift(): lax.ppermute(array, axis, [(i, (i + step) % count) for i in range(count)])  38.8 us
    all_to_all x1, waiting for transfers between devices, local(): lax.all_to_all(terms, 'z', 0, 0, tiled=True).astype(f32)  17.8 us
    all_to_all x1, blocking collectives, from_everyone(): return lax.all_to_all(copies, axis, split_axis=0, concat_axis=0, tiled=True)  16.5 us
    all_to_all x2, starting transfers between devices, from_everyone(): return lax.all_to_all(copies, axis, split_axis=0, concat_axis=0, tiled=True)  15.7 us
    pallas_call x5, Pallas kernels, call(): pl.pallas_call(kernel, out_shape=[jax.ShapeDtypeStruct(s, d) for s, d in...  8.52 us
    all_to_all x2, waiting for transfers between devices, from_everyone(): return lax.all_to_all(copies, axis, split_axis=0, concat_axis=0, tiled=True)  8.48 us
    ppermute x12, waiting for transfers between devices, shift(): lax.ppermute(array, axis, [(i, (i + step) % count) for i in range(count)])  7.76 us
    all_to_all x1, starting transfers between devices, local(): lax.all_to_all(terms, 'z', 0, 0, tiled=True).astype(f32)  6.65 us
  transfers between devices with their start and end apart: 15, of which 5 were waited for; matrix products, arithmetic and copies ran while one was open for 1% of the time, Pallas kernels for 2%

profile of v2, /device:TPU:1, one launch (start us, length us, event | category | flops | bytes accessed | tf_op | source)
XLA Modules:
  0.0 129.2 jit_solution(4463578761974437574)
XLA Ops:
  0.6 0.9 bitcast_convert_fusion
  1.5 0.9 broadcast_in_dim.31
  2.4 11.0 %all-to-all-start = ((bf16[8,2,64,256]{3,2,1,0:T(8,128)(2,1)}), bf16[8,2,64,256]{3,2,1,0:T(8,128)(2,1)S(1)}, u32[]{:S(2)}, u32[]{:S(2)}) async-start(bf16[8,2,64,256]{3,2,1,0:T(8,128)(2,1)} %broadcast_in_dim.31), calls=%async_computation | async-start | bytes 1048576 | tf_op jit(solution)/shard_map/all_to_all | solution.py:188
  13.4 0.7 copy-done.10
  14.1 1.9 %cut.1 = (bf16[128,512]{1,0:T(8,128)(2,1)S(1)}, bf16[128,512]{1,0:T(8,128)(2,1)S(1)}, bf16[128,512]{1,0:T(8,128)(2,1)S(1)}, bf16[128,512]{1,0:T(8,128)(2,1)S(1)}...) custom-call(s32[1]{0:T(128)} %bitcast.2.place, ...), custom_call_target="tpu_custom_call" | custom-call | flops 5242880 | bytes 1056772 | tf_op jit(solution)/shard_map/cut/pallas_call | solution.py:28
  16.0 3.1 %collective-permute-start.6 = (bf16[256,512]{1,0:T(8,128)(2,1)}, bf16[256,512]{1,0:T(8,128)(2,1)S(1)}, u32[]{:S(2)}, u32[]{:S(2)}) collective-permute-start(bf16[256,512]{1,0:T(8,128)(2,1)} %get-tuple-element.43), channel_id=1, source_target_pairs={{0,1},{1,2},{2,3},{3,0},{4,5},{5,6},{6,7},{7,4},{8,9},{9,10},{10,1... | collective-permute-start | bytes 786440 | tf_op jit(solution)/shard_map/ppermute | solution.py:193
  19.1 3.1 %collective-permute-start = (bf16[128,512]{1,0:T(8,128)(2,1)S(1)}, bf16[128,512]{1,0:T(8,128)(2,1)S(1)}, u32[]{:S(2)}, u32[]{:S(2)}) collective-permute-start(bf16[128,512]{1,0:T(8,128)(2,1)S(1)} %get-tuple-element.35), channel_id=1, source_target_pairs={{0,1},{1,2},{2,3},{3,0},{4,5},{5,6},{6,7},{7,4},{8,9},{9,10},{10,1... | collective-permute-start | bytes 393224 | tf_op jit(solution)/shard_map/ppermute | solution.py:193
  22.2 3.3 %collective-permute-start.1 = (bf16[128,512]{1,0:T(8,128)(2,1)S(1)}, bf16[128,512]{1,0:T(8,128)(2,1)S(1)}, u32[]{:S(2)}, u32[]{:S(2)}) collective-permute-start(bf16[128,512]{1,0:T(8,128)(2,1)S(1)} %get-tuple-element.36), channel_id=1, source_target_pairs={{0,2},{1,3},{2,0},{3,1},{4,6},{5,7},{6,4},{7,5},{8,10},{9,11},{10,... | collective-permute-start | bytes 393224 | tf_op jit(solution)/shard_map/ppermute | solution.py:193
  25.6 3.8 %collective-permute-start.2 = (bf16[128,512]{1,0:T(8,128)(2,1)S(1)}, bf16[128,512]{1,0:T(8,128)(2,1)S(1)}, u32[]{:S(2)}, u32[]{:S(2)}) collective-permute-start(bf16[128,512]{1,0:T(8,128)(2,1)S(1)} %get-tuple-element.37), channel_id=1, source_target_pairs={{0,3},{1,0},{2,1},{3,2},{4,7},{5,4},{6,5},{7,6},{8,11},{9,8},{10,9... | collective-permute-start | bytes 393224 | tf_op jit(solution)/shard_map/ppermute | solution.py:193
  29.4 2.4 %collective-permute-start.7 = (bf16[256,512]{1,0:T(8,128)(2,1)}, bf16[256,512]{1,0:T(8,128)(2,1)S(1)}, u32[]{:S(2)}, u32[]{:S(2)}) collective-permute-start(bf16[256,512]{1,0:T(8,128)(2,1)} %get-tuple-element.44), channel_id=1, source_target_pairs={{0,2},{1,3},{2,0},{3,1},{4,6},{5,7},{6,4},{7,5},{8,10},{9,11},{10,... | collective-permute-start | bytes 786440 | tf_op jit(solution)/shard_map/ppermute | solution.py:193
  31.8 0.0 collective-permute-done.n1
  31.8 3.4 %collective-permute-start.8 = (bf16[256,512]{1,0:T(8,128)(2,1)S(1)}, bf16[256,512]{1,0:T(8,128)(2,1)S(1)}, u32[]{:S(2)}, u32[]{:S(2)}) collective-permute-start(bf16[256,512]{1,0:T(8,128)(2,1)S(1)} %get-tuple-element.45), channel_id=1, source_target_pairs={{0,3},{1,0},{2,1},{3,2},{4,7},{5,4},{6,5},{7,6},{8,11},{9,8},{10,9... | collective-permute-start | bytes 786440 | tf_op jit(solution)/shard_map/ppermute | solution.py:193
  35.2 0.0 collective-permute-done.1.n2
  35.2 0.0 all-to-all-done.gathered
  35.2 0.3 first.1
  35.6 1.9 %collective-permute-start.3 = (bf16[512,256]{1,0:T(8,128)(2,1)S(1)}, bf16[512,256]{1,0:T(8,128)(2,1)S(1)}, u32[]{:S(2)}, u32[]{:S(2)}) collective-permute-start(bf16[512,256]{1,0:T(8,128)(2,1)S(1)} %get-tuple-element.39), channel_id=1, source_target_pairs={{0,1},{1,2},{2,3},{3,0},{4,5},{5,6},{6,7},{7,4},{8,9},{9,10},{10,1... | collective-permute-start | bytes 786440 | tf_op jit(solution)/shard_map/ppermute | solution.py:193
  37.5 4.3 %collective-permute-start.4 = (bf16[512,256]{1,0:T(8,128)(2,1)S(1)}, bf16[512,256]{1,0:T(8,128)(2,1)S(1)}, u32[]{:S(2)}, u32[]{:S(2)}) collective-permute-start(bf16[512,256]{1,0:T(8,128)(2,1)S(1)} %get-tuple-element.40), channel_id=1, source_target_pairs={{0,2},{1,3},{2,0},{3,1},{4,6},{5,7},{6,4},{7,5},{8,10},{9,11},{10,... | collective-permute-start | bytes 786440 | tf_op jit(solution)/shard_map/ppermute | solution.py:193
  41.9 0.0 collective-permute-done.6.t1
  41.9 2.5 %collective-permute-start.5 = (bf16[512,256]{1,0:T(8,128)(2,1)S(1)}, bf16[512,256]{1,0:T(8,128)(2,1)S(1)}, u32[]{:S(2)}, u32[]{:S(2)}) collective-permute-start(bf16[512,256]{1,0:T(8,128)(2,1)S(1)} %get-tuple-element.41), channel_id=1, source_target_pairs={{0,3},{1,0},{2,1},{3,2},{4,7},{5,4},{6,5},{7,6},{8,11},{9,8},{10,9... | collective-permute-start | bytes 786440 | tf_op jit(solution)/shard_map/ppermute | solution.py:193
  44.4 0.0 collective-permute-done.7.t2
  44.4 0.7 copy-done.3
  45.1 0.7 copy-done.5
  45.8 1.3 collective-permute-done.3.r1
  47.1 0.5 collective-permute-done.4.r2
  47.5 6.0 %collective-permute-done.5.r3 = bf16[512,256]{1,0:T(8,128)(2,1)S(1)} collective-permute-done((bf16[512,256]{1,0:T(8,128)(2,1)S(1)}, bf16[512,256]{1,0:T(8,128)(2,1)S(1)}, u32[]{:S(2)}, u32[]{:S(2)}) %collective-permute-start.5) | collective-permute-done | bytes 262176 | tf_op jit(solution)/shard_map/ppermute | solution.py:193
  53.6 0.9 copy-done.4
  54.5 0.9 copy-done.6
  55.5 1.9 %middle.1 = (f32[512,256]{1,0:T(8,128)S(1)}, bf16[512,256]{1,0:T(8,128)(2,1)S(1)}, bf16[512,512]{1,0:T(8,128)(2,1)S(1)}, f32[1,512]{1,0:T(1,128)S(1)}, f32[512,2...) custom-call(f32[512,256]{1,0:T(8,128)S(1)} %get-tuple-element.38.own, ...), custom_call_target="tpu_custom_call" | custom-call | flops 268435456 | bytes 2883584 | tf_op jit(solution)/shard_map/middle/pallas_call | solution.py:28
  57.4 4.4 %collective-permute-start.10 = (bf16[512,256]{1,0:T(8,128)(2,1)}, bf16[512,256]{1,0:T(8,128)(2,1)S(1)}, u32[]{:S(2)}, u32[]{:S(2)}) collective-permute-start(bf16[512,256]{1,0:T(8,128)(2,1)} %get-tuple-element.48), channel_id=1, source_target_pairs={{0,2},{1,3},{2,0},{3,1},{4,6},{5,7},{6,4},{7,5},{8,10},{9,11},{10,... | collective-permute-start | bytes 786440 | tf_op jit(solution)/shard_map/ppermute | solution.py:193
  61.8 4.5 %collective-permute-start.11 = (bf16[512,256]{1,0:T(8,128)(2,1)}, bf16[512,256]{1,0:T(8,128)(2,1)S(1)}, u32[]{:S(2)}, u32[]{:S(2)}) collective-permute-start(bf16[512,256]{1,0:T(8,128)(2,1)} %get-tuple-element.49), channel_id=1, source_target_pairs={{0,3},{1,0},{2,1},{3,2},{4,7},{5,4},{6,5},{7,6},{8,11},{9,8},{10,9... | collective-permute-start | bytes 786440 | tf_op jit(solution)/shard_map/ppermute | solution.py:193
  66.3 1.9 %collective-permute-start.9 = (bf16[512,256]{1,0:T(8,128)(2,1)}, bf16[512,256]{1,0:T(8,128)(2,1)S(1)}, u32[]{:S(2)}, u32[]{:S(2)}) collective-permute-start(bf16[512,256]{1,0:T(8,128)(2,1)} %get-tuple-element.47), channel_id=1, source_target_pairs={{0,1},{1,2},{2,3},{3,0},{4,5},{5,6},{6,7},{7,4},{8,9},{9,10},{10,1... | collective-permute-start | bytes 786440 | tf_op jit(solution)/shard_map/ppermute | solution.py:193
  68.3 0.6 reduce_sum.27
  68.9 0.6 broadcast_in_dim.32
  69.5 16.5 %all_to_all.23 = f32[16,1,1]{2,1,0:T(1,128)S(1)} all-to-all(f32[16,1,1]{2,1,0:T(1,128)S(1)} %broadcast_in_dim.32), channel_id=1, replica_groups=mesh['y'=8,'core'=2,'z'=8,'x'=4] {'y','core'}, dimensions={0} | all-to-all | bytes 128 | tf_op jit(solution)/shard_map/all_to_all | solution.py:188
  86.0 1.4 %last.1 = bf16[8,2,64,256]{3,2,1,0:T(8,128)(2,1)} custom-call(f32[512,256]{1,0:T(8,128)S(1)} %get-tuple-element.46.own, bf16[512,256]{1,0:T(8,128)(2,1)S(1)} %collective-permute-done.9.r1, bf16[512,256]{1,0:T(8,128)(2,1)S(1)} %collective-permute-done.10.r2, bf16[512,256]{1,0:T(8,128)(2,1)S(1)} %collective-permute-done.11.r3, ...), custom_call_target="tpu_custom_call" | custom-call | flops 268435456 | bytes 3145728 | tf_op jit(solution)/shard_map/last/pallas_call | solution.py:28
  87.4 6.6 %all-to-all-start.2 = ((bf16[8,2,64,256]{3,2,1,0:T(8,128)(2,1)}), bf16[8,2,64,256]{3,2,1,0:T(8,128)(2,1)S(1)}, u32[]{:S(2)}, u32[]{:S(2)}) async-start(bf16[8,2,64,256]{3,2,1,0:T(8,128)(2,1)} %last.1), calls=%async_computation.2 | async-start | bytes 1048576 | tf_op jit(solution)/shard_map/all_to_all | solution.py:253
  94.1 0.2 multiply_reduce_fusion.1
  94.3 17.8 %all-to-all-done.2 = bf16[8,2,64,256]{3,2,1,0:T(8,128)(2,1)S(1)} async-done(((bf16[8,2,64,256]{3,2,1,0:T(8,128)(2,1)}), bf16[8,2,64,256]{3,2,1,0:T(8,128)(2,1)S(1)}, u32[]{:S(2)}, u32[]{:S(2)}) %all-to-all-start.2) | async-done | bytes 524320 | tf_op jit(solution)/shard_map/all_to_all | solution.py:253
  112.0 0.1 convert_reduce_fusion.gradient
  112.1 0.0 copy-start.12
  112.1 0.0 copy-start
  112.1 0.1 multiply_reduce_fusion
  112.2 0.1 fusion
  112.3 0.6 broadcast_in_dim.33
  112.9 4.7 %all-to-all-start.3 = ((f32[32,1,128]{2,1,0:T(1,128)}), f32[32,1,128]{2,1,0:T(1,128)S(1)}, u32[]{:S(2)}, u32[]{:S(2)}) async-start(f32[32,1,128]{2,1,0:T(1,128)} %broadcast_in_dim.33), calls=%async_computation.3 | async-start | bytes 32768 | tf_op jit(solution)/shard_map/all_to_all | solution.py:188
  117.7 0.0 copy-start.11
  117.8 8.5 %all-to-all-done.3 = f32[32,1,128]{2,1,0:T(1,128)S(1)} async-done(((f32[32,1,128]{2,1,0:T(1,128)}), f32[32,1,128]{2,1,0:T(1,128)S(1)}, u32[]{:S(2)}, u32[]{:S(2)}) %all-to-all-start.3) | async-done | bytes 16416 | tf_op jit(solution)/shard_map/all_to_all | solution.py:188
  126.3 3.0 %update.1 = (f32[2,64,256]{2,1,0:T(8,128)}, f32[2,64,256]{2,1,0:T(8,128)}, f32[2,64,256]{2,1,0:T(8,128)}, f32[1,1]{1,0:T(1,128)}, f32[1,192]{1,0:T(1,128)}) custom-call(s32[1]{0:T(128)} %bitcast.number, f32[192]{0:T(256)S(1)} %add.20.learned, f32[32,128]{1,0:T(8,128)S(1)} %bitcast.17, f32[2,64,256]{2,1,0:T(8,128)S(1)} %convert_reduce_fusion.gradient, ...), custom_call_target="tpu_custom_call" | custom-call | flops 13107200 | bytes 553732 | tf_op jit(solution)/shard_map/update/pallas_call | solution.py:28
  (25 shorter events, 0.1 us)
Async XLA Ops:
  2.4 11.0 %copy-start.1 = (bf16[128,2048]{1,0:T(8,128)(2,1)S(1)}, bf16[128,2048]{1,0:T(8,128)(2,1)}, u32[]{:S(2)}) copy-start(bf16[128,2048]{1,0:T(8,128)(2,1)} %tokens.1) | copy-start | bytes 1572868
  2.4 11.0 %copy-start.2 = (bf16[128,2048]{1,0:T(8,128)(2,1)S(1)}, bf16[128,2048]{1,0:T(8,128)(2,1)}, u32[]{:S(2)}) copy-start(bf16[128,2048]{1,0:T(8,128)(2,1)} %targets.1) | copy-start | bytes 1572868
  2.4 32.8 %all-to-all-start = ((bf16[8,2,64,256]{3,2,1,0:T(8,128)(2,1)}), bf16[8,2,64,256]{3,2,1,0:T(8,128)(2,1)S(1)}, u32[]{:S(2)}, u32[]{:S(2)}) async-start(bf16[8,2,64,256]{3,2,1,0:T(8,128)(2,1)} %broadcast_in_dim.31), calls=%async_computation | async-start | bytes 1048576 | tf_op jit(solution)/shard_map/all_to_all | solution.py:188
  13.4 0.7 copy-start.10
  16.0 25.9 %collective-permute-start.6 = (bf16[256,512]{1,0:T(8,128)(2,1)}, bf16[256,512]{1,0:T(8,128)(2,1)S(1)}, u32[]{:S(2)}, u32[]{:S(2)}) collective-permute-start(bf16[256,512]{1,0:T(8,128)(2,1)} %get-tuple-element.43), channel_id=1, source_target_pairs={{0,1},{1,2},{2,3},{3,0},{4,5},{5,6},{6,7},{7,4},{8,9},{9,10},{10,1... | collective-permute-start | bytes 786440 | tf_op jit(solution)/shard_map/ppermute | solution.py:193
  19.1 12.7 %collective-permute-start = (bf16[128,512]{1,0:T(8,128)(2,1)S(1)}, bf16[128,512]{1,0:T(8,128)(2,1)S(1)}, u32[]{:S(2)}, u32[]{:S(2)}) collective-permute-start(bf16[128,512]{1,0:T(8,128)(2,1)S(1)} %get-tuple-element.35), channel_id=1, source_target_pairs={{0,1},{1,2},{2,3},{3,0},{4,5},{5,6},{6,7},{7,4},{8,9},{9,10},{10,1... | collective-permute-start | bytes 393224 | tf_op jit(solution)/shard_map/ppermute | solution.py:193
  22.2 13.0 %collective-permute-start.1 = (bf16[128,512]{1,0:T(8,128)(2,1)S(1)}, bf16[128,512]{1,0:T(8,128)(2,1)S(1)}, u32[]{:S(2)}, u32[]{:S(2)}) collective-permute-start(bf16[128,512]{1,0:T(8,128)(2,1)S(1)} %get-tuple-element.36), channel_id=1, source_target_pairs={{0,2},{1,3},{2,0},{3,1},{4,6},{5,7},{6,4},{7,5},{8,10},{9,11},{10,... | collective-permute-start | bytes 393224 | tf_op jit(solution)/shard_map/ppermute | solution.py:193
  25.6 9.6 %collective-permute-start.2 = (bf16[128,512]{1,0:T(8,128)(2,1)S(1)}, bf16[128,512]{1,0:T(8,128)(2,1)S(1)}, u32[]{:S(2)}, u32[]{:S(2)}) collective-permute-start(bf16[128,512]{1,0:T(8,128)(2,1)S(1)} %get-tuple-element.37), channel_id=1, source_target_pairs={{0,3},{1,0},{2,1},{3,2},{4,7},{5,4},{6,5},{7,6},{8,11},{9,8},{10,9... | collective-permute-start | bytes 393224 | tf_op jit(solution)/shard_map/ppermute | solution.py:193
  29.4 15.0 %collective-permute-start.7 = (bf16[256,512]{1,0:T(8,128)(2,1)}, bf16[256,512]{1,0:T(8,128)(2,1)S(1)}, u32[]{:S(2)}, u32[]{:S(2)}) collective-permute-start(bf16[256,512]{1,0:T(8,128)(2,1)} %get-tuple-element.44), channel_id=1, source_target_pairs={{0,2},{1,3},{2,0},{3,1},{4,6},{5,7},{6,4},{7,5},{8,10},{9,11},{10,... | collective-permute-start | bytes 786440 | tf_op jit(solution)/shard_map/ppermute | solution.py:193
  31.8 13.3 %collective-permute-start.8 = (bf16[256,512]{1,0:T(8,128)(2,1)S(1)}, bf16[256,512]{1,0:T(8,128)(2,1)S(1)}, u32[]{:S(2)}, u32[]{:S(2)}) collective-permute-start(bf16[256,512]{1,0:T(8,128)(2,1)S(1)} %get-tuple-element.45), channel_id=1, source_target_pairs={{0,3},{1,0},{2,1},{3,2},{4,7},{5,4},{6,5},{7,6},{8,11},{9,8},{10,9... | collective-permute-start | bytes 786440 | tf_op jit(solution)/shard_map/ppermute | solution.py:193
  35.6 11.5 %collective-permute-start.3 = (bf16[512,256]{1,0:T(8,128)(2,1)S(1)}, bf16[512,256]{1,0:T(8,128)(2,1)S(1)}, u32[]{:S(2)}, u32[]{:S(2)}) collective-permute-start(bf16[512,256]{1,0:T(8,128)(2,1)S(1)} %get-tuple-element.39), channel_id=1, source_target_pairs={{0,1},{1,2},{2,3},{3,0},{4,5},{5,6},{6,7},{7,4},{8,9},{9,10},{10,1... | collective-permute-start | bytes 786440 | tf_op jit(solution)/shard_map/ppermute | solution.py:193
  37.5 10.0 %collective-permute-start.4 = (bf16[512,256]{1,0:T(8,128)(2,1)S(1)}, bf16[512,256]{1,0:T(8,128)(2,1)S(1)}, u32[]{:S(2)}, u32[]{:S(2)}) collective-permute-start(bf16[512,256]{1,0:T(8,128)(2,1)S(1)} %get-tuple-element.40), channel_id=1, source_target_pairs={{0,2},{1,3},{2,0},{3,1},{4,6},{5,7},{6,4},{7,5},{8,10},{9,11},{10,... | collective-permute-start | bytes 786440 | tf_op jit(solution)/shard_map/ppermute | solution.py:193
  41.9 11.7 %collective-permute-start.5 = (bf16[512,256]{1,0:T(8,128)(2,1)S(1)}, bf16[512,256]{1,0:T(8,128)(2,1)S(1)}, u32[]{:S(2)}, u32[]{:S(2)}) collective-permute-start(bf16[512,256]{1,0:T(8,128)(2,1)S(1)} %get-tuple-element.41), channel_id=1, source_target_pairs={{0,3},{1,0},{2,1},{3,2},{4,7},{5,4},{6,5},{7,6},{8,11},{9,8},{10,9... | collective-permute-start | bytes 786440 | tf_op jit(solution)/shard_map/ppermute | solution.py:193
  44.4 0.7 copy-start.3
  45.1 0.7 copy-start.5
  53.6 0.9 copy-start.4
  54.5 0.9 copy-start.6
  57.4 28.6 %collective-permute-start.10 = (bf16[512,256]{1,0:T(8,128)(2,1)}, bf16[512,256]{1,0:T(8,128)(2,1)S(1)}, u32[]{:S(2)}, u32[]{:S(2)}) collective-permute-start(bf16[512,256]{1,0:T(8,128)(2,1)} %get-tuple-element.48), channel_id=1, source_target_pairs={{0,2},{1,3},{2,0},{3,1},{4,6},{5,7},{6,4},{7,5},{8,10},{9,11},{10,... | collective-permute-start | bytes 786440 | tf_op jit(solution)/shard_map/ppermute | solution.py:193
  61.8 24.2 %collective-permute-start.11 = (bf16[512,256]{1,0:T(8,128)(2,1)}, bf16[512,256]{1,0:T(8,128)(2,1)S(1)}, u32[]{:S(2)}, u32[]{:S(2)}) collective-permute-start(bf16[512,256]{1,0:T(8,128)(2,1)} %get-tuple-element.49), channel_id=1, source_target_pairs={{0,3},{1,0},{2,1},{3,2},{4,7},{5,4},{6,5},{7,6},{8,11},{9,8},{10,9... | collective-permute-start | bytes 786440 | tf_op jit(solution)/shard_map/ppermute | solution.py:193
  66.3 19.7 %collective-permute-start.9 = (bf16[512,256]{1,0:T(8,128)(2,1)}, bf16[512,256]{1,0:T(8,128)(2,1)S(1)}, u32[]{:S(2)}, u32[]{:S(2)}) collective-permute-start(bf16[512,256]{1,0:T(8,128)(2,1)} %get-tuple-element.47), channel_id=1, source_target_pairs={{0,1},{1,2},{2,3},{3,0},{4,5},{5,6},{6,7},{7,4},{8,9},{9,10},{10,1... | collective-permute-start | bytes 786440 | tf_op jit(solution)/shard_map/ppermute | solution.py:193
  87.4 24.6 %all-to-all-start.2 = ((bf16[8,2,64,256]{3,2,1,0:T(8,128)(2,1)}), bf16[8,2,64,256]{3,2,1,0:T(8,128)(2,1)S(1)}, u32[]{:S(2)}, u32[]{:S(2)}) async-start(bf16[8,2,64,256]{3,2,1,0:T(8,128)(2,1)} %last.1), calls=%async_computation.2 | async-start | bytes 1048576 | tf_op jit(solution)/shard_map/all_to_all | solution.py:253
  112.0 14.2 %copy-start.7 = (f32[1,2,64,256]{3,2,1,0:T(8,128)S(1)}, f32[1,2,64,256]{3,2,1,0:T(8,128)}, u32[]{:S(2)}) copy-start(f32[1,2,64,256]{3,2,1,0:T(8,128)} %param.13) | copy-start | bytes 393220
  112.0 14.2 %copy-start.8 = (f32[1,2,64,256]{3,2,1,0:T(8,128)S(1)}, f32[1,2,64,256]{3,2,1,0:T(8,128)}, u32[]{:S(2)}) copy-start(f32[1,2,64,256]{3,2,1,0:T(8,128)} %param.14) | copy-start | bytes 393220
  112.1 5.6 %copy-start.12 = (f32[192]{0:T(256)S(1)}, f32[192]{0:T(256)}, u32[]{:S(2)}) copy-start(f32[192]{0:T(256)} %param.15) | copy-start | bytes 2308
  112.1 14.1 %copy-start = (f32[1,2,64,256]{3,2,1,0:T(8,128)S(1)}, f32[1,2,64,256]{3,2,1,0:T(8,128)}, u32[]{:S(2)}) copy-start(f32[1,2,64,256]{3,2,1,0:T(8,128)} %param.12) | copy-start | bytes 393220
  112.9 4.8 %copy-start.9 = (f32[8,192]{1,0:T(8,128)S(1)}, f32[8,192]{1,0:T(8,128)}, u32[]{:S(2)}) copy-start(f32[8,192]{1,0:T(8,128)} %perturbation.1) | copy-start | bytes 18436
  112.9 13.3 %all-to-all-start.3 = ((f32[32,1,128]{2,1,0:T(1,128)}), f32[32,1,128]{2,1,0:T(1,128)S(1)}, u32[]{:S(2)}, u32[]{:S(2)}) async-start(f32[32,1,128]{2,1,0:T(1,128)} %broadcast_in_dim.33), calls=%async_computation.3 | async-start | bytes 32768 | tf_op jit(solution)/shard_map/all_to_all | solution.py:188
  117.7 8.5 %copy-start.11 = (f32[8,192]{1,0:T(8,128)S(1)}, f32[8,192]{1,0:T(8,128)}, u32[]{:S(2)}) copy-start(f32[8,192]{1,0:T(8,128)} %accumulated.1) | copy-start | bytes 18436

commit v3 on v2

--- a/solution.py
+++ b/solution.py
@@ -23,7 +23,7 @@
 
 
 def call(kernel, outs, args, flops, name):
-    scalars = [a.dtype == jnp.int32 or a.ndim == 1 for a in args]
+    scalars = [a.ndim == 1 for a in args]
     moved = sum(a.size * a.dtype.itemsize for a in args)
     return pl.pallas_call(
         kernel,
@@ -36,13 +36,19 @@
     )(*args)
 
 
-def cut_kernel(place, tokens, targets, gain, *outs):
+def copies_kernel(weights, copies):
+    for i in range(copies.shape[0]):
+        copies[i] = weights[...].astype(bf16)
+
+
+def cut_kernel(tokens, targets, gain, *outs):
     block, rows = tokens.shape[0], 64
     lanes = lax.broadcasted_iota(jnp.int32, (block, 128), 1) < rows
+    my_x = lax.axis_index("x")
     values = tokens[...].astype(f32)
     inverse = lax.rsqrt(jnp.mean(values * values, axis=-1, keepdims=True) + norm_eps)
-    for k in range(4):
-        x = lax.rem(place[0] + k, 4)
+    for k, dest in enumerate(outs):
+        x = jnp.bitwise_xor(my_x, k)
         high, odd = x // 2, lax.rem(x, 2) == 1
         keep = jnp.logical_xor(lanes, odd)
         for q in range(4):
@@ -57,11 +63,13 @@
             out = pl.ds(q * 128, 128)
             toks = [tokens[:, s].astype(f32) for s in spots]
             norms = [t * inverse * gain[:, s] for t, s in zip(toks, spots)]
-            outs[k][:, out] = merged(norms).astype(bf16)
-            outs[4 + k][0:block, out] = merged(toks).astype(bf16)
-            outs[4 + k][block : 2 * block, out] = merged(
-                [targets[:, s].astype(f32) for s in spots]
-            ).astype(bf16)
+            gaps = [t - targets[:, s].astype(f32) for t, s in zip(toks, spots)]
+            dest[0:block, out] = merged(norms).astype(bf16)
+            dest[block : 2 * block, out] = merged(gaps).astype(bf16)
+
+
+def particle_index():
+    return lax.axis_index("y") * lax.axis_size("core") + lax.axis_index("core")
 
 
 def spread(parts, own, sends):
@@ -71,14 +79,16 @@
         own[i * height : (i + 1) * height, :] = part
         small = part.astype(bf16)
         for k in range(1, count):
-            j = (i + k) % count
+            j = i ^ k
             sends[k - 1][j * height : (j + 1) * height, :] = small
 
 
 def first_kernel(n0, n1, n2, n3, gathered, own, s1, s2, s3):
     down_w = gathered[:, 0].reshape(-1, RANK)
+    block = n0.shape[0] // 2
     parts = [
-        jnp.dot(n[...], down_w, preferred_element_type=f32) * down_scale for n in (n0, n1, n2, n3)
+        jnp.dot(n[0:block, :], down_w, preferred_element_type=f32) * down_scale
+        for n in (n0, n1, n2, n3)
     ]
     spread(parts, own, (s1, s2, s3))
 
@@ -99,14 +109,14 @@
         branch = lax.dot_general(
             active, up_w, (((1,), (1,)), ((), ())), preferred_element_type=f32
         )
-        residual = (
-            t[0:block, :].astype(f32) + branch * up_scale - t[block : 2 * block, :].astype(f32)
-        )
+        residual = t[block : 2 * block, :].astype(f32) + branch * up_scale
         losses = losses + jnp.sum(residual * residual, axis=0, keepdims=True)
         upstream = (2.0 * residual).astype(bf16)
         upstream_out[at, :] = upstream
         parts.append(jnp.dot(upstream, up_w, preferred_element_type=f32) * up_scale)
-    loss[...] = losses
+    lane = lax.broadcasted_iota(jnp.int32, loss.shape, 1)
+    mean = jnp.sum(losses, axis=1, keepdims=True) / (own.shape[0] * lax.axis_size("z") * D)
+    loss[...] = jnp.where(lane == 2 + particle_index(), mean, 0.0)
     spread(parts, back, (s1, s2, s3))
 
 
@@ -119,15 +129,40 @@
     terms[:, 1] = up.astype(bf16).reshape(count, rows, RANK)
     down = 0.0
     for i, n in enumerate((n0, n1, n2, n3)):
-        block = n.shape[0]
+        block = n.shape[0] // 2
         down = down + lax.dot_general(
-            n[...], back[i * block : (i + 1) * block], turned, preferred_element_type=f32
+            n[0:block, :], back[i * block : (i + 1) * block], turned, preferred_element_type=f32
         )
     terms[:, 0] = (down * down_scale).astype(bf16).reshape(count, rows, RANK)
 
 
+def total_kernel(received, losses, gradient, line):
+    lane = lax.broadcasted_iota(jnp.int32, losses.shape, 1)
+    full = losses[...]
+    for half in range(gradient.shape[0]):
+        total = received[0, half].astype(f32)
+        for i in range(1, received.shape[0]):
+            total = total + received[i, half].astype(f32)
+        gradient[half] = total
+        square = jnp.sum(jnp.sum(total * total, axis=0, keepdims=True), axis=1, keepdims=True)
+        full = full + jnp.where(lane == half, square, 0.0)
+    line[...] = jnp.broadcast_to(full[None], line.shape)
+
+
+def add_kernel(a, b, out):
+    out[...] = a[...] + b[...]
+
+
+def learned_kernel(base, perturbation, out):
+    particle = particle_index()
+    row = lax.broadcasted_iota(jnp.int32, perturbation.shape, 0)
+    own = jnp.sum(
+        jnp.where(row == particle // 2, perturbation[...], 0.0), axis=0, keepdims=True
+    )
+    out[...] = base[...] + jnp.where(lax.rem(particle, 2) == 0, own, -own)
+
+
 def update_kernel(
-    number,
     learned,
     sums,
     gradient,
@@ -142,11 +177,11 @@
     own_loss,
     outer,
 ):
-    total = jnp.sum(sums[...], axis=0, keepdims=True)
+    total = jnp.sum(sums[...], axis=0)
     lane = lax.broadcasted_iota(jnp.int32, total.shape, 1)
     elements = weights.shape[0] * weights.shape[1] * weights.shape[2] * sums.shape[0] // 2
     pairs = accumulated.shape[0]
-    own_loss[...] = jnp.sum(jnp.where(lane == 2 + number[0], total, 0.0), axis=1, keepdims=True)
+    own_loss[...] = jnp.sum(jnp.where(lane == 2 + particle_index(), total, 0.0), axis=1, keepdims=True)
     row = lax.broadcasted_iota(jnp.int32, (pairs, total.shape[1]), 0)
     spot = lax.broadcasted_iota(jnp.int32, (pairs, total.shape[1]), 1)
     signs = jnp.where(spot == 2 + 2 * row, 1.0, 0.0) - jnp.where(spot == 3 + 2 * row, 1.0, 0.0)
@@ -183,14 +218,12 @@
             new_weights[at] = weight - step_size * (momentum + out_a) * jnp.exp(jnp.tanh(out_b))
 
 
-def from_everyone(array, axis):
-    copies = jnp.broadcast_to(array, (lax.axis_size(axis), *array.shape))
-    return lax.all_to_all(copies, axis, split_axis=0, concat_axis=0, tiled=True)
-
-
-def shift(array, axis, step):
-    count = lax.axis_size(axis)
-    return lax.ppermute(array, axis, [(i, (i + step) % count) for i in range(count)])
+def swap(array, axis, mask):
+    return lax.ppermute(array, axis, [(i, i ^ mask) for i in range(lax.axis_size(axis))])
+
+
+def plus(a, b):
+    return call(add_kernel, [(a.shape, a.dtype)], (a, b), a.size, "plus")[0]
 
 
 def local(
@@ -205,62 +238,67 @@
     accumulated,
 ):
     nz, nx = lax.axis_size("z"), lax.axis_size("x")
-    particles = lax.axis_size("y") * lax.axis_size("core")
     rows = weights.shape[2]
     block = tokens.shape[0]
     width = nz * rows
     tall = nx * block
-    total_tokens = tall * nz
-    particle = lax.axis_index("y") * lax.axis_size("core") + lax.axis_index("core")
-    polarity = (1 - 2 * (particle % 2)).astype(f32)
-    learned = learned_params + polarity * lax.dynamic_index_in_dim(
-        perturbation, particle // 2, 0, keepdims=False
-    )
-
-    gathered = from_everyone(weights[0].astype(bf16), "z")
-    place = lax.axis_index("x").astype(jnp.int32)[None]
+    shape = (weights.shape[1], rows, RANK)
+    (copies,) = call(copies_kernel, [((nz, *shape), bf16)], (weights[0],), weights.size, "copies")
+    gathered = lax.all_to_all(copies, "z", 0, 0, tiled=True)
     pieces = call(
         cut_kernel,
-        [((block, width), bf16)] * 4 + [((2 * block, width), bf16)] * 4,
-        (place, tokens, targets, norm_gain[None]),
+        [((2 * block, width), bf16)] * nx,
+        (tokens, targets, norm_gain[None]),
         20 * block * D,
         "cut",
     )
-    normed = [pieces[0]] + [shift(pieces[k], "x", k) for k in range(1, nx)]
-    pairs = [pieces[4]] + [shift(pieces[4 + k], "x", k) for k in range(1, nx)]
+    pieces = [pieces[0]] + [swap(pieces[k], "x", k) for k in range(1, nx)]
 
     wide, thin = ((tall, RANK), f32), ((tall, RANK), bf16)
     product = 2 * tall * width * RANK
-    pre, *sends = call(first_kernel, [wide] + [thin] * 3, (*normed, gathered), product, "first")
-    sends = [shift(s, "x", k + 1) for k, s in enumerate(sends)]
+    pre, *sends = call(first_kernel, [wide] + [thin] * 3, (*pieces, gathered), product, "first")
+    sends = [swap(s, "x", k + 1) for k, s in enumerate(sends)]
     slope, active, upstream, loss, back, *sends = call(
         middle_kernel,
-        [wide, thin, ((tall, width), bf16), ((1, width), f32), wide] + [thin] * 3,
-        (pre, *sends, *pairs, gathered),
+        [wide, thin, ((tall, width), bf16), ((1, 128), f32), wide] + [thin] * 3,
+        (pre, *sends, *pieces, gathered),
         2 * product,
         "middle",
     )
-    sends = [shift(s, "x", k + 1) for k, s in enumerate(sends)]
-    shares = from_everyone(jnp.sum(loss)[None, None], ("y", "core"))
-    sends, shares = lax.optimization_barrier((sends, shares))
+    sends = [swap(s, "x", k + 1) for k, s in enumerate(sends)]
+    loss = plus(loss, swap(loss, "core", 1))
+    loss = plus(loss, swap(loss, "y", 1))
+    sends, loss = lax.optimization_barrier((sends, loss))
     (terms,) = call(
         last_kernel,
-        [((nz, 2, rows, RANK), bf16)],
-        (back, *sends, slope, *normed, upstream, active),
+        [((nz, *shape), bf16)],
+        (back, *sends, slope, *pieces, upstream, active),
         2 * product,
         "last",
     )
-    gradient = jnp.sum(lax.all_to_all(terms, "z", 0, 0, tiled=True).astype(f32), axis=0)
-    squares = jnp.sum(gradient * gradient, axis=(1, 2))
-    line = jnp.concatenate([squares, shares.reshape(-1) / (total_tokens * D)])
-    line = jnp.pad(line, (0, 128 - line.shape[0]))
-    sums = from_everyone(line, ("z", "x"))
-    shape = (weights.shape[1], rows, RANK)
+    terms = lax.all_to_all(terms, "z", 0, 0, tiled=True)
+    loss = plus(loss, swap(loss, "y", 2))
+    loss = plus(loss, swap(loss, "y", 4))
+    gradient, line = call(
+        total_kernel,
+        [(shape, f32), ((nz * nx, 1, 128), f32)],
+        (terms, loss),
+        10 * terms.size,
+        "total",
+    )
+    sums = lax.all_to_all(line, ("z", "x"), 0, 0, tiled=True)
+    (learned,) = call(
+        learned_kernel,
+        [((1, learned_params.shape[0]), f32)],
+        (learned_params[None], perturbation),
+        10 * perturbation.size,
+        "learned",
+    )
+    learned = learned.reshape(-1)
     new_w, new_m, new_v, own_loss, outer = call(
         update_kernel,
         [(shape, f32)] * 3 + [((1, 1), f32), ((1, learned.shape[0]), f32)],
         (
-            particle.astype(jnp.int32)[None],
             learned,
             sums,
             gradient,

time: 130 us -> 128 us (0.985)
  the two profiles are of different devices: /device:TPU:1 before, /device:TPU:32 now
where the time goes in v3:
time: 128 us; the launch traced here: 127 us
  starting transfers between devices  63.5 us (50%)
  waiting for transfers between devices  52.8 us (41%)
  Pallas kernels  8.39 us (7%)
  local copies, waits for them, and re-layouts  1.59 us (1%)
    ppermute x13, waiting for transfers between devices, swap(): lax.ppermute(array, axis, [(i, i ^ mask) for i in range(lax.axis_size(axi...  42 us
    ppermute x13, starting transfers between devices, swap(): lax.ppermute(array, axis, [(i, i ^ mask) for i in range(lax.axis_size(axi...  40.5 us
    all_to_all x1, starting transfers between devices, local(): gathered = lax.all_to_all(copies, 'z', 0, 0, tiled=True)  10.4 us
    all_to_all x1, waiting for transfers between devices, local(): sums = lax.all_to_all(line, ('z', 'x'), 0, 0, tiled=True)  8.98 us
    pallas_call x12, Pallas kernels, call(): pl.pallas_call(kernel, out_shape=[jax.ShapeDtypeStruct(s, d) for s, d in...  8.39 us
    all_to_all x1, starting transfers between devices, local(): terms = lax.all_to_all(terms, 'z', 0, 0, tiled=True)  6.45 us
    all_to_all x1, starting transfers between devices, local(): sums = lax.all_to_all(line, ('z', 'x'), 0, 0, tiled=True)  6.09 us
  transfers between devices with their start and end apart: 16, of which 13 were waited for; matrix products, arithmetic and copies ran while one was open for 0% of the time, Pallas kernels for 1%

profile of v3, /device:TPU:32, one launch (start us, length us, event | category | flops | bytes accessed | tf_op | source)
XLA Modules:
  0.0 127.1 jit_solution(2169587942966791869)
XLA Ops:
  0.6 0.0 copy-start
  0.6 0.9 copy-done
  1.5 0.8 copies.1
  2.4 10.4 %all-to-all-start = ((bf16[8,2,64,256]{3,2,1,0:T(8,128)(2,1)}), bf16[8,2,64,256]{3,2,1,0:T(8,128)(2,1)S(1)}, u32[]{:S(2)}, u32[]{:S(2)}) async-start(bf16[8,2,64,256]{3,2,1,0:T(8,128)(2,1)} %copies.1), calls=%async_computation | async-start | bytes 1048576 | tf_op jit(solution)/shard_map/all_to_all | solution.py:247
  12.8 0.0 copy-done.7
  12.8 0.0 copy-done.2
  12.8 0.0 copy-done.3
  12.8 1.0 cut.1
  13.9 3.4 %collective-permute-start = (bf16[256,512]{1,0:T(8,128)(2,1)S(1)}, bf16[256,512]{1,0:T(8,128)(2,1)S(1)}, u32[]{:S(2)}, u32[]{:S(2)}) collective-permute-start(bf16[256,512]{1,0:T(8,128)(2,1)S(1)} %get-tuple-element.33), channel_id=1, source_target_pairs={{0,1},{1,0},{2,3},{3,2},{4,5},{5,4},{6,7},{7,6},{8,9},{9,8},{10,11... | collective-permute-start | bytes 786440 | tf_op jit(solution)/shard_map/ppermute | solution.py:222
  17.3 4.6 %collective-permute-start.1 = (bf16[256,512]{1,0:T(8,128)(2,1)S(1)}, bf16[256,512]{1,0:T(8,128)(2,1)S(1)}, u32[]{:S(2)}, u32[]{:S(2)}) collective-permute-start(bf16[256,512]{1,0:T(8,128)(2,1)S(1)} %get-tuple-element.34), channel_id=1, source_target_pairs={{0,2},{1,3},{2,0},{3,1},{4,6},{5,7},{6,4},{7,5},{8,10},{9,11},{10,... | collective-permute-start | bytes 786440 | tf_op jit(solution)/shard_map/ppermute | solution.py:222
  21.9 2.4 %collective-permute-start.2 = (bf16[256,512]{1,0:T(8,128)(2,1)S(1)}, bf16[256,512]{1,0:T(8,128)(2,1)S(1)}, u32[]{:S(2)}, u32[]{:S(2)}) collective-permute-start(bf16[256,512]{1,0:T(8,128)(2,1)S(1)} %get-tuple-element.35), channel_id=1, source_target_pairs={{0,3},{1,2},{2,1},{3,0},{4,7},{5,6},{6,5},{7,4},{8,11},{9,10},{10,... | collective-permute-start | bytes 786440 | tf_op jit(solution)/shard_map/ppermute | solution.py:222
  24.3 0.6 collective-permute-done.n1.t1
  24.9 6.5 %collective-permute-done.1.n2.t2 = bf16[256,512]{1,0:T(8,128)(2,1)S(1)} collective-permute-done((bf16[256,512]{1,0:T(8,128)(2,1)S(1)}, bf16[256,512]{1,0:T(8,128)(2,1)S(1)}, u32[]{:S(2)}, u32[]{:S(2)}) %collective-permute-start.1) | collective-permute-done | bytes 262176 | tf_op jit(solution)/shard_map/ppermute | solution.py:222
  31.4 5.3 %collective-permute-done.2.n3.t3 = bf16[256,512]{1,0:T(8,128)(2,1)S(1)} collective-permute-done((bf16[256,512]{1,0:T(8,128)(2,1)S(1)}, bf16[256,512]{1,0:T(8,128)(2,1)S(1)}, u32[]{:S(2)}, u32[]{:S(2)}) %collective-permute-start.2) | collective-permute-done | bytes 262176 | tf_op jit(solution)/shard_map/ppermute | solution.py:222
  36.7 0.0 all-to-all-done.gathered
  36.7 0.3 first.1
  37.0 1.9 %collective-permute-start.3 = (bf16[512,256]{1,0:T(8,128)(2,1)S(1)}, bf16[512,256]{1,0:T(8,128)(2,1)S(1)}, u32[]{:S(2)}, u32[]{:S(2)}) collective-permute-start(bf16[512,256]{1,0:T(8,128)(2,1)S(1)} %get-tuple-element.37), channel_id=1, source_target_pairs={{0,1},{1,0},{2,3},{3,2},{4,5},{5,4},{6,7},{7,6},{8,9},{9,8},{10,11... | collective-permute-start | bytes 786440 | tf_op jit(solution)/shard_map/ppermute | solution.py:222
  39.0 3.8 %collective-permute-start.4 = (bf16[512,256]{1,0:T(8,128)(2,1)S(1)}, bf16[512,256]{1,0:T(8,128)(2,1)S(1)}, u32[]{:S(2)}, u32[]{:S(2)}) collective-permute-start(bf16[512,256]{1,0:T(8,128)(2,1)S(1)} %get-tuple-element.38), channel_id=1, source_target_pairs={{0,2},{1,3},{2,0},{3,1},{4,6},{5,7},{6,4},{7,5},{8,10},{9,11},{10,... | collective-permute-start | bytes 786440 | tf_op jit(solution)/shard_map/ppermute | solution.py:222
  42.8 4.7 %collective-permute-start.5 = (bf16[512,256]{1,0:T(8,128)(2,1)S(1)}, bf16[512,256]{1,0:T(8,128)(2,1)S(1)}, u32[]{:S(2)}, u32[]{:S(2)}) collective-permute-start(bf16[512,256]{1,0:T(8,128)(2,1)S(1)} %get-tuple-element.39), channel_id=1, source_target_pairs={{0,3},{1,2},{2,1},{3,0},{4,7},{5,6},{6,5},{7,4},{8,11},{9,10},{10,... | collective-permute-start | bytes 786440 | tf_op jit(solution)/shard_map/ppermute | solution.py:222
  47.5 0.6 collective-permute-done.3.r1
  48.1 4.4 %collective-permute-done.4.r2 = bf16[512,256]{1,0:T(8,128)(2,1)S(1)} collective-permute-done((bf16[512,256]{1,0:T(8,128)(2,1)S(1)}, bf16[512,256]{1,0:T(8,128)(2,1)S(1)}, u32[]{:S(2)}, u32[]{:S(2)}) %collective-permute-start.4) | collective-permute-done | bytes 262176 | tf_op jit(solution)/shard_map/ppermute | solution.py:222
  52.5 5.4 %collective-permute-done.5.r3 = bf16[512,256]{1,0:T(8,128)(2,1)S(1)} collective-permute-done((bf16[512,256]{1,0:T(8,128)(2,1)S(1)}, bf16[512,256]{1,0:T(8,128)(2,1)S(1)}, u32[]{:S(2)}, u32[]{:S(2)}) %collective-permute-start.5) | collective-permute-done | bytes 262176 | tf_op jit(solution)/shard_map/ppermute | solution.py:222
  57.9 1.0 middle.1
  58.9 1.9 %collective-permute-start.6 = (bf16[512,256]{1,0:T(8,128)(2,1)S(1)}, bf16[512,256]{1,0:T(8,128)(2,1)S(1)}, u32[]{:S(2)}, u32[]{:S(2)}) collective-permute-start(bf16[512,256]{1,0:T(8,128)(2,1)S(1)} %get-tuple-element.41), channel_id=1, source_target_pairs={{0,1},{1,0},{2,3},{3,2},{4,5},{5,4},{6,7},{7,6},{8,9},{9,8},{10,11... | collective-permute-start | bytes 786440 | tf_op jit(solution)/shard_map/ppermute | solution.py:222
  60.8 6.1 %collective-permute-start.7 = (bf16[512,256]{1,0:T(8,128)(2,1)S(1)}, bf16[512,256]{1,0:T(8,128)(2,1)S(1)}, u32[]{:S(2)}, u32[]{:S(2)}) collective-permute-start(bf16[512,256]{1,0:T(8,128)(2,1)S(1)} %get-tuple-element.42), channel_id=1, source_target_pairs={{0,2},{1,3},{2,0},{3,1},{4,6},{5,7},{6,4},{7,5},{8,10},{9,11},{10,... | collective-permute-start | bytes 786440 | tf_op jit(solution)/shard_map/ppermute | solution.py:222
  66.9 2.4 %collective-permute-start.8 = (bf16[512,256]{1,0:T(8,128)(2,1)S(1)}, bf16[512,256]{1,0:T(8,128)(2,1)S(1)}, u32[]{:S(2)}, u32[]{:S(2)}) collective-permute-start(bf16[512,256]{1,0:T(8,128)(2,1)S(1)} %get-tuple-element.43), channel_id=1, source_target_pairs={{0,3},{1,2},{2,1},{3,0},{4,7},{5,6},{6,5},{7,4},{8,11},{9,10},{10,... | collective-permute-start | bytes 786440 | tf_op jit(solution)/shard_map/ppermute | solution.py:222
  69.3 1.9 %collective-permute-start.9 = (f32[1,128]{1,0:T(1,128)S(1)}, f32[1,128]{1,0:T(1,128)S(1)}, u32[]{:S(2)}, u32[]{:S(2)}) collective-permute-start(f32[1,128]{1,0:T(1,128)S(1)} %get-tuple-element.44.a), channel_id=1, source_target_pairs={{0,32},{32,0},{1,33},{33,1},{2,34},{34,2},{3,35},{35,3},{4,36},{36... | collective-permute-start | bytes 1544 | tf_op jit(solution)/shard_map/ppermute | solution.py:222
  71.2 1.1 collective-permute-done.9.b
  72.4 2.6 %collective-permute-start.10 = (f32[1,128]{1,0:T(1,128)S(1)}, f32[1,128]{1,0:T(1,128)S(1)}, u32[]{:S(2)}, u32[]{:S(2)}) collective-permute-start(f32[1,128]{1,0:T(1,128)S(1)} %plus.4.a), channel_id=1, source_target_pairs={{0,64},{64,0},{128,192},{192,128},{256,320},{320,256},{384,448},{4... | collective-permute-start | bytes 1544 | tf_op jit(solution)/shard_map/ppermute | solution.py:222
  75.0 2.9 %collective-permute-done.10.b = f32[1,128]{1,0:T(1,128)S(1)} collective-permute-done((f32[1,128]{1,0:T(1,128)S(1)}, f32[1,128]{1,0:T(1,128)S(1)}, u32[]{:S(2)}, u32[]{:S(2)}) %collective-permute-start.10) | collective-permute-done | bytes 544 | tf_op jit(solution)/shard_map/ppermute | solution.py:222
  77.8 0.0 collective-permute-done.6.r1
  77.8 0.0 collective-permute-done.7.r2
  77.8 4.3 %collective-permute-done.8.r3 = bf16[512,256]{1,0:T(8,128)(2,1)S(1)} collective-permute-done((bf16[512,256]{1,0:T(8,128)(2,1)S(1)}, bf16[512,256]{1,0:T(8,128)(2,1)S(1)}, u32[]{:S(2)}, u32[]{:S(2)}) %collective-permute-start.8) | collective-permute-done | bytes 262176 | tf_op jit(solution)/shard_map/ppermute | solution.py:222
  82.1 1.4 %last.1 = bf16[8,2,64,256]{3,2,1,0:T(8,128)(2,1)} custom-call(f32[512,256]{1,0:T(8,128)S(1)} %get-tuple-element.40.own, bf16[512,256]{1,0:T(8,128)(2,1)S(1)} %collective-permute-done.6.r1, bf16[512,256]{1,0:T(8,128)(2,1)S(1)} %collective-permute-done.7.r2, bf16[512,256]{1,0:T(8,128)(2,1)S(1)} %collective-permute-done.8.r3, ...), custom_call_target="tpu_custom_call" | custom-call | flops 268435456 | bytes 3670016 | tf_op jit(solution)/shard_map/last/pallas_call | solution.py:28
  83.6 6.5 %all-to-all-start.1 = ((bf16[8,2,64,256]{3,2,1,0:T(8,128)(2,1)}), bf16[8,2,64,256]{3,2,1,0:T(8,128)(2,1)S(1)}, u32[]{:S(2)}, u32[]{:S(2)}) async-start(bf16[8,2,64,256]{3,2,1,0:T(8,128)(2,1)} %last.1), calls=%async_computation.1 | async-start | bytes 1048576 | tf_op jit(solution)/shard_map/all_to_all | solution.py:279
  90.0 2.7 %collective-permute-start.11 = (f32[1,128]{1,0:T(1,128)S(1)}, f32[1,128]{1,0:T(1,128)S(1)}, u32[]{:S(2)}, u32[]{:S(2)}) collective-permute-start(f32[1,128]{1,0:T(1,128)S(1)} %plus.5.a), channel_id=1, source_target_pairs={{0,128},{64,192},{128,0},{192,64},{256,384},{320,448},{384,256},{4... | collective-permute-start | bytes 1544 | tf_op jit(solution)/shard_map/ppermute | solution.py:222
  92.7 3.6 %collective-permute-done.11.b = f32[1,128]{1,0:T(1,128)S(1)} collective-permute-done((f32[1,128]{1,0:T(1,128)S(1)}, f32[1,128]{1,0:T(1,128)S(1)}, u32[]{:S(2)}, u32[]{:S(2)}) %collective-permute-start.11) | collective-permute-done | bytes 544 | tf_op jit(solution)/shard_map/ppermute | solution.py:222
  96.4 2.0 %collective-permute-start.12 = (f32[1,128]{1,0:T(1,128)S(1)}, f32[1,128]{1,0:T(1,128)S(1)}, u32[]{:S(2)}, u32[]{:S(2)}) collective-permute-start(f32[1,128]{1,0:T(1,128)S(1)} %plus.6.a), channel_id=1, source_target_pairs={{0,256},{64,320},{128,384},{192,448},{256,0},{320,64},{384,128},{4... | collective-permute-start | bytes 1544 | tf_op jit(solution)/shard_map/ppermute | solution.py:222
  98.4 7.3 %collective-permute-done.12.b = f32[1,128]{1,0:T(1,128)S(1)} collective-permute-done((f32[1,128]{1,0:T(1,128)S(1)}, f32[1,128]{1,0:T(1,128)S(1)}, u32[]{:S(2)}, u32[]{:S(2)}) %collective-permute-start.12) | collective-permute-done | bytes 544 | tf_op jit(solution)/shard_map/ppermute | solution.py:222
  105.7 1.8 %all-to-all-done.1.received = bf16[8,2,64,256]{3,2,1,0:T(8,128)(2,1)S(1)} async-done(((bf16[8,2,64,256]{3,2,1,0:T(8,128)(2,1)}), bf16[8,2,64,256]{3,2,1,0:T(8,128)(2,1)S(1)}, u32[]{:S(2)}, u32[]{:S(2)}) %all-to-all-start.1) | async-done | bytes 524320 | tf_op jit(solution)/shard_map/all_to_all | solution.py:279
  107.6 0.8 total.1
  108.3 6.1 %all-to-all-start.2 = ((f32[32,1,128]{2,1,0:T(1,128)}), f32[32,1,128]{2,1,0:T(1,128)S(1)}, u32[]{:S(2)}, u32[]{:S(2)}) async-start(f32[32,1,128]{2,1,0:T(1,128)} %get-tuple-element.52), calls=%async_computation.2 | async-start | bytes 32768 | tf_op jit(solution)/shard_map/all_to_all | solution.py:289
  114.4 0.0 copy-start.9
  114.5 0.7 copy-done.9
  115.1 9.0 %all-to-all-done.2.sums = f32[32,1,128]{2,1,0:T(1,128)S(1)} async-done(((f32[32,1,128]{2,1,0:T(1,128)}), f32[32,1,128]{2,1,0:T(1,128)S(1)}, u32[]{:S(2)}, u32[]{:S(2)}) %all-to-all-start.2) | async-done | bytes 16416 | tf_op jit(solution)/shard_map/all_to_all | solution.py:289
  124.1 0.0 copy-done.5
  124.1 0.0 copy-done.8
  124.1 3.0 %update.1 = (f32[2,64,256]{2,1,0:T(8,128)}, f32[2,64,256]{2,1,0:T(8,128)}, f32[2,64,256]{2,1,0:T(8,128)}, f32[1,1]{1,0:T(1,128)}, f32[1,192]{1,0:T(1,128)}) custom-call(f32[192]{0:T(256)S(1)} %bitcast.16, f32[32,1,128]{2,1,0:T(1,128)S(1)} %all-to-all-done.2.sums, f32[2,64,256]{2,1,0:T(8,128)S(1)} %get-tuple-element.53.gradient, f32[2,64,256]{2,1,0:T(8,128)S(1)} %bitcast.12, ...), custom_call_target="tpu_custom_call" | custom-call | flops 13107200 | bytes 553728 | tf_op jit(solution)/shard_map/update/pallas_call | solution.py:28
  (16 shorter events, 0.1 us)
Async XLA Ops:
  0.6 0.9 copy-start
  1.5 11.3 %copy-start.7 = (f32[2048]{0:T(1024)S(1)}, f32[2048]{0:T(1024)}, u32[]{:S(2)}) copy-start(f32[2048]{0:T(1024)} %param.11) | copy-start | bytes 24580
  2.4 10.5 %copy-start.2 = (bf16[128,2048]{1,0:T(8,128)(2,1)S(1)}, bf16[128,2048]{1,0:T(8,128)(2,1)}, u32[]{:S(2)}) copy-start(bf16[128,2048]{1,0:T(8,128)(2,1)} %tokens.1) | copy-start | bytes 1572868
  2.4 10.5 %copy-start.3 = (bf16[128,2048]{1,0:T(8,128)(2,1)S(1)}, bf16[128,2048]{1,0:T(8,128)(2,1)}, u32[]{:S(2)}) copy-start(bf16[128,2048]{1,0:T(8,128)(2,1)} %targets.1) | copy-start | bytes 1572868
  2.4 34.3 %all-to-all-start = ((bf16[8,2,64,256]{3,2,1,0:T(8,128)(2,1)}), bf16[8,2,64,256]{3,2,1,0:T(8,128)(2,1)S(1)}, u32[]{:S(2)}, u32[]{:S(2)}) async-start(bf16[8,2,64,256]{3,2,1,0:T(8,128)(2,1)} %copies.1), calls=%async_computation | async-start | bytes 1048576 | tf_op jit(solution)/shard_map/all_to_all | solution.py:247
  13.9 11.1 %collective-permute-start = (bf16[256,512]{1,0:T(8,128)(2,1)S(1)}, bf16[256,512]{1,0:T(8,128)(2,1)S(1)}, u32[]{:S(2)}, u32[]{:S(2)}) collective-permute-start(bf16[256,512]{1,0:T(8,128)(2,1)S(1)} %get-tuple-element.33), channel_id=1, source_target_pairs={{0,1},{1,0},{2,3},{3,2},{4,5},{5,4},{6,7},{7,6},{8,9},{9,8},{10,11... | collective-permute-start | bytes 786440 | tf_op jit(solution)/shard_map/ppermute | solution.py:222
  17.3 14.2 %collective-permute-start.1 = (bf16[256,512]{1,0:T(8,128)(2,1)S(1)}, bf16[256,512]{1,0:T(8,128)(2,1)S(1)}, u32[]{:S(2)}, u32[]{:S(2)}) collective-permute-start(bf16[256,512]{1,0:T(8,128)(2,1)S(1)} %get-tuple-element.34), channel_id=1, source_target_pairs={{0,2},{1,3},{2,0},{3,1},{4,6},{5,7},{6,4},{7,5},{8,10},{9,11},{10,... | collective-permute-start | bytes 786440 | tf_op jit(solution)/shard_map/ppermute | solution.py:222
  21.9 14.8 %collective-permute-start.2 = (bf16[256,512]{1,0:T(8,128)(2,1)S(1)}, bf16[256,512]{1,0:T(8,128)(2,1)S(1)}, u32[]{:S(2)}, u32[]{:S(2)}) collective-permute-start(bf16[256,512]{1,0:T(8,128)(2,1)S(1)} %get-tuple-element.35), channel_id=1, source_target_pairs={{0,3},{1,2},{2,1},{3,0},{4,7},{5,6},{6,5},{7,4},{8,11},{9,10},{10,... | collective-permute-start | bytes 786440 | tf_op jit(solution)/shard_map/ppermute | solution.py:222
  37.0 11.1 %collective-permute-start.3 = (bf16[512,256]{1,0:T(8,128)(2,1)S(1)}, bf16[512,256]{1,0:T(8,128)(2,1)S(1)}, u32[]{:S(2)}, u32[]{:S(2)}) collective-permute-start(bf16[512,256]{1,0:T(8,128)(2,1)S(1)} %get-tuple-element.37), channel_id=1, source_target_pairs={{0,1},{1,0},{2,3},{3,2},{4,5},{5,4},{6,7},{7,6},{8,9},{9,8},{10,11... | collective-permute-start | bytes 786440 | tf_op jit(solution)/shard_map/ppermute | solution.py:222
  39.0 13.6 %collective-permute-start.4 = (bf16[512,256]{1,0:T(8,128)(2,1)S(1)}, bf16[512,256]{1,0:T(8,128)(2,1)S(1)}, u32[]{:S(2)}, u32[]{:S(2)}) collective-permute-start(bf16[512,256]{1,0:T(8,128)(2,1)S(1)} %get-tuple-element.38), channel_id=1, source_target_pairs={{0,2},{1,3},{2,0},{3,1},{4,6},{5,7},{6,4},{7,5},{8,10},{9,11},{10,... | collective-permute-start | bytes 786440 | tf_op jit(solution)/shard_map/ppermute | solution.py:222
  42.8 15.1 %collective-permute-start.5 = (bf16[512,256]{1,0:T(8,128)(2,1)S(1)}, bf16[512,256]{1,0:T(8,128)(2,1)S(1)}, u32[]{:S(2)}, u32[]{:S(2)}) collective-permute-start(bf16[512,256]{1,0:T(8,128)(2,1)S(1)} %get-tuple-element.39), channel_id=1, source_target_pairs={{0,3},{1,2},{2,1},{3,0},{4,7},{5,6},{6,5},{7,4},{8,11},{9,10},{10,... | collective-permute-start | bytes 786440 | tf_op jit(solution)/shard_map/ppermute | solution.py:222
  58.9 19.0 %collective-permute-start.6 = (bf16[512,256]{1,0:T(8,128)(2,1)S(1)}, bf16[512,256]{1,0:T(8,128)(2,1)S(1)}, u32[]{:S(2)}, u32[]{:S(2)}) collective-permute-start(bf16[512,256]{1,0:T(8,128)(2,1)S(1)} %get-tuple-element.41), channel_id=1, source_target_pairs={{0,1},{1,0},{2,3},{3,2},{4,5},{5,4},{6,7},{7,6},{8,9},{9,8},{10,11... | collective-permute-start | bytes 786440 | tf_op jit(solution)/shard_map/ppermute | solution.py:222
  60.8 17.0 %collective-permute-start.7 = (bf16[512,256]{1,0:T(8,128)(2,1)S(1)}, bf16[512,256]{1,0:T(8,128)(2,1)S(1)}, u32[]{:S(2)}, u32[]{:S(2)}) collective-permute-start(bf16[512,256]{1,0:T(8,128)(2,1)S(1)} %get-tuple-element.42), channel_id=1, source_target_pairs={{0,2},{1,3},{2,0},{3,1},{4,6},{5,7},{6,4},{7,5},{8,10},{9,11},{10,... | collective-permute-start | bytes 786440 | tf_op jit(solution)/shard_map/ppermute | solution.py:222
  66.9 15.2 %collective-permute-start.8 = (bf16[512,256]{1,0:T(8,128)(2,1)S(1)}, bf16[512,256]{1,0:T(8,128)(2,1)S(1)}, u32[]{:S(2)}, u32[]{:S(2)}) collective-permute-start(bf16[512,256]{1,0:T(8,128)(2,1)S(1)} %get-tuple-element.43), channel_id=1, source_target_pairs={{0,3},{1,2},{2,1},{3,0},{4,7},{5,6},{6,5},{7,4},{8,11},{9,10},{10,... | collective-permute-start | bytes 786440 | tf_op jit(solution)/shard_map/ppermute | solution.py:222
  69.3 3.1 %collective-permute-start.9 = (f32[1,128]{1,0:T(1,128)S(1)}, f32[1,128]{1,0:T(1,128)S(1)}, u32[]{:S(2)}, u32[]{:S(2)}) collective-permute-start(f32[1,128]{1,0:T(1,128)S(1)} %get-tuple-element.44.a), channel_id=1, source_target_pairs={{0,32},{32,0},{1,33},{33,1},{2,34},{34,2},{3,35},{35,3},{4,36},{36... | collective-permute-start | bytes 1544 | tf_op jit(solution)/shard_map/ppermute | solution.py:222
  72.4 5.5 %collective-permute-start.10 = (f32[1,128]{1,0:T(1,128)S(1)}, f32[1,128]{1,0:T(1,128)S(1)}, u32[]{:S(2)}, u32[]{:S(2)}) collective-permute-start(f32[1,128]{1,0:T(1,128)S(1)} %plus.4.a), channel_id=1, source_target_pairs={{0,64},{64,0},{128,192},{192,128},{256,320},{320,256},{384,448},{4... | collective-permute-start | bytes 1544 | tf_op jit(solution)/shard_map/ppermute | solution.py:222
  83.6 24.0 %all-to-all-start.1 = ((bf16[8,2,64,256]{3,2,1,0:T(8,128)(2,1)}), bf16[8,2,64,256]{3,2,1,0:T(8,128)(2,1)S(1)}, u32[]{:S(2)}, u32[]{:S(2)}) async-start(bf16[8,2,64,256]{3,2,1,0:T(8,128)(2,1)} %last.1), calls=%async_computation.1 | async-start | bytes 1048576 | tf_op jit(solution)/shard_map/all_to_all | solution.py:279
  90.0 6.3 %collective-permute-start.11 = (f32[1,128]{1,0:T(1,128)S(1)}, f32[1,128]{1,0:T(1,128)S(1)}, u32[]{:S(2)}, u32[]{:S(2)}) collective-permute-start(f32[1,128]{1,0:T(1,128)S(1)} %plus.5.a), channel_id=1, source_target_pairs={{0,128},{64,192},{128,0},{192,64},{256,384},{320,448},{384,256},{4... | collective-permute-start | bytes 1544 | tf_op jit(solution)/shard_map/ppermute | solution.py:222
  96.4 9.4 %collective-permute-start.12 = (f32[1,128]{1,0:T(1,128)S(1)}, f32[1,128]{1,0:T(1,128)S(1)}, u32[]{:S(2)}, u32[]{:S(2)}) collective-permute-start(f32[1,128]{1,0:T(1,128)S(1)} %plus.6.a), channel_id=1, source_target_pairs={{0,256},{64,320},{128,384},{192,448},{256,0},{320,64},{384,128},{4... | collective-permute-start | bytes 1544 | tf_op jit(solution)/shard_map/ppermute | solution.py:222
  107.6 16.6 %copy-start.1 = (f32[1,2,64,256]{3,2,1,0:T(8,128)S(1)}, f32[1,2,64,256]{3,2,1,0:T(8,128)}, u32[]{:S(2)}) copy-start(f32[1,2,64,256]{3,2,1,0:T(8,128)} %param.12) | copy-start | bytes 393220
  107.6 16.6 %copy-start.4 = (f32[1,2,64,256]{3,2,1,0:T(8,128)S(1)}, f32[1,2,64,256]{3,2,1,0:T(8,128)}, u32[]{:S(2)}) copy-start(f32[1,2,64,256]{3,2,1,0:T(8,128)} %param.13) | copy-start | bytes 393220
  107.6 16.6 %copy-start.5 = (f32[1,2,64,256]{3,2,1,0:T(8,128)S(1)}, f32[1,2,64,256]{3,2,1,0:T(8,128)}, u32[]{:S(2)}) copy-start(f32[1,2,64,256]{3,2,1,0:T(8,128)} %param.14) | copy-start | bytes 393220
  108.3 6.1 %copy-start.6 = (f32[8,192]{1,0:T(8,128)S(1)}, f32[8,192]{1,0:T(8,128)}, u32[]{:S(2)}) copy-start(f32[8,192]{1,0:T(8,128)} %perturbation.3) | copy-start | bytes 18436
  108.3 15.8 %all-to-all-start.2 = ((f32[32,1,128]{2,1,0:T(1,128)}), f32[32,1,128]{2,1,0:T(1,128)S(1)}, u32[]{:S(2)}, u32[]{:S(2)}) async-start(f32[32,1,128]{2,1,0:T(1,128)} %get-tuple-element.52), calls=%async_computation.2 | async-start | bytes 32768 | tf_op jit(solution)/shard_map/all_to_all | solution.py:289
  114.4 0.7 copy-start.9
  115.1 9.0 %copy-start.8 = (f32[8,192]{1,0:T(8,128)S(1)}, f32[8,192]{1,0:T(8,128)}, u32[]{:S(2)}) copy-start(f32[8,192]{1,0:T(8,128)} %accumulated.1) | copy-start | bytes 18436

commit v4 on v3

--- a/solution.py
+++ b/solution.py
@@ -22,7 +22,7 @@
 SMEM = pl.BlockSpec(memory_space=pltpu.SMEM)
 
 
-def call(kernel, outs, args, flops, name):
+def call(kernel, outs, args, flops, name, scratch=()):
     scalars = [a.ndim == 1 for a in args]
     moved = sum(a.size * a.dtype.itemsize for a in args)
     return pl.pallas_call(
@@ -30,6 +30,7 @@
         out_shape=[jax.ShapeDtypeStruct(s, d) for s, d in outs],
         in_specs=[SMEM if s else VMEM for s in scalars],
         out_specs=[VMEM] * len(outs),
+        scratch_shapes=[pltpu.VMEM(s, d) for s, d in scratch],
         compiler_params=pltpu.CompilerParams(vmem_limit_bytes=16 * 2**20),
         cost_estimate=pl.CostEstimate(flops=flops, bytes_accessed=moved, transcendentals=0),
         name=name,
@@ -42,66 +43,66 @@
 
 
 def cut_kernel(tokens, targets, gain, *outs):
-    block, rows = tokens.shape[0], 64
-    lanes = lax.broadcasted_iota(jnp.int32, (block, 128), 1) < rows
+    block, tile = tokens.shape[0], 128
     my_x = lax.axis_index("x")
+    outer = my_x // 2 == lax.rem(my_x, 2)
+    lanes = lax.broadcasted_iota(jnp.int32, (block, tile), 1) < tile // 2
     values = tokens[...].astype(f32)
     inverse = lax.rsqrt(jnp.mean(values * values, axis=-1, keepdims=True) + norm_eps)
-    for k, dest in enumerate(outs):
-        x = jnp.bitwise_xor(my_x, k)
-        high, odd = x // 2, lax.rem(x, 2) == 1
-        keep = jnp.logical_xor(lanes, odd)
-        for q in range(4):
-            spots = [pl.ds(pl.multiple_of((2 * q + j) * 256 + high * 128, 128), 128) for j in range(2)]
-
-            def merged(pair):
-                a, b = pair
-                return jnp.where(
-                    keep, jnp.where(odd, b, a), pltpu.roll(jnp.where(odd, a, b), rows, 1)
-                )
-
-            out = pl.ds(q * 128, 128)
-            toks = [tokens[:, s].astype(f32) for s in spots]
-            norms = [t * inverse * gain[:, s] for t, s in zip(toks, spots)]
-            gaps = [t - targets[:, s].astype(f32) for t, s in zip(toks, spots)]
-            dest[0:block, out] = merged(norms).astype(bf16)
-            dest[block : 2 * block, out] = merged(gaps).astype(bf16)
+    for q in range(tokens.shape[1] // (2 * tile)):
+        norms, gaps = [], []
+        for j in range(2):
+            at = slice((2 * q + j) * tile, (2 * q + j + 1) * tile)
+            token = tokens[:, at].astype(f32)
+            norms.append((token * inverse * gain[:, at]).astype(bf16).astype(f32))
+            gaps.append(token - targets[:, at].astype(f32))
+        out = slice(q * tile, (q + 1) * tile)
+        for k, dest in enumerate(outs):
+            first = jnp.logical_xor(lanes, outer if k else jnp.logical_not(outer))
+            dest[0:block, out] = jnp.where(first, *norms).astype(bf16)
+            dest[block : 2 * block, out] = jnp.where(first, *gaps).astype(bf16)
+
+
+def split_kernel(gathered, down_w, up_w):
+    down_w[...] = gathered[:, 0]
+    up_w[...] = gathered[:, 1]
+
+
+def halves():
+    half = lax.rem(lax.axis_index("x"), 2)
+    rows = 64
+    return [pl.ds(pl.multiple_of(h * rows, rows), rows) for h in (half, 1 - half)]
 
 
 def particle_index():
     return lax.axis_index("y") * lax.axis_size("core") + lax.axis_index("core")
 
 
-def spread(parts, own, sends):
-    count = len(parts)
-    for i, part in enumerate(parts):
-        height = part.shape[0]
-        own[i * height : (i + 1) * height, :] = part
-        small = part.astype(bf16)
-        for k in range(1, count):
-            j = i ^ k
-            sends[k - 1][j * height : (j + 1) * height, :] = small
-
-
-def first_kernel(n0, n1, n2, n3, gathered, own, s1, s2, s3):
-    down_w = gathered[:, 0].reshape(-1, RANK)
+def joined(mine, theirs, full):
+    own, other = halves()
+    full[:, own] = mine[...]
+    full[:, other] = theirs[...]
+    return full[...].reshape(-1, full.shape[-1])
+
+
+def first_kernel(n0, n1, mine, theirs, own, send, full):
+    down_w = joined(mine, theirs, full)
     block = n0.shape[0] // 2
-    parts = [
-        jnp.dot(n[0:block, :], down_w, preferred_element_type=f32) * down_scale
-        for n in (n0, n1, n2, n3)
-    ]
-    spread(parts, own, (s1, s2, s3))
+    for i, n in enumerate((n0, n1)):
+        part = jnp.dot(n[0:block, :], down_w, preferred_element_type=f32) * down_scale
+        own[i * block : (i + 1) * block, :] = part
+        send[(1 - i) * block : (2 - i) * block, :] = part.astype(bf16)
 
 
 def middle_kernel(
-    own, r1, r2, r3, t0, t1, t2, t3, gathered, slope, active_out, upstream_out, loss, back, s1, s2, s3
+    own, received, d0, d1, mine, theirs, slope, active_out, upstream_out, loss, back, send, full
 ):
-    up_w = gathered[:, 1].reshape(-1, RANK)
-    parts, losses = [], 0.0
-    for i, t in enumerate((t0, t1, t2, t3)):
-        block = t.shape[0] // 2
-        at = pl.ds(i * block, block)
-        pre = (own[at, :] + r1[at, :].astype(f32)) + (r2[at, :].astype(f32) + r3[at, :].astype(f32))
+    up_w = joined(mine, theirs, full)
+    losses = 0.0
+    block = d0.shape[0] // 2
+    for i, d in enumerate((d0, d1)):
+        at = slice(i * block, (i + 1) * block)
+        pre = own[at, :] + received[at, :].astype(f32)
         logistic = jax.nn.sigmoid(pre)
         slope[at, :] = logistic * (1.0 + pre * (1.0 - logistic))
         active = (pre * logistic).astype(bf16)
@@ -109,31 +110,49 @@
         branch = lax.dot_general(
             active, up_w, (((1,), (1,)), ((), ())), preferred_element_type=f32
         )
-        residual = t[block : 2 * block, :].astype(f32) + branch * up_scale
+        residual = d[block : 2 * block, :].astype(f32) + branch * up_scale
         losses = losses + jnp.sum(residual * residual, axis=0, keepdims=True)
         upstream = (2.0 * residual).astype(bf16)
         upstream_out[at, :] = upstream
-        parts.append(jnp.dot(upstream, up_w, preferred_element_type=f32) * up_scale)
+        part = jnp.dot(upstream, up_w, preferred_element_type=f32) * up_scale
+        back[at, :] = part
+        send[(1 - i) * block : (2 - i) * block, :] = part.astype(bf16)
     lane = lax.broadcasted_iota(jnp.int32, loss.shape, 1)
-    mean = jnp.sum(losses, axis=1, keepdims=True) / (own.shape[0] * lax.axis_size("z") * D)
+    tokens = own.shape[0] * (lax.axis_size("x") // 2) * lax.axis_size("z")
+    mean = jnp.sum(losses, axis=1, keepdims=True) / (tokens * D)
     loss[...] = jnp.where(lane == 2 + particle_index(), mean, 0.0)
-    spread(parts, back, (s1, s2, s3))
-
-
-def last_kernel(own, r1, r2, r3, slope, n0, n1, n2, n3, upstream, active, terms):
-    count, _, rows, _ = terms.shape
-    total = (own[...] + r1[...].astype(f32)) + (r2[...].astype(f32) + r3[...].astype(f32))
-    back = (total * slope[...]).astype(bf16)
+
+
+def parted(product, mine, theirs, full):
+    own, other = halves()
+    full[...] = product.reshape(full.shape)
+    mine[...] = full[:, own]
+    theirs[...] = full[:, other].astype(bf16)
+
+
+def up_kernel(upstream, active, mine, theirs, full):
     turned = (((0,), (0,)), ((), ()))
-    up = lax.dot_general(upstream[...], active[...], turned, preferred_element_type=f32) * up_scale
-    terms[:, 1] = up.astype(bf16).reshape(count, rows, RANK)
+    up = lax.dot_general(upstream[...], active[...], turned, preferred_element_type=f32)
+    parted(up * up_scale, mine, theirs, full)
+
+
+def down_kernel(own, received, slope, n0, n1, mine, theirs, full):
+    back = ((own[...] + received[...].astype(f32)) * slope[...]).astype(bf16)
     down = 0.0
-    for i, n in enumerate((n0, n1, n2, n3)):
+    for i, n in enumerate((n0, n1)):
         block = n.shape[0] // 2
         down = down + lax.dot_general(
-            n[0:block, :], back[i * block : (i + 1) * block], turned, preferred_element_type=f32
+            n[0:block, :],
+            back[i * block : (i + 1) * block],
+            (((0,), (0,)), ((), ())),
+            preferred_element_type=f32,
         )
-    terms[:, 0] = (down * down_scale).astype(bf16).reshape(count, rows, RANK)
+    parted(down * down_scale, mine, theirs, full)
+
+
+def terms_kernel(down, down_in, up, up_in, terms):
+    terms[:, 0] = (down[...] + down_in[...].astype(f32)).astype(bf16)
+    terms[:, 1] = (up[...] + up_in[...].astype(f32)).astype(bf16)
 
 
 def total_kernel(received, losses, gradient, line):
@@ -240,41 +259,50 @@
     nz, nx = lax.axis_size("z"), lax.axis_size("x")
     rows = weights.shape[2]
     block = tokens.shape[0]
-    width = nz * rows
-    tall = nx * block
+    width = 2 * nz * rows
+    tall = 2 * block
     shape = (weights.shape[1], rows, RANK)
+    column = (nz, rows, RANK)
+    full = (nz, 2 * rows, RANK)
     (copies,) = call(copies_kernel, [((nz, *shape), bf16)], (weights[0],), weights.size, "copies")
     gathered = lax.all_to_all(copies, "z", 0, 0, tiled=True)
-    pieces = call(
+    piece, send = call(
         cut_kernel,
-        [((2 * block, width), bf16)] * nx,
+        [((2 * block, width), bf16)] * 2,
         (tokens, targets, norm_gain[None]),
         20 * block * D,
         "cut",
     )
-    pieces = [pieces[0]] + [swap(pieces[k], "x", k) for k in range(1, nx)]
+    pieces = (piece, swap(send, "x", 1))
+    down_w, up_w = call(split_kernel, [(column, bf16)] * 2, (gathered,), gathered.size, "split")
+    down_w, up_w = (down_w, swap(down_w, "x", 3)), (up_w, swap(up_w, "x", 3))
 
     wide, thin = ((tall, RANK), f32), ((tall, RANK), bf16)
     product = 2 * tall * width * RANK
-    pre, *sends = call(first_kernel, [wide] + [thin] * 3, (*pieces, gathered), product, "first")
-    sends = [swap(s, "x", k + 1) for k, s in enumerate(sends)]
-    slope, active, upstream, loss, back, *sends = call(
+    joint, sums_of = [(full, bf16)], [(full, f32)]
+    pre, send = call(first_kernel, [wide, thin], (*pieces, *down_w), product, "first", joint)
+    slope, active, upstream, loss, back, send = call(
         middle_kernel,
-        [wide, thin, ((tall, width), bf16), ((1, 128), f32), wide] + [thin] * 3,
-        (pre, *sends, *pieces, gathered),
+        [wide, thin, ((tall, width), bf16), ((1, 128), f32), wide, thin],
+        (pre, swap(send, "x", 1), *pieces, *up_w),
         2 * product,
         "middle",
-    )
-    sends = [swap(s, "x", k + 1) for k, s in enumerate(sends)]
+        joint,
+    )
+    received = swap(send, "x", 1)
+    parts = [(column, f32), (column, bf16)]
+    up, send_up = call(up_kernel, parts, (upstream, active), product, "up", sums_of)
+    up_in = swap(send_up, "x", 3)
     loss = plus(loss, swap(loss, "core", 1))
+    received, _, loss = lax.optimization_barrier((received, send_up, loss))
+    down, send_down = call(
+        down_kernel, parts, (back, received, slope, *pieces), product, "down", sums_of
+    )
+    down_in = swap(send_down, "x", 3)
     loss = plus(loss, swap(loss, "y", 1))
-    sends, loss = lax.optimization_barrier((sends, loss))
+    down_in, loss = lax.optimization_barrier((down_in, loss))
     (terms,) = call(
-        last_kernel,
-        [((nz, *shape), bf16)],
-        (back, *sends, slope, *pieces, upstream, active),
-        2 * product,
-        "last",
+        terms_kernel, [((nz, *shape), bf16)], (down, down_in, up, up_in), 4 * down.size, "terms"
     )
     terms = lax.all_to_all(terms, "z", 0, 0, tiled=True)
     loss = plus(loss, swap(loss, "y", 2))

time: 128 us -> 118 us (0.922)
  the two profiles are of different devices: /device:TPU:32 before, /device:TPU:48 now
where the time goes in v4:
time: 118 us; the launch traced here: 117 us
  starting transfers between devices  57.3 us (49%)
  waiting for transfers between devices  49 us (42%)
  Pallas kernels  8.56 us (7%)
  local copies, waits for them, and re-layouts  1.59 us (1%)
    ppermute x11, starting transfers between devices, swap(): lax.ppermute(array, axis, [(i, i ^ mask) for i in range(lax.axis_size(axi...  34.2 us
    ppermute x11, waiting for transfers between devices, swap(): lax.ppermute(array, axis, [(i, i ^ mask) for i in range(lax.axis_size(axi...  25.8 us
    all_to_all x1, waiting for transfers between devices, local(): gathered = lax.all_to_all(copies, 'z', 0, 0, tiled=True)  13.5 us
    all_to_all x1, starting transfers between devices, local(): gathered = lax.all_to_all(copies, 'z', 0, 0, tiled=True)  10.4 us
    all_to_all x1, starting transfers between devices, local(): sums = lax.all_to_all(line, ('z', 'x'), 0, 0, tiled=True)  9.08 us
    all_to_all x1, waiting for transfers between devices, local(): sums = lax.all_to_all(line, ('z', 'x'), 0, 0, tiled=True)  8.98 us
    pallas_call x15, Pallas kernels, call(): pl.pallas_call(kernel, out_shape=[jax.ShapeDtypeStruct(s, d) for s, d in...  8.56 us
    all_to_all x1, starting transfers between devices, local(): terms = lax.all_to_all(terms, 'z', 0, 0, tiled=True)  3.49 us
  transfers between devices with their start and end apart: 14, of which 12 were waited for; matrix products, arithmetic and copies ran while one was open for 0% of the time, Pallas kernels for 1%

profile of v4, /device:TPU:48, one launch (start us, length us, event | category | flops | bytes accessed | tf_op | source)
XLA Modules:
  0.0 117.2 jit_solution(15690804425192563287)
XLA Ops:
  0.6 0.0 copy-start
  0.6 0.9 copy-done
  1.5 0.8 copies.1
  2.4 10.4 %all-to-all-start = ((bf16[8,2,64,256]{3,2,1,0:T(8,128)(2,1)}), bf16[8,2,64,256]{3,2,1,0:T(8,128)(2,1)S(1)}, u32[]{:S(2)}, u32[]{:S(2)}) async-start(bf16[8,2,64,256]{3,2,1,0:T(8,128)(2,1)} %copies.1), calls=%async_computation | async-start | bytes 1048576 | tf_op jit(solution)/shard_map/all_to_all | solution.py:268
  12.8 0.0 copy-done.7
  12.8 0.0 copy-done.2
  12.8 0.0 copy-done.3
  12.9 0.6 cut.1
  13.5 3.4 %collective-permute-start = (bf16[256,1024]{1,0:T(8,128)(2,1)S(1)}, bf16[256,1024]{1,0:T(8,128)(2,1)S(1)}, u32[]{:S(2)}, u32[]{:S(2)}) collective-permute-start(bf16[256,1024]{1,0:T(8,128)(2,1)S(1)} %get-tuple-element.33), channel_id=1, source_target_pairs={{0,1},{1,0},{2,3},{3,2},{4,5},{5,4},{6,7},{7,6},{8,9},{9,8},{10,11... | collective-permute-start | bytes 1572872 | tf_op jit(solution)/shard_map/ppermute | solution.py:241
  16.9 13.5 %all-to-all-done.gathered = bf16[8,2,64,256]{3,2,1,0:T(8,128)(2,1)S(1)} async-done(((bf16[8,2,64,256]{3,2,1,0:T(8,128)(2,1)}), bf16[8,2,64,256]{3,2,1,0:T(8,128)(2,1)S(1)}, u32[]{:S(2)}, u32[]{:S(2)}) %all-to-all-start) | async-done | bytes 524320 | tf_op jit(solution)/shard_map/all_to_all | solution.py:268
  30.4 4.7 %collective-permute-start.1 = (bf16[8,64,256]{2,1,0:T(8,128)(2,1)S(1)}, bf16[8,64,256]{2,1,0:T(8,128)(2,1)S(1)}, u32[]{:S(2)}, u32[]{:S(2)}) collective-permute-start(bf16[8,64,256]{2,1,0:T(8,128)(2,1)S(1)} %get-tuple-element.34.mine), channel_id=1, source_target_pairs={{0,3},{1,2},{2,1},{3,0},{4,7},{5,6},{6,5},{7,4},{8,11},{9,10},{10,... | collective-permute-start | bytes 786440 | tf_op jit(solution)/shard_map/ppermute | solution.py:241
  35.0 2.4 %collective-permute-start.3 = (bf16[8,64,256]{2,1,0:T(8,128)(2,1)S(1)}, bf16[8,64,256]{2,1,0:T(8,128)(2,1)S(1)}, u32[]{:S(2)}, u32[]{:S(2)}) collective-permute-start(bf16[8,64,256]{2,1,0:T(8,128)(2,1)S(1)} %get-tuple-element.37.mine), channel_id=1, source_target_pairs={{0,3},{1,2},{2,1},{3,0},{4,7},{5,6},{6,5},{7,4},{8,11},{9,10},{10,... | collective-permute-start | bytes 786440 | tf_op jit(solution)/shard_map/ppermute | solution.py:241
  37.4 0.0 collective-permute-done.n1.d1
  37.4 5.2 %collective-permute-done.1.theirs = bf16[8,64,256]{2,1,0:T(8,128)(2,1)S(1)} collective-permute-done((bf16[8,64,256]{2,1,0:T(8,128)(2,1)S(1)}, bf16[8,64,256]{2,1,0:T(8,128)(2,1)S(1)}, u32[]{:S(2)}, u32[]{:S(2)}) %collective-permute-start.1) | collective-permute-done | bytes 262176 | tf_op jit(solution)/shard_map/ppermute | solution.py:241
  42.6 0.4 first.1
  43.0 2.2 %collective-permute-start.2 = (bf16[256,256]{1,0:T(8,128)(2,1)S(1)}, bf16[256,256]{1,0:T(8,128)(2,1)S(1)}, u32[]{:S(2)}, u32[]{:S(2)}) collective-permute-start(bf16[256,256]{1,0:T(8,128)(2,1)S(1)} %get-tuple-element.36), channel_id=1, source_target_pairs={{0,1},{1,0},{2,3},{3,2},{4,5},{5,4},{6,7},{7,6},{8,9},{9,8},{10,11... | collective-permute-start | bytes 393224 | tf_op jit(solution)/shard_map/ppermute | solution.py:241
  45.2 2.1 %collective-permute-done.3.theirs = bf16[8,64,256]{2,1,0:T(8,128)(2,1)S(1)} collective-permute-done((bf16[8,64,256]{2,1,0:T(8,128)(2,1)S(1)}, bf16[8,64,256]{2,1,0:T(8,128)(2,1)S(1)}, u32[]{:S(2)}, u32[]{:S(2)}) %collective-permute-start.3) | collective-permute-done | bytes 262176 | tf_op jit(solution)/shard_map/ppermute | solution.py:241
  47.3 2.6 %collective-permute-done.2.received = bf16[256,256]{1,0:T(8,128)(2,1)S(1)} collective-permute-done((bf16[256,256]{1,0:T(8,128)(2,1)S(1)}, bf16[256,256]{1,0:T(8,128)(2,1)S(1)}, u32[]{:S(2)}, u32[]{:S(2)}) %collective-permute-start.2) | collective-permute-done | bytes 131104 | tf_op jit(solution)/shard_map/ppermute | solution.py:241
  49.9 0.8 middle.1
  50.7 2.2 %collective-permute-start.4 = (bf16[256,256]{1,0:T(8,128)(2,1)S(1)}, bf16[256,256]{1,0:T(8,128)(2,1)S(1)}, u32[]{:S(2)}, u32[]{:S(2)}) collective-permute-start(bf16[256,256]{1,0:T(8,128)(2,1)S(1)} %get-tuple-element.39), channel_id=1, source_target_pairs={{0,1},{1,0},{2,3},{3,2},{4,5},{5,4},{6,7},{7,6},{8,9},{9,8},{10,11... | collective-permute-start | bytes 393224 | tf_op jit(solution)/shard_map/ppermute | solution.py:241
  52.9 1.9 %collective-permute-start.5 = (f32[1,128]{1,0:T(1,128)S(1)}, f32[1,128]{1,0:T(1,128)S(1)}, u32[]{:S(2)}, u32[]{:S(2)}) collective-permute-start(f32[1,128]{1,0:T(1,128)S(1)} %get-tuple-element.43.a), channel_id=1, source_target_pairs={{0,32},{32,0},{1,33},{33,1},{2,34},{34,2},{3,35},{35,3},{4,36},{36... | collective-permute-start | bytes 1544 | tf_op jit(solution)/shard_map/ppermute | solution.py:241
  54.8 0.5 up.1
  55.3 0.6 collective-permute-done.5.b
  55.9 1.6 %collective-permute-done.4.received = bf16[256,256]{1,0:T(8,128)(2,1)S(1)} collective-permute-done((bf16[256,256]{1,0:T(8,128)(2,1)S(1)}, bf16[256,256]{1,0:T(8,128)(2,1)S(1)}, u32[]{:S(2)}, u32[]{:S(2)}) %collective-permute-start.4) | collective-permute-done | bytes 131104 | tf_op jit(solution)/shard_map/ppermute | solution.py:241
  57.5 0.7 down.1
  58.3 4.7 %collective-permute-start.6 = (bf16[8,64,256]{2,1,0:T(8,128)(2,1)S(1)}, bf16[8,64,256]{2,1,0:T(8,128)(2,1)S(1)}, u32[]{:S(2)}, u32[]{:S(2)}) collective-permute-start(bf16[8,64,256]{2,1,0:T(8,128)(2,1)S(1)} %get-tuple-element.47), channel_id=1, source_target_pairs={{0,3},{1,2},{2,1},{3,0},{4,7},{5,6},{6,5},{7,4},{8,11},{9,10},{10,... | collective-permute-start | bytes 786440 | tf_op jit(solution)/shard_map/ppermute | solution.py:241
  63.0 2.4 %collective-permute-start.8 = (bf16[8,64,256]{2,1,0:T(8,128)(2,1)S(1)}, bf16[8,64,256]{2,1,0:T(8,128)(2,1)S(1)}, u32[]{:S(2)}, u32[]{:S(2)}) collective-permute-start(bf16[8,64,256]{2,1,0:T(8,128)(2,1)S(1)} %get-tuple-element.42), channel_id=1, source_target_pairs={{0,3},{1,2},{2,1},{3,0},{4,7},{5,6},{6,5},{7,4},{8,11},{9,10},{10,... | collective-permute-start | bytes 786440 | tf_op jit(solution)/shard_map/ppermute | solution.py:241
  65.3 2.6 %collective-permute-start.7 = (f32[1,128]{1,0:T(1,128)S(1)}, f32[1,128]{1,0:T(1,128)S(1)}, u32[]{:S(2)}, u32[]{:S(2)}) collective-permute-start(f32[1,128]{1,0:T(1,128)S(1)} %plus.4.a), channel_id=1, source_target_pairs={{0,64},{64,0},{128,192},{192,128},{256,320},{320,256},{384,448},{4... | collective-permute-start | bytes 1544 | tf_op jit(solution)/shard_map/ppermute | solution.py:241
  67.9 2.9 %collective-permute-done.7.b = f32[1,128]{1,0:T(1,128)S(1)} collective-permute-done((f32[1,128]{1,0:T(1,128)S(1)}, f32[1,128]{1,0:T(1,128)S(1)}, u32[]{:S(2)}, u32[]{:S(2)}) %collective-permute-start.7) | collective-permute-done | bytes 544 | tf_op jit(solution)/shard_map/ppermute | solution.py:241
  70.8 0.0 collective-permute-done.6.down_in
  70.8 3.0 %collective-permute-done.8.up_in = bf16[8,64,256]{2,1,0:T(8,128)(2,1)S(1)} collective-permute-done((bf16[8,64,256]{2,1,0:T(8,128)(2,1)S(1)}, bf16[8,64,256]{2,1,0:T(8,128)(2,1)S(1)}, u32[]{:S(2)}, u32[]{:S(2)}) %collective-permute-start.8) | collective-permute-done | bytes 262176 | tf_op jit(solution)/shard_map/ppermute | solution.py:241
  73.8 0.9 terms.1
  74.7 3.5 %all-to-all-start.1 = ((bf16[8,2,64,256]{3,2,1,0:T(8,128)(2,1)}), bf16[8,2,64,256]{3,2,1,0:T(8,128)(2,1)S(1)}, u32[]{:S(2)}, u32[]{:S(2)}) async-start(bf16[8,2,64,256]{3,2,1,0:T(8,128)(2,1)} %terms.1), calls=%async_computation.1 | async-start | bytes 1048576 | tf_op jit(solution)/shard_map/all_to_all | solution.py:307
  78.2 4.0 %collective-permute-start.9 = (f32[1,128]{1,0:T(1,128)S(1)}, f32[1,128]{1,0:T(1,128)S(1)}, u32[]{:S(2)}, u32[]{:S(2)}) collective-permute-start(f32[1,128]{1,0:T(1,128)S(1)} %plus.5.a), channel_id=1, source_target_pairs={{0,128},{64,192},{128,0},{192,64},{256,384},{320,448},{384,256},{4... | collective-permute-start | bytes 1544 | tf_op jit(solution)/shard_map/ppermute | solution.py:241
  82.2 2.3 %collective-permute-done.9.b = f32[1,128]{1,0:T(1,128)S(1)} collective-permute-done((f32[1,128]{1,0:T(1,128)S(1)}, f32[1,128]{1,0:T(1,128)S(1)}, u32[]{:S(2)}, u32[]{:S(2)}) %collective-permute-start.9) | collective-permute-done | bytes 544 | tf_op jit(solution)/shard_map/ppermute | solution.py:241
  84.5 3.8 %collective-permute-start.10 = (f32[1,128]{1,0:T(1,128)S(1)}, f32[1,128]{1,0:T(1,128)S(1)}, u32[]{:S(2)}, u32[]{:S(2)}) collective-permute-start(f32[1,128]{1,0:T(1,128)S(1)} %plus.6.a), channel_id=1, source_target_pairs={{0,256},{64,320},{128,384},{192,448},{256,0},{320,64},{384,128},{4... | collective-permute-start | bytes 1544 | tf_op jit(solution)/shard_map/ppermute | solution.py:241
  88.3 5.5 %collective-permute-done.10.b = f32[1,128]{1,0:T(1,128)S(1)} collective-permute-done((f32[1,128]{1,0:T(1,128)S(1)}, f32[1,128]{1,0:T(1,128)S(1)}, u32[]{:S(2)}, u32[]{:S(2)}) %collective-permute-start.10) | collective-permute-done | bytes 544 | tf_op jit(solution)/shard_map/ppermute | solution.py:241
  93.9 0.8 all-to-all-done.1.received
  94.7 0.8 total.1
  95.4 9.1 %all-to-all-start.2 = ((f32[32,1,128]{2,1,0:T(1,128)}), f32[32,1,128]{2,1,0:T(1,128)S(1)}, u32[]{:S(2)}, u32[]{:S(2)}) async-start(f32[32,1,128]{2,1,0:T(1,128)} %get-tuple-element.52), calls=%async_computation.2 | async-start | bytes 32768 | tf_op jit(solution)/shard_map/all_to_all | solution.py:317
  104.5 0.0 copy-start.9
  104.5 0.0 copy-done.6
  104.5 0.7 copy-done.9
  105.2 9.0 %all-to-all-done.2.sums = f32[32,1,128]{2,1,0:T(1,128)S(1)} async-done(((f32[32,1,128]{2,1,0:T(1,128)}), f32[32,1,128]{2,1,0:T(1,128)S(1)}, u32[]{:S(2)}, u32[]{:S(2)}) %all-to-all-start.2) | async-done | bytes 16416 | tf_op jit(solution)/shard_map/all_to_all | solution.py:317
  114.2 0.0 copy-done.1
  114.2 0.0 copy-done.4
  114.2 0.0 copy-done.5
  114.2 3.0 %update.1 = (f32[2,64,256]{2,1,0:T(8,128)}, f32[2,64,256]{2,1,0:T(8,128)}, f32[2,64,256]{2,1,0:T(8,128)}, f32[1,1]{1,0:T(1,128)}, f32[1,192]{1,0:T(1,128)}) custom-call(f32[192]{0:T(256)S(1)} %bitcast.16, f32[32,1,128]{2,1,0:T(1,128)S(1)} %all-to-all-done.2.sums, f32[2,64,256]{2,1,0:T(8,128)S(1)} %get-tuple-element.53.gradient, f32[2,64,256]{2,1,0:T(8,128)S(1)} %bitcast.12, ...), custom_call_target="tpu_custom_call" | custom-call | flops 13107200 | bytes 553728 | tf_op jit(solution)/shard_map/update/pallas_call | solution.py:28
  (15 shorter events, 0.1 us)
Async XLA Ops:
  0.6 0.9 copy-start
  1.5 11.3 %copy-start.7 = (f32[2048]{0:T(1024)S(1)}, f32[2048]{0:T(1024)}, u32[]{:S(2)}) copy-start(f32[2048]{0:T(1024)} %param.11) | copy-start | bytes 24580
  2.4 10.5 %copy-start.2 = (bf16[128,2048]{1,0:T(8,128)(2,1)S(1)}, bf16[128,2048]{1,0:T(8,128)(2,1)}, u32[]{:S(2)}) copy-start(bf16[128,2048]{1,0:T(8,128)(2,1)} %tokens.1) | copy-start | bytes 1572868
  2.4 10.5 %copy-start.3 = (bf16[128,2048]{1,0:T(8,128)(2,1)S(1)}, bf16[128,2048]{1,0:T(8,128)(2,1)}, u32[]{:S(2)}) copy-start(bf16[128,2048]{1,0:T(8,128)(2,1)} %targets.1) | copy-start | bytes 1572868
  2.4 27.9 %all-to-all-start = ((bf16[8,2,64,256]{3,2,1,0:T(8,128)(2,1)}), bf16[8,2,64,256]{3,2,1,0:T(8,128)(2,1)S(1)}, u32[]{:S(2)}, u32[]{:S(2)}) async-start(bf16[8,2,64,256]{3,2,1,0:T(8,128)(2,1)} %copies.1), calls=%async_computation | async-start | bytes 1048576 | tf_op jit(solution)/shard_map/all_to_all | solution.py:268
  13.5 24.0 %collective-permute-start = (bf16[256,1024]{1,0:T(8,128)(2,1)S(1)}, bf16[256,1024]{1,0:T(8,128)(2,1)S(1)}, u32[]{:S(2)}, u32[]{:S(2)}) collective-permute-start(bf16[256,1024]{1,0:T(8,128)(2,1)S(1)} %get-tuple-element.33), channel_id=1, source_target_pairs={{0,1},{1,0},{2,3},{3,2},{4,5},{5,4},{6,7},{7,6},{8,9},{9,8},{10,11... | collective-permute-start | bytes 1572872 | tf_op jit(solution)/shard_map/ppermute | solution.py:241
  30.4 12.3 %collective-permute-start.1 = (bf16[8,64,256]{2,1,0:T(8,128)(2,1)S(1)}, bf16[8,64,256]{2,1,0:T(8,128)(2,1)S(1)}, u32[]{:S(2)}, u32[]{:S(2)}) collective-permute-start(bf16[8,64,256]{2,1,0:T(8,128)(2,1)S(1)} %get-tuple-element.34.mine), channel_id=1, source_target_pairs={{0,3},{1,2},{2,1},{3,0},{4,7},{5,6},{6,5},{7,4},{8,11},{9,10},{10,... | collective-permute-start | bytes 786440 | tf_op jit(solution)/shard_map/ppermute | solution.py:241
  35.0 12.3 %collective-permute-start.3 = (bf16[8,64,256]{2,1,0:T(8,128)(2,1)S(1)}, bf16[8,64,256]{2,1,0:T(8,128)(2,1)S(1)}, u32[]{:S(2)}, u32[]{:S(2)}) collective-permute-start(bf16[8,64,256]{2,1,0:T(8,128)(2,1)S(1)} %get-tuple-element.37.mine), channel_id=1, source_target_pairs={{0,3},{1,2},{2,1},{3,0},{4,7},{5,6},{6,5},{7,4},{8,11},{9,10},{10,... | collective-permute-start | bytes 786440 | tf_op jit(solution)/shard_map/ppermute | solution.py:241
  43.0 6.9 %collective-permute-start.2 = (bf16[256,256]{1,0:T(8,128)(2,1)S(1)}, bf16[256,256]{1,0:T(8,128)(2,1)S(1)}, u32[]{:S(2)}, u32[]{:S(2)}) collective-permute-start(bf16[256,256]{1,0:T(8,128)(2,1)S(1)} %get-tuple-element.36), channel_id=1, source_target_pairs={{0,1},{1,0},{2,3},{3,2},{4,5},{5,4},{6,7},{7,6},{8,9},{9,8},{10,11... | collective-permute-start | bytes 393224 | tf_op jit(solution)/shard_map/ppermute | solution.py:241
  50.7 6.9 %collective-permute-start.4 = (bf16[256,256]{1,0:T(8,128)(2,1)S(1)}, bf16[256,256]{1,0:T(8,128)(2,1)S(1)}, u32[]{:S(2)}, u32[]{:S(2)}) collective-permute-start(bf16[256,256]{1,0:T(8,128)(2,1)S(1)} %get-tuple-element.39), channel_id=1, source_target_pairs={{0,1},{1,0},{2,3},{3,2},{4,5},{5,4},{6,7},{7,6},{8,9},{9,8},{10,11... | collective-permute-start | bytes 393224 | tf_op jit(solution)/shard_map/ppermute | solution.py:241
  52.9 3.1 %collective-permute-start.5 = (f32[1,128]{1,0:T(1,128)S(1)}, f32[1,128]{1,0:T(1,128)S(1)}, u32[]{:S(2)}, u32[]{:S(2)}) collective-permute-start(f32[1,128]{1,0:T(1,128)S(1)} %get-tuple-element.43.a), channel_id=1, source_target_pairs={{0,32},{32,0},{1,33},{33,1},{2,34},{34,2},{3,35},{35,3},{4,36},{36... | collective-permute-start | bytes 1544 | tf_op jit(solution)/shard_map/ppermute | solution.py:241
  58.3 12.5 %collective-permute-start.6 = (bf16[8,64,256]{2,1,0:T(8,128)(2,1)S(1)}, bf16[8,64,256]{2,1,0:T(8,128)(2,1)S(1)}, u32[]{:S(2)}, u32[]{:S(2)}) collective-permute-start(bf16[8,64,256]{2,1,0:T(8,128)(2,1)S(1)} %get-tuple-element.47), channel_id=1, source_target_pairs={{0,3},{1,2},{2,1},{3,0},{4,7},{5,6},{6,5},{7,4},{8,11},{9,10},{10,... | collective-permute-start | bytes 786440 | tf_op jit(solution)/shard_map/ppermute | solution.py:241
  63.0 10.8 %collective-permute-start.8 = (bf16[8,64,256]{2,1,0:T(8,128)(2,1)S(1)}, bf16[8,64,256]{2,1,0:T(8,128)(2,1)S(1)}, u32[]{:S(2)}, u32[]{:S(2)}) collective-permute-start(bf16[8,64,256]{2,1,0:T(8,128)(2,1)S(1)} %get-tuple-element.42), channel_id=1, source_target_pairs={{0,3},{1,2},{2,1},{3,0},{4,7},{5,6},{6,5},{7,4},{8,11},{9,10},{10,... | collective-permute-start | bytes 786440 | tf_op jit(solution)/shard_map/ppermute | solution.py:241
  65.3 5.5 %collective-permute-start.7 = (f32[1,128]{1,0:T(1,128)S(1)}, f32[1,128]{1,0:T(1,128)S(1)}, u32[]{:S(2)}, u32[]{:S(2)}) collective-permute-start(f32[1,128]{1,0:T(1,128)S(1)} %plus.4.a), channel_id=1, source_target_pairs={{0,64},{64,0},{128,192},{192,128},{256,320},{320,256},{384,448},{4... | collective-permute-start | bytes 1544 | tf_op jit(solution)/shard_map/ppermute | solution.py:241
  74.7 20.0 %all-to-all-start.1 = ((bf16[8,2,64,256]{3,2,1,0:T(8,128)(2,1)}), bf16[8,2,64,256]{3,2,1,0:T(8,128)(2,1)S(1)}, u32[]{:S(2)}, u32[]{:S(2)}) async-start(bf16[8,2,64,256]{3,2,1,0:T(8,128)(2,1)} %terms.1), calls=%async_computation.1 | async-start | bytes 1048576 | tf_op jit(solution)/shard_map/all_to_all | solution.py:307
  78.2 6.4 %collective-permute-start.9 = (f32[1,128]{1,0:T(1,128)S(1)}, f32[1,128]{1,0:T(1,128)S(1)}, u32[]{:S(2)}, u32[]{:S(2)}) collective-permute-start(f32[1,128]{1,0:T(1,128)S(1)} %plus.5.a), channel_id=1, source_target_pairs={{0,128},{64,192},{128,0},{192,64},{256,384},{320,448},{384,256},{4... | collective-permute-start | bytes 1544 | tf_op jit(solution)/shard_map/ppermute | solution.py:241
  84.5 9.4 %collective-permute-start.10 = (f32[1,128]{1,0:T(1,128)S(1)}, f32[1,128]{1,0:T(1,128)S(1)}, u32[]{:S(2)}, u32[]{:S(2)}) collective-permute-start(f32[1,128]{1,0:T(1,128)S(1)} %plus.6.a), channel_id=1, source_target_pairs={{0,256},{64,320},{128,384},{192,448},{256,0},{320,64},{384,128},{4... | collective-permute-start | bytes 1544 | tf_op jit(solution)/shard_map/ppermute | solution.py:241
  94.7 19.6 %copy-start.1 = (f32[1,2,64,256]{3,2,1,0:T(8,128)S(1)}, f32[1,2,64,256]{3,2,1,0:T(8,128)}, u32[]{:S(2)}) copy-start(f32[1,2,64,256]{3,2,1,0:T(8,128)} %param.12) | copy-start | bytes 393220
  94.7 19.6 %copy-start.4 = (f32[1,2,64,256]{3,2,1,0:T(8,128)S(1)}, f32[1,2,64,256]{3,2,1,0:T(8,128)}, u32[]{:S(2)}) copy-start(f32[1,2,64,256]{3,2,1,0:T(8,128)} %param.13) | copy-start | bytes 393220
  94.7 19.6 %copy-start.5 = (f32[1,2,64,256]{3,2,1,0:T(8,128)S(1)}, f32[1,2,64,256]{3,2,1,0:T(8,128)}, u32[]{:S(2)}) copy-start(f32[1,2,64,256]{3,2,1,0:T(8,128)} %param.14) | copy-start | bytes 393220
  95.4 9.1 %copy-start.6 = (f32[8,192]{1,0:T(8,128)S(1)}, f32[8,192]{1,0:T(8,128)}, u32[]{:S(2)}) copy-start(f32[8,192]{1,0:T(8,128)} %perturbation.3) | copy-start | bytes 18436
  95.4 18.8 %all-to-all-start.2 = ((f32[32,1,128]{2,1,0:T(1,128)}), f32[32,1,128]{2,1,0:T(1,128)S(1)}, u32[]{:S(2)}, u32[]{:S(2)}) async-start(f32[32,1,128]{2,1,0:T(1,128)} %get-tuple-element.52), calls=%async_computation.2 | async-start | bytes 32768 | tf_op jit(solution)/shard_map/all_to_all | solution.py:317
  104.5 0.7 copy-start.9
  105.2 9.0 %copy-start.8 = (f32[8,192]{1,0:T(8,128)S(1)}, f32[8,192]{1,0:T(8,128)}, u32[]{:S(2)}) copy-start(f32[8,192]{1,0:T(8,128)} %accumulated.1) | copy-start | bytes 18436

commit v5 on v4

--- a/solution.py
+++ b/solution.py
@@ -4,6 +4,7 @@
 from jax.experimental import pallas as pl
 from jax.experimental.pallas import tpu as pltpu
 from jax.sharding import Mesh, PartitionSpec as P
+
 
 D = 2048
 RANK = 256
@@ -22,7 +23,7 @@
 SMEM = pl.BlockSpec(memory_space=pltpu.SMEM)
 
 
-def call(kernel, outs, args, flops, name, scratch=()):
+def call(kernel, outs, args, flops, scratch=()):
     scalars = [a.ndim == 1 for a in args]
     moved = sum(a.size * a.dtype.itemsize for a in args)
     return pl.pallas_call(
@@ -33,7 +34,6 @@
         scratch_shapes=[pltpu.VMEM(s, d) for s, d in scratch],
         compiler_params=pltpu.CompilerParams(vmem_limit_bytes=16 * 2**20),
         cost_estimate=pl.CostEstimate(flops=flops, bytes_accessed=moved, transcendentals=0),
-        name=name,
     )(*args)
 
 
@@ -117,10 +117,11 @@
         part = jnp.dot(upstream, up_w, preferred_element_type=f32) * up_scale
         back[at, :] = part
         send[(1 - i) * block : (2 - i) * block, :] = part.astype(bf16)
-    lane = lax.broadcasted_iota(jnp.int32, loss.shape, 1)
+    lane = lax.broadcasted_iota(jnp.int32, (1, 128), 1)
     tokens = own.shape[0] * (lax.axis_size("x") // 2) * lax.axis_size("z")
     mean = jnp.sum(losses, axis=1, keepdims=True) / (tokens * D)
-    loss[...] = jnp.where(lane == 2 + particle_index(), mean, 0.0)
+    line = jnp.where(lane == 2 + particle_index(), mean, 0.0)
+    loss[...] = jnp.broadcast_to(line[None], loss.shape)
 
 
 def parted(product, mine, theirs, full):
@@ -156,8 +157,8 @@
 
 
 def total_kernel(received, losses, gradient, line):
-    lane = lax.broadcasted_iota(jnp.int32, losses.shape, 1)
-    full = losses[...]
+    full = jnp.sum(losses[...], axis=0)
+    lane = lax.broadcasted_iota(jnp.int32, full.shape, 1)
     for half in range(gradient.shape[0]):
         total = received[0, half].astype(f32)
         for i in range(1, received.shape[0]):
@@ -166,10 +167,6 @@
         square = jnp.sum(jnp.sum(total * total, axis=0, keepdims=True), axis=1, keepdims=True)
         full = full + jnp.where(lane == half, square, 0.0)
     line[...] = jnp.broadcast_to(full[None], line.shape)
-
-
-def add_kernel(a, b, out):
-    out[...] = a[...] + b[...]
 
 
 def learned_kernel(base, perturbation, out):
@@ -238,11 +235,12 @@
 
 
 def swap(array, axis, mask):
-    return lax.ppermute(array, axis, [(i, i ^ mask) for i in range(lax.axis_size(axis))])
-
-
-def plus(a, b):
-    return call(add_kernel, [(a.shape, a.dtype)], (a, b), a.size, "plus")[0]
+    pairs = [(i, i ^ mask) for i in range(lax.axis_size(axis))]
+    return lax.ppermute(array, axis, pairs)
+
+
+def exchange(array, axis):
+    return lax.all_to_all(array, axis, 0, 0, tiled=True)
 
 
 def local(
@@ -257,6 +255,7 @@
     accumulated,
 ):
     nz, nx = lax.axis_size("z"), lax.axis_size("x")
+    particles = lax.axis_size("y") * lax.axis_size("core")
     rows = weights.shape[2]
     block = tokens.shape[0]
     width = 2 * nz * rows
@@ -264,63 +263,47 @@
     shape = (weights.shape[1], rows, RANK)
     column = (nz, rows, RANK)
     full = (nz, 2 * rows, RANK)
-    (copies,) = call(copies_kernel, [((nz, *shape), bf16)], (weights[0],), weights.size, "copies")
-    gathered = lax.all_to_all(copies, "z", 0, 0, tiled=True)
+    (copies,) = call(copies_kernel, [((nz, *shape), bf16)], (weights[0],), weights.size)
+    gathered = exchange(copies, "z")
     piece, send = call(
         cut_kernel,
         [((2 * block, width), bf16)] * 2,
         (tokens, targets, norm_gain[None]),
         20 * block * D,
-        "cut",
     )
     pieces = (piece, swap(send, "x", 1))
-    down_w, up_w = call(split_kernel, [(column, bf16)] * 2, (gathered,), gathered.size, "split")
+    down_w, up_w = call(split_kernel, [(column, bf16)] * 2, (gathered,), gathered.size)
     down_w, up_w = (down_w, swap(down_w, "x", 3)), (up_w, swap(up_w, "x", 3))
 
     wide, thin = ((tall, RANK), f32), ((tall, RANK), bf16)
     product = 2 * tall * width * RANK
     joint, sums_of = [(full, bf16)], [(full, f32)]
-    pre, send = call(first_kernel, [wide, thin], (*pieces, *down_w), product, "first", joint)
+    pre, send = call(first_kernel, [wide, thin], (*pieces, *down_w), product, joint)
     slope, active, upstream, loss, back, send = call(
         middle_kernel,
-        [wide, thin, ((tall, width), bf16), ((1, 128), f32), wide, thin],
+        [wide, thin, ((tall, width), bf16), ((particles, 1, 128), f32), wide, thin],
         (pre, swap(send, "x", 1), *pieces, *up_w),
         2 * product,
-        "middle",
         joint,
     )
     received = swap(send, "x", 1)
     parts = [(column, f32), (column, bf16)]
-    up, send_up = call(up_kernel, parts, (upstream, active), product, "up", sums_of)
+    up, send_up = call(up_kernel, parts, (upstream, active), product, sums_of)
     up_in = swap(send_up, "x", 3)
-    loss = plus(loss, swap(loss, "core", 1))
-    received, _, loss = lax.optimization_barrier((received, send_up, loss))
-    down, send_down = call(
-        down_kernel, parts, (back, received, slope, *pieces), product, "down", sums_of
-    )
+    down, send_down = call(down_kernel, parts, (back, received, slope, *pieces), product, sums_of)
     down_in = swap(send_down, "x", 3)
-    loss = plus(loss, swap(loss, "y", 1))
-    down_in, loss = lax.optimization_barrier((down_in, loss))
-    (terms,) = call(
-        terms_kernel, [((nz, *shape), bf16)], (down, down_in, up, up_in), 4 * down.size, "terms"
-    )
-    terms = lax.all_to_all(terms, "z", 0, 0, tiled=True)
-    loss = plus(loss, swap(loss, "y", 2))
-    loss = plus(loss, swap(loss, "y", 4))
+    loss = exchange(loss, ("y", "core"))
+    (terms,) = call(terms_kernel, [((nz, *shape), bf16)], (down, down_in, up, up_in), 4 * down.size)
+    terms = exchange(terms, "z")
     gradient, line = call(
-        total_kernel,
-        [(shape, f32), ((nz * nx, 1, 128), f32)],
-        (terms, loss),
-        10 * terms.size,
-        "total",
-    )
-    sums = lax.all_to_all(line, ("z", "x"), 0, 0, tiled=True)
+        total_kernel, [(shape, f32), ((nz * nx, 1, 128), f32)], (terms, loss), 10 * terms.size
+    )
+    sums = exchange(line, ("z", "x"))
     (learned,) = call(
         learned_kernel,
         [((1, learned_params.shape[0]), f32)],
         (learned_params[None], perturbation),
         10 * perturbation.size,
-        "learned",
     )
     learned = learned.reshape(-1)
     new_w, new_m, new_v, own_loss, outer = call(
@@ -337,7 +320,6 @@
             perturbation,
         ),
         400 * weights.size,
-        "update",
     )
     return (new_w[None], new_m[None], new_v[None], own_loss.reshape(1), outer.reshape(-1))
 

time: 118 us -> 116 us (0.983)
  the two profiles are of different devices: /device:TPU:48 before, /device:TPU:1 now
where the time goes in v5:
time: 116 us; the launch traced here: 115 us
  starting transfers between devices  47.7 us (41%)
  waiting for transfers between devices  36.9 us (32%)
  blocking collectives  19.1 us (16%)
  Pallas kernels  8.36 us (7%)
  local copies, waits for them, and re-layouts  1.59 us (1%)
    all_to_all x3, waiting for transfers between devices, exchange(): return lax.all_to_all(array, axis, 0, 0, tiled=True)  28.9 us
    all_to_all x3, starting transfers between devices, exchange(): return lax.all_to_all(array, axis, 0, 0, tiled=True)  26.6 us
    ppermute x7, starting transfers between devices, swap(): return lax.ppermute(array, axis, pairs)  21.1 us
    all_to_all x1, blocking collectives, exchange(): return lax.all_to_all(array, axis, 0, 0, tiled=True)  19.1 us
    pallas_call x11, Pallas kernels, call(): pl.pallas_call(kernel, out_shape=[jax.ShapeDtypeStruct(s, d) for s, d in...  8.36 us
    ppermute x7, waiting for transfers between devices, swap(): return lax.ppermute(array, axis, pairs)  8.04 us
  transfers between devices with their start and end apart: 10, of which 6 were waited for; matrix products, arithmetic and copies ran while one was open for 0% of the time, Pallas kernels for 2%

profile of v5, /device:TPU:1, one launch (start us, length us, event | category | flops | bytes accessed | tf_op | source)
XLA Modules:
  0.0 114.6 jit_solution(4375134929177948000)
XLA Ops:
  0.6 0.0 copy-start
  0.6 0.9 copy-done
  1.5 0.0 copy-start.7
  1.5 0.9 shard_map.130
  2.4 0.0 copy-start.2
  2.4 0.0 copy-start.3
  2.4 11.0 %all-to-all-start = ((bf16[8,2,64,256]{3,2,1,0:T(8,128)(2,1)}), bf16[8,2,64,256]{3,2,1,0:T(8,128)(2,1)S(1)}, u32[]{:S(2)}, u32[]{:S(2)}) async-start(bf16[8,2,64,256]{3,2,1,0:T(8,128)(2,1)} %shard_map.130), calls=%async_computation | async-start | bytes 1048576 | tf_op jit(solution)/shard_map/all_to_all | solution.py:243
  13.4 0.0 copy-done.7
  13.4 0.0 copy-done.2
  13.4 0.0 copy-done.3
  13.4 0.6 shard_map.129
  14.0 3.1 %collective-permute-start = (bf16[256,1024]{1,0:T(8,128)(2,1)S(1)}, bf16[256,1024]{1,0:T(8,128)(2,1)S(1)}, u32[]{:S(2)}, u32[]{:S(2)}) collective-permute-start(bf16[256,1024]{1,0:T(8,128)(2,1)S(1)} %get-tuple-element.29), channel_id=1, source_target_pairs={{0,1},{1,0},{2,3},{3,2},{4,5},{5,4},{6,7},{7,6},{8,9},{9,8},{10,11... | collective-permute-start | bytes 1572872 | tf_op jit(solution)/shard_map/ppermute | solution.py:239
  17.2 14.2 %all-to-all-done.gathered = bf16[8,2,64,256]{3,2,1,0:T(8,128)(2,1)S(1)} async-done(((bf16[8,2,64,256]{3,2,1,0:T(8,128)(2,1)}), bf16[8,2,64,256]{3,2,1,0:T(8,128)(2,1)S(1)}, u32[]{:S(2)}, u32[]{:S(2)}) %all-to-all-start) | async-done | bytes 524320 | tf_op jit(solution)/shard_map/all_to_all | solution.py:243
  31.4 4.4 %collective-permute-start.1 = (bf16[8,64,256]{2,1,0:T(8,128)(2,1)S(1)}, bf16[8,64,256]{2,1,0:T(8,128)(2,1)S(1)}, u32[]{:S(2)}, u32[]{:S(2)}) collective-permute-start(bf16[8,64,256]{2,1,0:T(8,128)(2,1)S(1)} %get-tuple-element.30.mine), channel_id=1, source_target_pairs={{0,3},{1,2},{2,1},{3,0},{4,7},{5,6},{6,5},{7,4},{8,11},{9,10},{10,... | collective-permute-start | bytes 786440 | tf_op jit(solution)/shard_map/ppermute | solution.py:239
  35.8 2.1 %collective-permute-start.3 = (bf16[8,64,256]{2,1,0:T(8,128)(2,1)S(1)}, bf16[8,64,256]{2,1,0:T(8,128)(2,1)S(1)}, u32[]{:S(2)}, u32[]{:S(2)}) collective-permute-start(bf16[8,64,256]{2,1,0:T(8,128)(2,1)S(1)} %get-tuple-element.33.mine), channel_id=1, source_target_pairs={{0,3},{1,2},{2,1},{3,0},{4,7},{5,6},{6,5},{7,4},{8,11},{9,10},{10,... | collective-permute-start | bytes 786440 | tf_op jit(solution)/shard_map/ppermute | solution.py:239
  37.9 0.0 collective-permute-done.n1.d1
  37.9 4.0 %collective-permute-done.1.theirs = bf16[8,64,256]{2,1,0:T(8,128)(2,1)S(1)} collective-permute-done((bf16[8,64,256]{2,1,0:T(8,128)(2,1)S(1)}, bf16[8,64,256]{2,1,0:T(8,128)(2,1)S(1)}, u32[]{:S(2)}, u32[]{:S(2)}) %collective-permute-start.1) | collective-permute-done | bytes 262176 | tf_op jit(solution)/shard_map/ppermute | solution.py:239
  41.9 0.4 shard_map.132
  42.2 1.9 %collective-permute-start.2 = (bf16[256,256]{1,0:T(8,128)(2,1)S(1)}, bf16[256,256]{1,0:T(8,128)(2,1)S(1)}, u32[]{:S(2)}, u32[]{:S(2)}) collective-permute-start(bf16[256,256]{1,0:T(8,128)(2,1)S(1)} %get-tuple-element.32), channel_id=1, source_target_pairs={{0,1},{1,0},{2,3},{3,2},{4,5},{5,4},{6,7},{7,6},{8,9},{9,8},{10,11... | collective-permute-start | bytes 393224 | tf_op jit(solution)/shard_map/ppermute | solution.py:239
  44.2 3.3 %collective-permute-done.3.theirs = bf16[8,64,256]{2,1,0:T(8,128)(2,1)S(1)} collective-permute-done((bf16[8,64,256]{2,1,0:T(8,128)(2,1)S(1)}, bf16[8,64,256]{2,1,0:T(8,128)(2,1)S(1)}, u32[]{:S(2)}, u32[]{:S(2)}) %collective-permute-start.3) | collective-permute-done | bytes 262176 | tf_op jit(solution)/shard_map/ppermute | solution.py:239
  47.5 0.8 collective-permute-done.2.received
  48.3 1.3 %shard_map.133 = (f32[256,256]{1,0:T(8,128)S(1)}, bf16[256,256]{1,0:T(8,128)(2,1)S(1)}, bf16[256,1024]{1,0:T(8,128)(2,1)S(1)}, f32[16,1,128]{2,1,0:T(1,128)}, f3...) custom-call(f32[256,256]{1,0:T(8,128)S(1)} %get-tuple-element.31.own, ...), custom_call_target="tpu_custom_call" | custom-call | flops 268435456 | bytes 1966080 | tf_op jit(solution)/shard_map/pallas_call | solution.py:29
  49.6 1.9 %collective-permute-start.4 = (bf16[256,256]{1,0:T(8,128)(2,1)S(1)}, bf16[256,256]{1,0:T(8,128)(2,1)S(1)}, u32[]{:S(2)}, u32[]{:S(2)}) collective-permute-start(bf16[256,256]{1,0:T(8,128)(2,1)S(1)} %get-tuple-element.35), channel_id=1, source_target_pairs={{0,1},{1,0},{2,3},{3,2},{4,5},{5,4},{6,7},{7,6},{8,9},{9,8},{10,11... | collective-permute-start | bytes 393224 | tf_op jit(solution)/shard_map/ppermute | solution.py:239
  51.5 0.5 shard_map.135
  52.0 4.4 %collective-permute-start.6 = (bf16[8,64,256]{2,1,0:T(8,128)(2,1)S(1)}, bf16[8,64,256]{2,1,0:T(8,128)(2,1)S(1)}, u32[]{:S(2)}, u32[]{:S(2)}) collective-permute-start(bf16[8,64,256]{2,1,0:T(8,128)(2,1)S(1)} %get-tuple-element.42), channel_id=1, source_target_pairs={{0,3},{1,2},{2,1},{3,0},{4,7},{5,6},{6,5},{7,4},{8,11},{9,10},{10,... | collective-permute-start | bytes 786440 | tf_op jit(solution)/shard_map/ppermute | solution.py:239
  56.4 0.0 collective-permute-done.4.received
  56.4 0.8 shard_map.134
  57.2 3.3 %collective-permute-start.5 = (bf16[8,64,256]{2,1,0:T(8,128)(2,1)S(1)}, bf16[8,64,256]{2,1,0:T(8,128)(2,1)S(1)}, u32[]{:S(2)}, u32[]{:S(2)}) collective-permute-start(bf16[8,64,256]{2,1,0:T(8,128)(2,1)S(1)} %get-tuple-element.38), channel_id=1, source_target_pairs={{0,3},{1,2},{2,1},{3,0},{4,7},{5,6},{6,5},{7,4},{8,11},{9,10},{10,... | collective-permute-start | bytes 786440 | tf_op jit(solution)/shard_map/ppermute | solution.py:239
  60.5 11.7 %all-to-all-start.2 = ((f32[16,1,128]{2,1,0:T(1,128)}), f32[16,1,128]{2,1,0:T(1,128)S(1)}, u32[]{:S(2)}, u32[]{:S(2)}) async-start(f32[16,1,128]{2,1,0:T(1,128)} %get-tuple-element.43), calls=%async_computation.2 | async-start | bytes 16384 | tf_op jit(solution)/shard_map/all_to_all | solution.py:243
  72.2 0.0 collective-permute-done.6.up_in
  72.2 0.0 collective-permute-done.5.down_in
  72.2 0.1 shard_map.136
  72.3 6.9 %all-to-all-done.2.losses = f32[16,1,128]{2,1,0:T(1,128)S(1)} async-done(((f32[16,1,128]{2,1,0:T(1,128)}), f32[16,1,128]{2,1,0:T(1,128)S(1)}, u32[]{:S(2)}, u32[]{:S(2)}) %all-to-all-start.2) | async-done | bytes 8224 | tf_op jit(solution)/shard_map/all_to_all | solution.py:243
  79.1 19.1 %all_to_all.20.received = bf16[8,2,64,256]{3,2,1,0:T(8,128)(2,1)S(1)} all-to-all(bf16[8,2,64,256]{3,2,1,0:T(8,128)(2,1)S(1)} %shard_map.136), channel_id=1, replica_groups=mesh['y'=8,'core'=2,'z'=8,'x'=4] {'z'}, dimensions={0} | all-to-all | bytes 1048576 | tf_op jit(solution)/shard_map/all_to_all | solution.py:243
  98.2 0.0 copy-start.1
  98.2 0.0 copy-start.4
  98.2 0.0 copy-start.5
  98.3 0.8 shard_map.137
  99.0 4.0 %all-to-all-start.3 = ((f32[32,1,128]{2,1,0:T(1,128)}), f32[32,1,128]{2,1,0:T(1,128)S(1)}, u32[]{:S(2)}, u32[]{:S(2)}) async-start(f32[32,1,128]{2,1,0:T(1,128)} %get-tuple-element.44), calls=%async_computation.3 | async-start | bytes 32768 | tf_op jit(solution)/shard_map/all_to_all | solution.py:243
  103.0 0.0 copy-start.9
  103.0 0.0 copy-done.6
  103.0 0.7 copy-done.9
  103.7 7.8 %all-to-all-done.3.sums = f32[32,1,128]{2,1,0:T(1,128)S(1)} async-done(((f32[32,1,128]{2,1,0:T(1,128)}), f32[32,1,128]{2,1,0:T(1,128)S(1)}, u32[]{:S(2)}, u32[]{:S(2)}) %all-to-all-start.3) | async-done | bytes 16416 | tf_op jit(solution)/shard_map/all_to_all | solution.py:243
  111.5 0.0 copy-done.1
  111.5 0.0 copy-done.4
  111.6 0.0 copy-done.5
  111.6 0.0 copy-done.8
  111.6 3.0 %shard_map.138 = (f32[2,64,256]{2,1,0:T(8,128)}, f32[2,64,256]{2,1,0:T(8,128)}, f32[2,64,256]{2,1,0:T(8,128)}, f32[1,1]{1,0:T(1,128)}, f32[1,192]{1,0:T(1,128)}) custom-call(f32[192]{0:T(256)S(1)} %bitcast.16, f32[32,1,128]{2,1,0:T(1,128)S(1)} %all-to-all-done.3.sums, f32[2,64,256]{2,1,0:T(8,128)S(1)} %get-tuple-element.45.gradient, ...), custom_call_target="tpu_custom_call" | custom-call | flops 13107200 | bytes 553728 | tf_op jit(solution)/shard_map/pallas_call | solution.py:29
  (4 shorter events, 0.1 us)
Async XLA Ops:
  0.6 0.9 copy-start
  1.5 11.9 %copy-start.7 = (f32[2048]{0:T(1024)S(1)}, f32[2048]{0:T(1024)}, u32[]{:S(2)}) copy-start(f32[2048]{0:T(1024)} %param.11) | copy-start | bytes 24580
  2.4 11.0 %copy-start.2 = (bf16[128,2048]{1,0:T(8,128)(2,1)S(1)}, bf16[128,2048]{1,0:T(8,128)(2,1)}, u32[]{:S(2)}) copy-start(bf16[128,2048]{1,0:T(8,128)(2,1)} %tokens.1) | copy-start | bytes 1572868
  2.4 11.0 %copy-start.3 = (bf16[128,2048]{1,0:T(8,128)(2,1)S(1)}, bf16[128,2048]{1,0:T(8,128)(2,1)}, u32[]{:S(2)}) copy-start(bf16[128,2048]{1,0:T(8,128)(2,1)} %targets.1) | copy-start | bytes 1572868
  2.4 28.9 %all-to-all-start = ((bf16[8,2,64,256]{3,2,1,0:T(8,128)(2,1)}), bf16[8,2,64,256]{3,2,1,0:T(8,128)(2,1)S(1)}, u32[]{:S(2)}, u32[]{:S(2)}) async-start(bf16[8,2,64,256]{3,2,1,0:T(8,128)(2,1)} %shard_map.130), calls=%async_computation | async-start | bytes 1048576 | tf_op jit(solution)/shard_map/all_to_all | solution.py:243
  14.0 23.9 %collective-permute-start = (bf16[256,1024]{1,0:T(8,128)(2,1)S(1)}, bf16[256,1024]{1,0:T(8,128)(2,1)S(1)}, u32[]{:S(2)}, u32[]{:S(2)}) collective-permute-start(bf16[256,1024]{1,0:T(8,128)(2,1)S(1)} %get-tuple-element.29), channel_id=1, source_target_pairs={{0,1},{1,0},{2,3},{3,2},{4,5},{5,4},{6,7},{7,6},{8,9},{9,8},{10,11... | collective-permute-start | bytes 1572872 | tf_op jit(solution)/shard_map/ppermute | solution.py:239
  31.4 10.5 %collective-permute-start.1 = (bf16[8,64,256]{2,1,0:T(8,128)(2,1)S(1)}, bf16[8,64,256]{2,1,0:T(8,128)(2,1)S(1)}, u32[]{:S(2)}, u32[]{:S(2)}) collective-permute-start(bf16[8,64,256]{2,1,0:T(8,128)(2,1)S(1)} %get-tuple-element.30.mine), channel_id=1, source_target_pairs={{0,3},{1,2},{2,1},{3,0},{4,7},{5,6},{6,5},{7,4},{8,11},{9,10},{10,... | collective-permute-start | bytes 786440 | tf_op jit(solution)/shard_map/ppermute | solution.py:239
  35.8 11.7 %collective-permute-start.3 = (bf16[8,64,256]{2,1,0:T(8,128)(2,1)S(1)}, bf16[8,64,256]{2,1,0:T(8,128)(2,1)S(1)}, u32[]{:S(2)}, u32[]{:S(2)}) collective-permute-start(bf16[8,64,256]{2,1,0:T(8,128)(2,1)S(1)} %get-tuple-element.33.mine), channel_id=1, source_target_pairs={{0,3},{1,2},{2,1},{3,0},{4,7},{5,6},{6,5},{7,4},{8,11},{9,10},{10,... | collective-permute-start | bytes 786440 | tf_op jit(solution)/shard_map/ppermute | solution.py:239
  42.2 6.0 %collective-permute-start.2 = (bf16[256,256]{1,0:T(8,128)(2,1)S(1)}, bf16[256,256]{1,0:T(8,128)(2,1)S(1)}, u32[]{:S(2)}, u32[]{:S(2)}) collective-permute-start(bf16[256,256]{1,0:T(8,128)(2,1)S(1)} %get-tuple-element.32), channel_id=1, source_target_pairs={{0,1},{1,0},{2,3},{3,2},{4,5},{5,4},{6,7},{7,6},{8,9},{9,8},{10,11... | collective-permute-start | bytes 393224 | tf_op jit(solution)/shard_map/ppermute | solution.py:239
  49.6 6.8 %collective-permute-start.4 = (bf16[256,256]{1,0:T(8,128)(2,1)S(1)}, bf16[256,256]{1,0:T(8,128)(2,1)S(1)}, u32[]{:S(2)}, u32[]{:S(2)}) collective-permute-start(bf16[256,256]{1,0:T(8,128)(2,1)S(1)} %get-tuple-element.35), channel_id=1, source_target_pairs={{0,1},{1,0},{2,3},{3,2},{4,5},{5,4},{6,7},{7,6},{8,9},{9,8},{10,11... | collective-permute-start | bytes 393224 | tf_op jit(solution)/shard_map/ppermute | solution.py:239
  52.0 20.1 %collective-permute-start.6 = (bf16[8,64,256]{2,1,0:T(8,128)(2,1)S(1)}, bf16[8,64,256]{2,1,0:T(8,128)(2,1)S(1)}, u32[]{:S(2)}, u32[]{:S(2)}) collective-permute-start(bf16[8,64,256]{2,1,0:T(8,128)(2,1)S(1)} %get-tuple-element.42), channel_id=1, source_target_pairs={{0,3},{1,2},{2,1},{3,0},{4,7},{5,6},{6,5},{7,4},{8,11},{9,10},{10,... | collective-permute-start | bytes 786440 | tf_op jit(solution)/shard_map/ppermute | solution.py:239
  57.2 15.0 %collective-permute-start.5 = (bf16[8,64,256]{2,1,0:T(8,128)(2,1)S(1)}, bf16[8,64,256]{2,1,0:T(8,128)(2,1)S(1)}, u32[]{:S(2)}, u32[]{:S(2)}) collective-permute-start(bf16[8,64,256]{2,1,0:T(8,128)(2,1)S(1)} %get-tuple-element.38), channel_id=1, source_target_pairs={{0,3},{1,2},{2,1},{3,0},{4,7},{5,6},{6,5},{7,4},{8,11},{9,10},{10,... | collective-permute-start | bytes 786440 | tf_op jit(solution)/shard_map/ppermute | solution.py:239
  60.5 18.7 %all-to-all-start.2 = ((f32[16,1,128]{2,1,0:T(1,128)}), f32[16,1,128]{2,1,0:T(1,128)S(1)}, u32[]{:S(2)}, u32[]{:S(2)}) async-start(f32[16,1,128]{2,1,0:T(1,128)} %get-tuple-element.43), calls=%async_computation.2 | async-start | bytes 16384 | tf_op jit(solution)/shard_map/all_to_all | solution.py:243
  98.2 13.3 %copy-start.1 = (f32[1,2,64,256]{3,2,1,0:T(8,128)S(1)}, f32[1,2,64,256]{3,2,1,0:T(8,128)}, u32[]{:S(2)}) copy-start(f32[1,2,64,256]{3,2,1,0:T(8,128)} %param.12) | copy-start | bytes 393220
  98.2 13.3 %copy-start.4 = (f32[1,2,64,256]{3,2,1,0:T(8,128)S(1)}, f32[1,2,64,256]{3,2,1,0:T(8,128)}, u32[]{:S(2)}) copy-start(f32[1,2,64,256]{3,2,1,0:T(8,128)} %param.13) | copy-start | bytes 393220
  98.2 13.3 %copy-start.5 = (f32[1,2,64,256]{3,2,1,0:T(8,128)S(1)}, f32[1,2,64,256]{3,2,1,0:T(8,128)}, u32[]{:S(2)}) copy-start(f32[1,2,64,256]{3,2,1,0:T(8,128)} %param.14) | copy-start | bytes 393220
  99.0 4.0 %copy-start.6 = (f32[8,192]{1,0:T(8,128)S(1)}, f32[8,192]{1,0:T(8,128)}, u32[]{:S(2)}) copy-start(f32[8,192]{1,0:T(8,128)} %perturbation.3) | copy-start | bytes 18436
  99.0 12.5 %all-to-all-start.3 = ((f32[32,1,128]{2,1,0:T(1,128)}), f32[32,1,128]{2,1,0:T(1,128)S(1)}, u32[]{:S(2)}, u32[]{:S(2)}) async-start(f32[32,1,128]{2,1,0:T(1,128)} %get-tuple-element.44), calls=%async_computation.3 | async-start | bytes 32768 | tf_op jit(solution)/shard_map/all_to_all | solution.py:243
  103.0 0.7 copy-start.9
  103.7 7.9 %copy-start.8 = (f32[8,192]{1,0:T(8,128)S(1)}, f32[8,192]{1,0:T(8,128)}, u32[]{:S(2)}) copy-start(f32[8,192]{1,0:T(8,128)} %accumulated.1) | copy-start | bytes 18436

commit v6 on v5

--- a/solution.py
+++ b/solution.py
@@ -43,28 +43,38 @@
 
 
 def cut_kernel(tokens, targets, gain, *outs):
-    block, tile = tokens.shape[0], 128
+    tile = 128
+    block, side = tokens.shape[0], tile // 2
     my_x = lax.axis_index("x")
     outer = my_x // 2 == lax.rem(my_x, 2)
-    lanes = lax.broadcasted_iota(jnp.int32, (block, tile), 1) < tile // 2
+    lanes = lax.broadcasted_iota(jnp.int32, (block, tile), 1) < side
     values = tokens[...].astype(f32)
     inverse = lax.rsqrt(jnp.mean(values * values, axis=-1, keepdims=True) + norm_eps)
+    norms = []
     for q in range(tokens.shape[1] // (2 * tile)):
-        norms, gaps = [], []
+        pair, gaps = [], []
         for j in range(2):
             at = slice((2 * q + j) * tile, (2 * q + j + 1) * tile)
             token = tokens[:, at].astype(f32)
-            norms.append((token * inverse * gain[:, at]).astype(bf16).astype(f32))
+            pair.append(token * inverse * gain[:, at])
             gaps.append(token - targets[:, at].astype(f32))
+        norms.append(pair)
         out = slice(q * tile, (q + 1) * tile)
-        for k, dest in enumerate(outs):
+        for k, dest in enumerate(outs[4:]):
             first = jnp.logical_xor(lanes, outer if k else jnp.logical_not(outer))
-            dest[0:block, out] = jnp.where(first, *norms).astype(bf16)
-            dest[block : 2 * block, out] = jnp.where(first, *gaps).astype(bf16)
-
-
-def split_kernel(gathered, down_w, up_w):
-    down_w[...] = gathered[:, 0]
+            dest[:, out] = jnp.where(first, *gaps).astype(bf16)
+    for k, dest in enumerate(outs[:4]):
+        x = jnp.bitwise_xor(my_x, k)
+        high, odd = x // 2 == 1, lax.rem(x, 2) == 1
+        keep = jnp.logical_xor(lanes, odd)
+        for q in range(len(norms) // 2):
+            a, b = (jnp.where(high, n[1], n[0]) for n in norms[2 * q : 2 * q + 2])
+            moved = pltpu.roll(jnp.where(odd, a, b), side, 1)
+            kept = jnp.where(odd, b, a)
+            dest[:, q * tile : (q + 1) * tile] = jnp.where(keep, kept, moved).astype(bf16)
+
+
+def split_kernel(gathered, up_w):
     up_w[...] = gathered[:, 1]
 
 
@@ -85,24 +95,26 @@
     return full[...].reshape(-1, full.shape[-1])
 
 
-def first_kernel(n0, n1, mine, theirs, own, send, full):
-    down_w = joined(mine, theirs, full)
-    block = n0.shape[0] // 2
-    for i, n in enumerate((n0, n1)):
-        part = jnp.dot(n[0:block, :], down_w, preferred_element_type=f32) * down_scale
-        own[i * block : (i + 1) * block, :] = part
-        send[(1 - i) * block : (2 - i) * block, :] = part.astype(bf16)
+def first_kernel(n0, n1, n2, n3, gathered, own, s1, s2, s3):
+    down_w = gathered[:, 0].reshape(-1, RANK)
+    block = n0.shape[0]
+    for i, n in enumerate((n0, n1, n2, n3)):
+        part = jnp.dot(n[...], down_w, preferred_element_type=f32) * down_scale
+        for k, dest in enumerate((own, s1, s2, s3)):
+            j = i ^ k
+            if j < 2:
+                dest[j * block : (j + 1) * block, :] = part.astype(dest.dtype)
 
 
 def middle_kernel(
-    own, received, d0, d1, mine, theirs, slope, active_out, upstream_out, loss, back, send, full
+    own, r1, r2, r3, d0, d1, mine, theirs, slope, active_out, upstream_out, loss, back, send, full
 ):
     up_w = joined(mine, theirs, full)
     losses = 0.0
-    block = d0.shape[0] // 2
+    block = d0.shape[0]
     for i, d in enumerate((d0, d1)):
         at = slice(i * block, (i + 1) * block)
-        pre = own[at, :] + received[at, :].astype(f32)
+        pre = (own[at, :] + r1[at, :].astype(f32)) + (r2[at, :].astype(f32) + r3[at, :].astype(f32))
         logistic = jax.nn.sigmoid(pre)
         slope[at, :] = logistic * (1.0 + pre * (1.0 - logistic))
         active = (pre * logistic).astype(bf16)
@@ -110,7 +122,7 @@
         branch = lax.dot_general(
             active, up_w, (((1,), (1,)), ((), ())), preferred_element_type=f32
         )
-        residual = d[block : 2 * block, :].astype(f32) + branch * up_scale
+        residual = d[...].astype(f32) + branch * up_scale
         losses = losses + jnp.sum(residual * residual, axis=0, keepdims=True)
         upstream = (2.0 * residual).astype(bf16)
         upstream_out[at, :] = upstream
@@ -120,8 +132,7 @@
     lane = lax.broadcasted_iota(jnp.int32, (1, 128), 1)
     tokens = own.shape[0] * (lax.axis_size("x") // 2) * lax.axis_size("z")
     mean = jnp.sum(losses, axis=1, keepdims=True) / (tokens * D)
-    line = jnp.where(lane == 2 + particle_index(), mean, 0.0)
-    loss[...] = jnp.broadcast_to(line[None], loss.shape)
+    loss[...] = jnp.where(lane == 4 + particle_index(), mean, 0.0)
 
 
 def parted(product, mine, theirs, full):
@@ -137,28 +148,27 @@
     parted(up * up_scale, mine, theirs, full)
 
 
-def down_kernel(own, received, slope, n0, n1, mine, theirs, full):
-    back = ((own[...] + received[...].astype(f32)) * slope[...]).astype(bf16)
+def back_kernel(own, received, slope, back):
+    back[...] = ((own[...] + received[...].astype(f32)) * slope[...]).astype(bf16)
+
+
+def last_kernel(back, received, n0, n1, n2, n3, up, up_in, terms):
+    block = n0.shape[0]
     down = 0.0
-    for i, n in enumerate((n0, n1)):
-        block = n.shape[0] // 2
+    for n, source, i in ((n0, back, 0), (n1, back, 1), (n3, received, 0), (n2, received, 1)):
         down = down + lax.dot_general(
-            n[0:block, :],
-            back[i * block : (i + 1) * block],
+            n[...],
+            source[i * block : (i + 1) * block, :],
             (((0,), (0,)), ((), ())),
             preferred_element_type=f32,
         )
-    parted(down * down_scale, mine, theirs, full)
-
-
-def terms_kernel(down, down_in, up, up_in, terms):
-    terms[:, 0] = (down[...] + down_in[...].astype(f32)).astype(bf16)
+    terms[:, 0] = (down * down_scale).astype(bf16).reshape(up.shape)
     terms[:, 1] = (up[...] + up_in[...].astype(f32)).astype(bf16)
 
 
 def total_kernel(received, losses, gradient, line):
-    full = jnp.sum(losses[...], axis=0)
-    lane = lax.broadcasted_iota(jnp.int32, full.shape, 1)
+    full = losses[...]
+    lane = lax.broadcasted_iota(jnp.int32, full.shape, 1) - 2 * lax.axis_index("core")
     for half in range(gradient.shape[0]):
         total = received[0, half].astype(f32)
         for i in range(1, received.shape[0]):
@@ -167,6 +177,10 @@
         square = jnp.sum(jnp.sum(total * total, axis=0, keepdims=True), axis=1, keepdims=True)
         full = full + jnp.where(lane == half, square, 0.0)
     line[...] = jnp.broadcast_to(full[None], line.shape)
+
+
+def add_kernel(a, b, out):
+    out[...] = a[...] + b[...]
 
 
 def learned_kernel(base, perturbation, out):
@@ -195,19 +209,20 @@
 ):
     total = jnp.sum(sums[...], axis=0)
     lane = lax.broadcasted_iota(jnp.int32, total.shape, 1)
-    elements = weights.shape[0] * weights.shape[1] * weights.shape[2] * sums.shape[0] // 2
+    elements = D * RANK
+    mine = 2 * lax.axis_index("core")
     pairs = accumulated.shape[0]
-    own_loss[...] = jnp.sum(jnp.where(lane == 2 + particle_index(), total, 0.0), axis=1, keepdims=True)
+    own_loss[...] = jnp.sum(jnp.where(lane == 4 + particle_index(), total, 0.0), axis=1, keepdims=True)
     row = lax.broadcasted_iota(jnp.int32, (pairs, total.shape[1]), 0)
     spot = lax.broadcasted_iota(jnp.int32, (pairs, total.shape[1]), 1)
-    signs = jnp.where(spot == 2 + 2 * row, 1.0, 0.0) - jnp.where(spot == 3 + 2 * row, 1.0, 0.0)
+    signs = jnp.where(spot == 4 + 2 * row, 1.0, 0.0) - jnp.where(spot == 5 + 2 * row, 1.0, 0.0)
     difference = jnp.sum(signs * total, axis=1, keepdims=True)
     outer[...] = jnp.sum(
         difference * (accumulated[...] + perturbation[...]), axis=0, keepdims=True
     ) / (2 * pairs)
     chunk = 32
     for half in range(2):
-        square = jnp.sum(jnp.where(lane == half, total, 0.0), axis=1, keepdims=True)
+        square = jnp.sum(jnp.where(lane == mine + half, total, 0.0), axis=1, keepdims=True)
         factor = lax.rsqrt(square / elements + grad_eps)
         for start in range(0, weights.shape[1], chunk):
             at = (half, pl.ds(start, chunk))
@@ -243,6 +258,10 @@
     return lax.all_to_all(array, axis, 0, 0, tiled=True)
 
 
+def plus(a, b):
+    return call(add_kernel, [(a.shape, a.dtype)], (a, b), a.size)[0]
+
+
 def local(
     tokens,
     targets,
@@ -255,7 +274,6 @@
     accumulated,
 ):
     nz, nx = lax.axis_size("z"), lax.axis_size("x")
-    particles = lax.axis_size("y") * lax.axis_size("core")
     rows = weights.shape[2]
     block = tokens.shape[0]
     width = 2 * nz * rows
@@ -263,42 +281,52 @@
     shape = (weights.shape[1], rows, RANK)
     column = (nz, rows, RANK)
     full = (nz, 2 * rows, RANK)
+    up_size = nz * rows * RANK
     (copies,) = call(copies_kernel, [((nz, *shape), bf16)], (weights[0],), weights.size)
     gathered = exchange(copies, "z")
-    piece, send = call(
+    cuts = call(
         cut_kernel,
-        [((2 * block, width), bf16)] * 2,
+        [((block, width // 2), bf16)] * nx + [((block, width), bf16)] * 2,
         (tokens, targets, norm_gain[None]),
         20 * block * D,
     )
-    pieces = (piece, swap(send, "x", 1))
-    down_w, up_w = call(split_kernel, [(column, bf16)] * 2, (gathered,), gathered.size)
-    down_w, up_w = (down_w, swap(down_w, "x", 3)), (up_w, swap(up_w, "x", 3))
+    normed = [cuts[0]] + [swap(cuts[k], "x", k) for k in range(1, nx)]
+    gaps = (cuts[nx], swap(cuts[nx + 1], "x", 1))
+    (up_w,) = call(split_kernel, [(column, bf16)], (gathered,), up_size)
+    up_w = (up_w, swap(up_w, "x", 3))
 
     wide, thin = ((tall, RANK), f32), ((tall, RANK), bf16)
     product = 2 * tall * width * RANK
-    joint, sums_of = [(full, bf16)], [(full, f32)]
-    pre, send = call(first_kernel, [wide, thin], (*pieces, *down_w), product, joint)
+    pre, *sends = call(first_kernel, [wide] + [thin] * 3, (*normed, gathered), product)
+    sends = [swap(s, "x", k + 1) for k, s in enumerate(sends)]
     slope, active, upstream, loss, back, send = call(
         middle_kernel,
-        [wide, thin, ((tall, width), bf16), ((particles, 1, 128), f32), wide, thin],
-        (pre, swap(send, "x", 1), *pieces, *up_w),
+        [wide, thin, ((tall, width), bf16), ((1, 128), f32), wide, thin],
+        (pre, *sends, *gaps, *up_w),
         2 * product,
-        joint,
+        [(full, bf16)],
     )
     received = swap(send, "x", 1)
     parts = [(column, f32), (column, bf16)]
-    up, send_up = call(up_kernel, parts, (upstream, active), product, sums_of)
-    up_in = swap(send_up, "x", 3)
-    down, send_down = call(down_kernel, parts, (back, received, slope, *pieces), product, sums_of)
-    down_in = swap(send_down, "x", 3)
-    loss = exchange(loss, ("y", "core"))
-    (terms,) = call(terms_kernel, [((nz, *shape), bf16)], (down, down_in, up, up_in), 4 * down.size)
+    up, send = call(up_kernel, parts, (upstream, active), product, [(full, f32)])
+    up_in = swap(send, "x", 3)
+    (back,) = call(back_kernel, [thin], (back, received, slope), 2 * back.size)
+    back_in = swap(back, "x", 3)
+    loss = plus(loss, swap(loss, "y", 1))
+    back_in, loss = lax.optimization_barrier((back_in, loss))
+    (terms,) = call(
+        last_kernel, [((nz, *shape), bf16)], (back, back_in, *normed, up, up_in), product
+    )
     terms = exchange(terms, "z")
+    loss = plus(loss, swap(loss, "y", 2))
+    loss = plus(loss, swap(loss, "y", 4))
     gradient, line = call(
-        total_kernel, [(shape, f32), ((nz * nx, 1, 128), f32)], (terms, loss), 10 * terms.size
-    )
-    sums = exchange(line, ("z", "x"))
+        total_kernel,
+        [(shape, f32), ((lax.axis_size("core") * nz * nx, 1, 128), f32)],
+        (terms, loss),
+        10 * terms.size,
+    )
+    sums = exchange(line, ("core", "z", "x"))
     (learned,) = call(
         learned_kernel,
         [((1, learned_params.shape[0]), f32)],

time: 116 us -> 111 us (0.957)
  starting transfers between devices: 47.7 us -> 75.1 us
  blocking collectives: 19.1 us -> 0 us
  waiting for transfers between devices: 36.9 us -> 24.4 us
    ppermute x7 -> x14, starting transfers between devices: 21.1 us -> 51.6 us  [swap(): return lax.ppermute(array, axis, pairs)]
    all_to_all x1 -> x0, blocking collectives: 19.1 us -> none  [exchange(): return lax.all_to_all(array, axis, 0, 0, tiled=True)]
    all_to_all x3, waiting for transfers between devices: 28.9 us -> 16.7 us  [exchange(): return lax.all_to_all(array, axis, 0, 0, tiled=True)]
    all_to_all x3, starting transfers between devices: 26.6 us -> 23.5 us  [exchange(): return lax.all_to_all(array, axis, 0, 0, tiled=True)]
    ppermute x7 -> x14, waiting for transfers between devices: 8.04 us -> 7.66 us  [swap(): return lax.ppermute(array, axis, pairs)]
    pallas_call x11 -> x14, Pallas kernels: 8.36 us -> 8.35 us  [call(): pl.pallas_call(kernel, out_shape=[jax.ShapeDtypeStruct(s, d) for s, d in...]
  transfers between devices with their start and end apart: 10 -> 17, of which waited for: 6 -> 8; matrix products, arithmetic and copies ran while one was open for 0% -> 0% of each run, Pallas kernels for 2% -> 1%
where the time goes in v6:
time: 111 us; the launch traced here: 110 us
  starting transfers between devices  75.1 us (68%)
  waiting for transfers between devices  24.4 us (22%)
  Pallas kernels  8.35 us (8%)
  local copies, waits for them, and re-layouts  1.59 us (1%)
    ppermute x14, starting transfers between devices, swap(): return lax.ppermute(array, axis, pairs)  51.6 us
    all_to_all x3, starting transfers between devices, exchange(): return lax.all_to_all(array, axis, 0, 0, tiled=True)  23.5 us
    all_to_all x3, waiting for transfers between devices, exchange(): return lax.all_to_all(array, axis, 0, 0, tiled=True)  16.7 us
    pallas_call x14, Pallas kernels, call(): pl.pallas_call(kernel, out_shape=[jax.ShapeDtypeStruct(s, d) for s, d in...  8.35 us
    ppermute x14, waiting for transfers between devices, swap(): return lax.ppermute(array, axis, pairs)  7.66 us
  transfers between devices with their start and end apart: 17, of which 8 were waited for; matrix products, arithmetic and copies ran while one was open for 0% of the time, Pallas kernels for 1%

profile of v6, /device:TPU:1, one launch (start us, length us, event | category | flops | bytes accessed | tf_op | source)
XLA Modules:
  0.0 110.4 jit_solution(13218126354866173544)
XLA Ops:
  0.6 0.0 copy-start.2
  0.6 0.9 copy-done.2
  1.5 0.8 shard_map.130
  2.4 11.0 %all-to-all-start = ((bf16[8,2,64,256]{3,2,1,0:T(8,128)(2,1)}), bf16[8,2,64,256]{3,2,1,0:T(8,128)(2,1)S(1)}, u32[]{:S(2)}, u32[]{:S(2)}) async-start(bf16[8,2,64,256]{3,2,1,0:T(8,128)(2,1)} %shard_map.130), calls=%async_computation | async-start | bytes 1048576 | tf_op jit(solution)/shard_map/all_to_all | solution.py:258
  13.4 0.0 copy-done
  13.4 0.0 copy-done.1
  13.4 0.7 shard_map.129
  14.1 3.1 %collective-permute-start = (bf16[128,512]{1,0:T(8,128)(2,1)S(1)}, bf16[128,512]{1,0:T(8,128)(2,1)S(1)}, u32[]{:S(2)}, u32[]{:S(2)}) collective-permute-start(bf16[128,512]{1,0:T(8,128)(2,1)S(1)} %get-tuple-element.33), channel_id=1, source_target_pairs={{0,1},{1,0},{2,3},{3,2},{4,5},{5,4},{6,7},{7,6},{8,9},{9,8},{10,11... | collective-permute-start | bytes 393224 | tf_op jit(solution)/shard_map/ppermute | solution.py:254
  17.2 4.4 %collective-permute-start.1 = (bf16[128,512]{1,0:T(8,128)(2,1)S(1)}, bf16[128,512]{1,0:T(8,128)(2,1)S(1)}, u32[]{:S(2)}, u32[]{:S(2)}) collective-permute-start(bf16[128,512]{1,0:T(8,128)(2,1)S(1)} %get-tuple-element.34), channel_id=1, source_target_pairs={{0,2},{1,3},{2,0},{3,1},{4,6},{5,7},{6,4},{7,5},{8,10},{9,11},{10,... | collective-permute-start | bytes 393224 | tf_op jit(solution)/shard_map/ppermute | solution.py:254
  21.6 2.1 %collective-permute-start.2 = (bf16[128,512]{1,0:T(8,128)(2,1)S(1)}, bf16[128,512]{1,0:T(8,128)(2,1)S(1)}, u32[]{:S(2)}, u32[]{:S(2)}) collective-permute-start(bf16[128,512]{1,0:T(8,128)(2,1)S(1)} %get-tuple-element.35), channel_id=1, source_target_pairs={{0,3},{1,2},{2,1},{3,0},{4,7},{5,6},{6,5},{7,4},{8,11},{9,10},{10,... | collective-permute-start | bytes 393224 | tf_op jit(solution)/shard_map/ppermute | solution.py:254
  23.7 1.9 %collective-permute-start.6 = (bf16[128,1024]{1,0:T(8,128)(2,1)S(1)}, bf16[128,1024]{1,0:T(8,128)(2,1)S(1)}, u32[]{:S(2)}, u32[]{:S(2)}) collective-permute-start(bf16[128,1024]{1,0:T(8,128)(2,1)S(1)} %get-tuple-element.41), channel_id=1, source_target_pairs={{0,1},{1,0},{2,3},{3,2},{4,5},{5,4},{6,7},{7,6},{8,9},{9,8},{10,11... | collective-permute-start | bytes 786440 | tf_op jit(solution)/shard_map/ppermute | solution.py:254
  25.6 5.7 %all-to-all-done.gathered = bf16[8,2,64,256]{3,2,1,0:T(8,128)(2,1)S(1)} async-done(((bf16[8,2,64,256]{3,2,1,0:T(8,128)(2,1)}), bf16[8,2,64,256]{3,2,1,0:T(8,128)(2,1)S(1)}, u32[]{:S(2)}, u32[]{:S(2)}) %all-to-all-start) | async-done | bytes 524320 | tf_op jit(solution)/shard_map/all_to_all | solution.py:258
  31.3 4.4 %collective-permute-start.7 = (bf16[8,64,256]{2,1,0:T(8,128)(2,1)S(1)}, bf16[8,64,256]{2,1,0:T(8,128)(2,1)S(1)}, u32[]{:S(2)}, u32[]{:S(2)}) collective-permute-start(bf16[8,64,256]{2,1,0:T(8,128)(2,1)S(1)} %shard_map.132.mine), channel_id=1, source_target_pairs={{0,3},{1,2},{2,1},{3,0},{4,7},{5,6},{6,5},{7,4},{8,11},{9,10},{10,... | collective-permute-start | bytes 786440 | tf_op jit(solution)/shard_map/ppermute | solution.py:254
  35.7 0.0 collective-permute-done.n1
  35.7 0.0 collective-permute-done.1.n2
  35.7 0.0 collective-permute-done.2.n3
  35.8 0.3 shard_map.131
  36.1 1.9 %collective-permute-start.3 = (bf16[256,256]{1,0:T(8,128)(2,1)S(1)}, bf16[256,256]{1,0:T(8,128)(2,1)S(1)}, u32[]{:S(2)}, u32[]{:S(2)}) collective-permute-start(bf16[256,256]{1,0:T(8,128)(2,1)S(1)} %get-tuple-element.37), channel_id=1, source_target_pairs={{0,1},{1,0},{2,3},{3,2},{4,5},{5,4},{6,7},{7,6},{8,9},{9,8},{10,11... | collective-permute-start | bytes 393224 | tf_op jit(solution)/shard_map/ppermute | solution.py:254
  38.0 3.3 %collective-permute-start.4 = (bf16[256,256]{1,0:T(8,128)(2,1)S(1)}, bf16[256,256]{1,0:T(8,128)(2,1)S(1)}, u32[]{:S(2)}, u32[]{:S(2)}) collective-permute-start(bf16[256,256]{1,0:T(8,128)(2,1)S(1)} %get-tuple-element.38), channel_id=1, source_target_pairs={{0,2},{1,3},{2,0},{3,1},{4,6},{5,7},{6,4},{7,5},{8,10},{9,11},{10,... | collective-permute-start | bytes 393224 | tf_op jit(solution)/shard_map/ppermute | solution.py:254
  41.3 4.4 %collective-permute-start.5 = (bf16[256,256]{1,0:T(8,128)(2,1)S(1)}, bf16[256,256]{1,0:T(8,128)(2,1)S(1)}, u32[]{:S(2)}, u32[]{:S(2)}) collective-permute-start(bf16[256,256]{1,0:T(8,128)(2,1)S(1)} %get-tuple-element.39), channel_id=1, source_target_pairs={{0,3},{1,2},{2,1},{3,0},{4,7},{5,6},{6,5},{7,4},{8,11},{9,10},{10,... | collective-permute-start | bytes 393224 | tf_op jit(solution)/shard_map/ppermute | solution.py:254
  45.7 0.0 collective-permute-done.6.d1
  45.7 0.0 collective-permute-done.3.r1
  45.7 0.0 collective-permute-done.4.r2
  45.7 2.5 %collective-permute-done.5.r3 = bf16[256,256]{1,0:T(8,128)(2,1)S(1)} collective-permute-done((bf16[256,256]{1,0:T(8,128)(2,1)S(1)}, bf16[256,256]{1,0:T(8,128)(2,1)S(1)}, u32[]{:S(2)}, u32[]{:S(2)}) %collective-permute-start.5) | collective-permute-done | bytes 131104 | tf_op jit(solution)/shard_map/ppermute | solution.py:254
  48.2 0.0 collective-permute-done.7.theirs
  48.2 0.8 shard_map.133
  49.0 4.8 %collective-permute-start.8 = (bf16[256,256]{1,0:T(8,128)(2,1)S(1)}, bf16[256,256]{1,0:T(8,128)(2,1)S(1)}, u32[]{:S(2)}, u32[]{:S(2)}) collective-permute-start(bf16[256,256]{1,0:T(8,128)(2,1)S(1)} %get-tuple-element.43), channel_id=1, source_target_pairs={{0,1},{1,0},{2,3},{3,2},{4,5},{5,4},{6,7},{7,6},{8,9},{9,8},{10,11... | collective-permute-start | bytes 393224 | tf_op jit(solution)/shard_map/ppermute | solution.py:254
  53.8 0.5 shard_map.136
  54.3 1.9 %collective-permute-start.11 = (bf16[8,64,256]{2,1,0:T(8,128)(2,1)S(1)}, bf16[8,64,256]{2,1,0:T(8,128)(2,1)S(1)}, u32[]{:S(2)}, u32[]{:S(2)}) collective-permute-start(bf16[8,64,256]{2,1,0:T(8,128)(2,1)S(1)} %get-tuple-element.50), channel_id=1, source_target_pairs={{0,3},{1,2},{2,1},{3,0},{4,7},{5,6},{6,5},{7,4},{8,11},{9,10},{10,... | collective-permute-start | bytes 786440 | tf_op jit(solution)/shard_map/ppermute | solution.py:254
  56.3 0.0 collective-permute-done.8.received
  56.3 4.6 %collective-permute-start.9 = (bf16[256,256]{1,0:T(8,128)(2,1)S(1)}, bf16[256,256]{1,0:T(8,128)(2,1)S(1)}, u32[]{:S(2)}, u32[]{:S(2)}) collective-permute-start(bf16[256,256]{1,0:T(8,128)(2,1)S(1)} %shard_map.134.back), channel_id=1, source_target_pairs={{0,3},{1,2},{2,1},{3,0},{4,7},{5,6},{6,5},{7,4},{8,11},{9,10},{10,... | collective-permute-start | bytes 393224 | tf_op jit(solution)/shard_map/ppermute | solution.py:254
  60.9 3.2 %collective-permute-start.10 = (f32[1,128]{1,0:T(1,128)S(1)}, f32[1,128]{1,0:T(1,128)S(1)}, u32[]{:S(2)}, u32[]{:S(2)}) collective-permute-start(f32[1,128]{1,0:T(1,128)S(1)} %get-tuple-element.45.a), channel_id=1, source_target_pairs={{0,64},{64,0},{128,192},{192,128},{256,320},{320,256},{384,448},{4... | collective-permute-start | bytes 1544 | tf_op jit(solution)/shard_map/ppermute | solution.py:254
  64.1 1.4 %collective-permute-done.10.b = f32[1,128]{1,0:T(1,128)S(1)} collective-permute-done((f32[1,128]{1,0:T(1,128)S(1)}, f32[1,128]{1,0:T(1,128)S(1)}, u32[]{:S(2)}, u32[]{:S(2)}) %collective-permute-start.10) | collective-permute-done | bytes 544 | tf_op jit(solution)/shard_map/ppermute | solution.py:254
  65.5 1.8 %collective-permute-done.9.received = bf16[256,256]{1,0:T(8,128)(2,1)S(1)} collective-permute-done((bf16[256,256]{1,0:T(8,128)(2,1)S(1)}, bf16[256,256]{1,0:T(8,128)(2,1)S(1)}, u32[]{:S(2)}, u32[]{:S(2)}) %collective-permute-start.9) | collective-permute-done | bytes 131104 | tf_op jit(solution)/shard_map/ppermute | solution.py:254
  67.3 0.0 collective-permute-done.11.up_in
  67.3 1.3 %shard_map.137 = bf16[8,2,64,256]{3,2,1,0:T(8,128)(2,1)} custom-call(bf16[256,256]{1,0:T(8,128)(2,1)S(1)} %shard_map.134.back, bf16[256,256]{1,0:T(8,128)(2,1)S(1)} %collective-permute-done.9.received, bf16[128,512]{1,0:T(8,128)(2,1)S(1)} %get-tuple-element.32.n0, bf16[128,512]{1,0:T(8,128)(2,1)S(1)} %collective-permute-done.n1, ...), custom_call_target="tpu_custom_call" | custom-call | flops 134217728 | bytes 1572864 | tf_op jit(solution)/shard_map/pallas_call | solution.py:29
  68.6 3.5 %all-to-all-start.1 = ((bf16[8,2,64,256]{3,2,1,0:T(8,128)(2,1)}), bf16[8,2,64,256]{3,2,1,0:T(8,128)(2,1)S(1)}, u32[]{:S(2)}, u32[]{:S(2)}) async-start(bf16[8,2,64,256]{3,2,1,0:T(8,128)(2,1)} %shard_map.137), calls=%async_computation.1 | async-start | bytes 1048576 | tf_op jit(solution)/shard_map/all_to_all | solution.py:258
  72.1 4.2 %collective-permute-start.12 = (f32[1,128]{1,0:T(1,128)S(1)}, f32[1,128]{1,0:T(1,128)S(1)}, u32[]{:S(2)}, u32[]{:S(2)}) collective-permute-start(f32[1,128]{1,0:T(1,128)S(1)} %shard_map.135.a), channel_id=1, source_target_pairs={{0,128},{64,192},{128,0},{192,64},{256,384},{320,448},{384,256},{4... | collective-permute-start | bytes 1544 | tf_op jit(solution)/shard_map/ppermute | solution.py:254
  76.3 1.0 collective-permute-done.12.b
  77.3 7.4 %collective-permute-start.13 = (f32[1,128]{1,0:T(1,128)S(1)}, f32[1,128]{1,0:T(1,128)S(1)}, u32[]{:S(2)}, u32[]{:S(2)}) collective-permute-start(f32[1,128]{1,0:T(1,128)S(1)} %shard_map.138.a), channel_id=1, source_target_pairs={{0,256},{64,320},{128,384},{192,448},{256,0},{320,64},{384,128},{4... | collective-permute-start | bytes 1544 | tf_op jit(solution)/shard_map/ppermute | solution.py:254
  84.8 0.9 collective-permute-done.13.b
  85.7 2.7 %all-to-all-done.1.received = bf16[8,2,64,256]{3,2,1,0:T(8,128)(2,1)S(1)} async-done(((bf16[8,2,64,256]{3,2,1,0:T(8,128)(2,1)}), bf16[8,2,64,256]{3,2,1,0:T(8,128)(2,1)S(1)}, u32[]{:S(2)}, u32[]{:S(2)}) %all-to-all-start.1) | async-done | bytes 524320 | tf_op jit(solution)/shard_map/all_to_all | solution.py:258
  88.4 0.8 shard_map.140
  89.2 9.0 %all-to-all-start.2 = ((f32[64,1,128]{2,1,0:T(1,128)}), f32[64,1,128]{2,1,0:T(1,128)S(1)}, u32[]{:S(2)}, u32[]{:S(2)}) async-start(f32[64,1,128]{2,1,0:T(1,128)} %get-tuple-element.52), calls=%async_computation.2 | async-start | bytes 65536 | tf_op jit(solution)/shard_map/all_to_all | solution.py:258
  98.3 0.0 copy-start.9
  98.3 0.7 copy-done.9
  99.0 8.4 %all-to-all-done.2.sums = f32[64,1,128]{2,1,0:T(1,128)S(1)} async-done(((f32[64,1,128]{2,1,0:T(1,128)}), f32[64,1,128]{2,1,0:T(1,128)S(1)}, u32[]{:S(2)}, u32[]{:S(2)}) %all-to-all-start.2) | async-done | bytes 32800 | tf_op jit(solution)/shard_map/all_to_all | solution.py:258
  107.3 3.0 %shard_map.141 = (f32[2,64,256]{2,1,0:T(8,128)}, f32[2,64,256]{2,1,0:T(8,128)}, f32[2,64,256]{2,1,0:T(8,128)}, f32[1,1]{1,0:T(1,128)}, f32[1,192]{1,0:T(1,128)}) custom-call(f32[192]{0:T(256)S(1)} %bitcast.16, f32[64,1,128]{2,1,0:T(1,128)S(1)} %all-to-all-done.2.sums, f32[2,64,256]{2,1,0:T(8,128)S(1)} %get-tuple-element.53.gradient, ...), custom_call_target="tpu_custom_call" | custom-call | flops 13107200 | bytes 570112 | tf_op jit(solution)/shard_map/pallas_call | solution.py:29
  (20 shorter events, 0.1 us)
Async XLA Ops:
  0.6 0.9 copy-start.2
  1.5 11.8 %copy-start.7 = (f32[2048]{0:T(1024)S(1)}, f32[2048]{0:T(1024)}, u32[]{:S(2)}) copy-start(f32[2048]{0:T(1024)} %param.11) | copy-start | bytes 24580
  2.4 11.0 %copy-start = (bf16[128,2048]{1,0:T(8,128)(2,1)S(1)}, bf16[128,2048]{1,0:T(8,128)(2,1)}, u32[]{:S(2)}) copy-start(bf16[128,2048]{1,0:T(8,128)(2,1)} %tokens.1) | copy-start | bytes 1572868
  2.4 11.0 %copy-start.1 = (bf16[128,2048]{1,0:T(8,128)(2,1)S(1)}, bf16[128,2048]{1,0:T(8,128)(2,1)}, u32[]{:S(2)}) copy-start(bf16[128,2048]{1,0:T(8,128)(2,1)} %targets.1) | copy-start | bytes 1572868
  2.4 28.9 %all-to-all-start = ((bf16[8,2,64,256]{3,2,1,0:T(8,128)(2,1)}), bf16[8,2,64,256]{3,2,1,0:T(8,128)(2,1)S(1)}, u32[]{:S(2)}, u32[]{:S(2)}) async-start(bf16[8,2,64,256]{3,2,1,0:T(8,128)(2,1)} %shard_map.130), calls=%async_computation | async-start | bytes 1048576 | tf_op jit(solution)/shard_map/all_to_all | solution.py:258
  14.1 21.7 %collective-permute-start = (bf16[128,512]{1,0:T(8,128)(2,1)S(1)}, bf16[128,512]{1,0:T(8,128)(2,1)S(1)}, u32[]{:S(2)}, u32[]{:S(2)}) collective-permute-start(bf16[128,512]{1,0:T(8,128)(2,1)S(1)} %get-tuple-element.33), channel_id=1, source_target_pairs={{0,1},{1,0},{2,3},{3,2},{4,5},{5,4},{6,7},{7,6},{8,9},{9,8},{10,11... | collective-permute-start | bytes 393224 | tf_op jit(solution)/shard_map/ppermute | solution.py:254
  17.2 18.6 %collective-permute-start.1 = (bf16[128,512]{1,0:T(8,128)(2,1)S(1)}, bf16[128,512]{1,0:T(8,128)(2,1)S(1)}, u32[]{:S(2)}, u32[]{:S(2)}) collective-permute-start(bf16[128,512]{1,0:T(8,128)(2,1)S(1)} %get-tuple-element.34), channel_id=1, source_target_pairs={{0,2},{1,3},{2,0},{3,1},{4,6},{5,7},{6,4},{7,5},{8,10},{9,11},{10,... | collective-permute-start | bytes 393224 | tf_op jit(solution)/shard_map/ppermute | solution.py:254
  21.6 14.2 %collective-permute-start.2 = (bf16[128,512]{1,0:T(8,128)(2,1)S(1)}, bf16[128,512]{1,0:T(8,128)(2,1)S(1)}, u32[]{:S(2)}, u32[]{:S(2)}) collective-permute-start(bf16[128,512]{1,0:T(8,128)(2,1)S(1)} %get-tuple-element.35), channel_id=1, source_target_pairs={{0,3},{1,2},{2,1},{3,0},{4,7},{5,6},{6,5},{7,4},{8,11},{9,10},{10,... | collective-permute-start | bytes 393224 | tf_op jit(solution)/shard_map/ppermute | solution.py:254
  23.7 22.0 %collective-permute-start.6 = (bf16[128,1024]{1,0:T(8,128)(2,1)S(1)}, bf16[128,1024]{1,0:T(8,128)(2,1)S(1)}, u32[]{:S(2)}, u32[]{:S(2)}) collective-permute-start(bf16[128,1024]{1,0:T(8,128)(2,1)S(1)} %get-tuple-element.41), channel_id=1, source_target_pairs={{0,1},{1,0},{2,3},{3,2},{4,5},{5,4},{6,7},{7,6},{8,9},{9,8},{10,11... | collective-permute-start | bytes 786440 | tf_op jit(solution)/shard_map/ppermute | solution.py:254
  31.3 16.9 %collective-permute-start.7 = (bf16[8,64,256]{2,1,0:T(8,128)(2,1)S(1)}, bf16[8,64,256]{2,1,0:T(8,128)(2,1)S(1)}, u32[]{:S(2)}, u32[]{:S(2)}) collective-permute-start(bf16[8,64,256]{2,1,0:T(8,128)(2,1)S(1)} %shard_map.132.mine), channel_id=1, source_target_pairs={{0,3},{1,2},{2,1},{3,0},{4,7},{5,6},{6,5},{7,4},{8,11},{9,10},{10,... | collective-permute-start | bytes 786440 | tf_op jit(solution)/shard_map/ppermute | solution.py:254
  36.1 9.6 %collective-permute-start.3 = (bf16[256,256]{1,0:T(8,128)(2,1)S(1)}, bf16[256,256]{1,0:T(8,128)(2,1)S(1)}, u32[]{:S(2)}, u32[]{:S(2)}) collective-permute-start(bf16[256,256]{1,0:T(8,128)(2,1)S(1)} %get-tuple-element.37), channel_id=1, source_target_pairs={{0,1},{1,0},{2,3},{3,2},{4,5},{5,4},{6,7},{7,6},{8,9},{9,8},{10,11... | collective-permute-start | bytes 393224 | tf_op jit(solution)/shard_map/ppermute | solution.py:254
  38.0 7.7 %collective-permute-start.4 = (bf16[256,256]{1,0:T(8,128)(2,1)S(1)}, bf16[256,256]{1,0:T(8,128)(2,1)S(1)}, u32[]{:S(2)}, u32[]{:S(2)}) collective-permute-start(bf16[256,256]{1,0:T(8,128)(2,1)S(1)} %get-tuple-element.38), channel_id=1, source_target_pairs={{0,2},{1,3},{2,0},{3,1},{4,6},{5,7},{6,4},{7,5},{8,10},{9,11},{10,... | collective-permute-start | bytes 393224 | tf_op jit(solution)/shard_map/ppermute | solution.py:254
  41.3 6.9 %collective-permute-start.5 = (bf16[256,256]{1,0:T(8,128)(2,1)S(1)}, bf16[256,256]{1,0:T(8,128)(2,1)S(1)}, u32[]{:S(2)}, u32[]{:S(2)}) collective-permute-start(bf16[256,256]{1,0:T(8,128)(2,1)S(1)} %get-tuple-element.39), channel_id=1, source_target_pairs={{0,3},{1,2},{2,1},{3,0},{4,7},{5,6},{6,5},{7,4},{8,11},{9,10},{10,... | collective-permute-start | bytes 393224 | tf_op jit(solution)/shard_map/ppermute | solution.py:254
  49.0 7.2 %collective-permute-start.8 = (bf16[256,256]{1,0:T(8,128)(2,1)S(1)}, bf16[256,256]{1,0:T(8,128)(2,1)S(1)}, u32[]{:S(2)}, u32[]{:S(2)}) collective-permute-start(bf16[256,256]{1,0:T(8,128)(2,1)S(1)} %get-tuple-element.43), channel_id=1, source_target_pairs={{0,1},{1,0},{2,3},{3,2},{4,5},{5,4},{6,7},{7,6},{8,9},{9,8},{10,11... | collective-permute-start | bytes 393224 | tf_op jit(solution)/shard_map/ppermute | solution.py:254
  54.3 13.0 %collective-permute-start.11 = (bf16[8,64,256]{2,1,0:T(8,128)(2,1)S(1)}, bf16[8,64,256]{2,1,0:T(8,128)(2,1)S(1)}, u32[]{:S(2)}, u32[]{:S(2)}) collective-permute-start(bf16[8,64,256]{2,1,0:T(8,128)(2,1)S(1)} %get-tuple-element.50), channel_id=1, source_target_pairs={{0,3},{1,2},{2,1},{3,0},{4,7},{5,6},{6,5},{7,4},{8,11},{9,10},{10,... | collective-permute-start | bytes 786440 | tf_op jit(solution)/shard_map/ppermute | solution.py:254
  56.3 11.0 %collective-permute-start.9 = (bf16[256,256]{1,0:T(8,128)(2,1)S(1)}, bf16[256,256]{1,0:T(8,128)(2,1)S(1)}, u32[]{:S(2)}, u32[]{:S(2)}) collective-permute-start(bf16[256,256]{1,0:T(8,128)(2,1)S(1)} %shard_map.134.back), channel_id=1, source_target_pairs={{0,3},{1,2},{2,1},{3,0},{4,7},{5,6},{6,5},{7,4},{8,11},{9,10},{10,... | collective-permute-start | bytes 393224 | tf_op jit(solution)/shard_map/ppermute | solution.py:254
  60.9 4.6 %collective-permute-start.10 = (f32[1,128]{1,0:T(1,128)S(1)}, f32[1,128]{1,0:T(1,128)S(1)}, u32[]{:S(2)}, u32[]{:S(2)}) collective-permute-start(f32[1,128]{1,0:T(1,128)S(1)} %get-tuple-element.45.a), channel_id=1, source_target_pairs={{0,64},{64,0},{128,192},{192,128},{256,320},{320,256},{384,448},{4... | collective-permute-start | bytes 1544 | tf_op jit(solution)/shard_map/ppermute | solution.py:254
  68.6 19.8 %all-to-all-start.1 = ((bf16[8,2,64,256]{3,2,1,0:T(8,128)(2,1)}), bf16[8,2,64,256]{3,2,1,0:T(8,128)(2,1)S(1)}, u32[]{:S(2)}, u32[]{:S(2)}) async-start(bf16[8,2,64,256]{3,2,1,0:T(8,128)(2,1)} %shard_map.137), calls=%async_computation.1 | async-start | bytes 1048576 | tf_op jit(solution)/shard_map/all_to_all | solution.py:258
  72.1 5.2 %collective-permute-start.12 = (f32[1,128]{1,0:T(1,128)S(1)}, f32[1,128]{1,0:T(1,128)S(1)}, u32[]{:S(2)}, u32[]{:S(2)}) collective-permute-start(f32[1,128]{1,0:T(1,128)S(1)} %shard_map.135.a), channel_id=1, source_target_pairs={{0,128},{64,192},{128,0},{192,64},{256,384},{320,448},{384,256},{4... | collective-permute-start | bytes 1544 | tf_op jit(solution)/shard_map/ppermute | solution.py:254
  77.3 8.4 %collective-permute-start.13 = (f32[1,128]{1,0:T(1,128)S(1)}, f32[1,128]{1,0:T(1,128)S(1)}, u32[]{:S(2)}, u32[]{:S(2)}) collective-permute-start(f32[1,128]{1,0:T(1,128)S(1)} %shard_map.138.a), channel_id=1, source_target_pairs={{0,256},{64,320},{128,384},{192,448},{256,0},{320,64},{384,128},{4... | collective-permute-start | bytes 1544 | tf_op jit(solution)/shard_map/ppermute | solution.py:254
  88.4 18.9 %copy-start.3 = (f32[1,2,64,256]{3,2,1,0:T(8,128)S(1)}, f32[1,2,64,256]{3,2,1,0:T(8,128)}, u32[]{:S(2)}) copy-start(f32[1,2,64,256]{3,2,1,0:T(8,128)} %param.12) | copy-start | bytes 393220
  88.4 18.9 %copy-start.4 = (f32[1,2,64,256]{3,2,1,0:T(8,128)S(1)}, f32[1,2,64,256]{3,2,1,0:T(8,128)}, u32[]{:S(2)}) copy-start(f32[1,2,64,256]{3,2,1,0:T(8,128)} %param.13) | copy-start | bytes 393220
  88.4 18.9 %copy-start.5 = (f32[1,2,64,256]{3,2,1,0:T(8,128)S(1)}, f32[1,2,64,256]{3,2,1,0:T(8,128)}, u32[]{:S(2)}) copy-start(f32[1,2,64,256]{3,2,1,0:T(8,128)} %param.14) | copy-start | bytes 393220
  89.2 9.1 %copy-start.6 = (f32[8,192]{1,0:T(8,128)S(1)}, f32[8,192]{1,0:T(8,128)}, u32[]{:S(2)}) copy-start(f32[8,192]{1,0:T(8,128)} %perturbation.3) | copy-start | bytes 18436
  89.2 18.1 %all-to-all-start.2 = ((f32[64,1,128]{2,1,0:T(1,128)}), f32[64,1,128]{2,1,0:T(1,128)S(1)}, u32[]{:S(2)}, u32[]{:S(2)}) async-start(f32[64,1,128]{2,1,0:T(1,128)} %get-tuple-element.52), calls=%async_computation.2 | async-start | bytes 65536 | tf_op jit(solution)/shard_map/all_to_all | solution.py:258
  98.3 0.7 copy-start.9
  98.9 8.4 %copy-start.8 = (f32[8,192]{1,0:T(8,128)S(1)}, f32[8,192]{1,0:T(8,128)}, u32[]{:S(2)}) copy-start(f32[8,192]{1,0:T(8,128)} %accumulated.1) | copy-start | bytes 18436

commit v7 on v6

--- a/solution.py
+++ b/solution.py
@@ -21,25 +21,33 @@
 bf16 = jnp.bfloat16
 VMEM = pl.BlockSpec(memory_space=pltpu.VMEM)
 SMEM = pl.BlockSpec(memory_space=pltpu.SMEM)
-
-
-def call(kernel, outs, args, flops, scratch=()):
+ANY = pl.BlockSpec(memory_space=pl.ANY)
+
+
+def call(kernel, outs, args, flops, scratch=(), copied=0, copies=0):
     scalars = [a.ndim == 1 for a in args]
     moved = sum(a.size * a.dtype.itemsize for a in args)
     return pl.pallas_call(
         kernel,
         out_shape=[jax.ShapeDtypeStruct(s, d) for s, d in outs],
         in_specs=[SMEM if s else VMEM for s in scalars],
-        out_specs=[VMEM] * len(outs),
-        scratch_shapes=[pltpu.VMEM(s, d) for s, d in scratch],
+        out_specs=[ANY] * copied + [VMEM] * (len(outs) - copied),
+        scratch_shapes=[pltpu.VMEM(s, d) for s, d in scratch]
+        + ([pltpu.SemaphoreType.DMA((copies,))] if copies else []),
         compiler_params=pltpu.CompilerParams(vmem_limit_bytes=16 * 2**20),
         cost_estimate=pl.CostEstimate(flops=flops, bytes_accessed=moved, transcendentals=0),
     )(*args)
 
 
-def copies_kernel(weights, copies):
-    for i in range(copies.shape[0]):
-        copies[i] = weights[...].astype(bf16)
+def copies_kernel(weights, copies, rounded, sems):
+    rounded[...] = weights[...].astype(bf16)
+    moves = [
+        pltpu.make_async_copy(rounded, copies.at[i], sems.at[i]) for i in range(copies.shape[0])
+    ]
+    for move in moves:
+        move.start()
+    for move in moves:
+        move.wait()
 
 
 def cut_kernel(tokens, targets, gain, *outs):
@@ -74,10 +82,6 @@
             dest[:, q * tile : (q + 1) * tile] = jnp.where(keep, kept, moved).astype(bf16)
 
 
-def split_kernel(gathered, up_w):
-    up_w[...] = gathered[:, 1]
-
-
 def halves():
     half = lax.rem(lax.axis_index("x"), 2)
     rows = 64
@@ -90,8 +94,8 @@
 
 def joined(mine, theirs, full):
     own, other = halves()
-    full[:, own] = mine[...]
-    full[:, other] = theirs[...]
+    full[:, own] = mine
+    full[:, other] = theirs.reshape(mine.shape)
     return full[...].reshape(-1, full.shape[-1])
 
 
@@ -104,12 +108,13 @@
             j = i ^ k
             if j < 2:
                 dest[j * block : (j + 1) * block, :] = part.astype(dest.dtype)
+    s3[2 * block :, :] = gathered[:, 1].reshape(-1, RANK)
 
 
 def middle_kernel(
-    own, r1, r2, r3, d0, d1, mine, theirs, slope, active_out, upstream_out, loss, back, send, full
+    own, r1, r2, r3, d0, d1, gathered, slope, active_out, upstream_out, loss, back, send, full
 ):
-    up_w = joined(mine, theirs, full)
+    up_w = joined(gathered[:, 1], r3[own.shape[0] :, :], full)
     losses = 0.0
     block = d0.shape[0]
     for i, d in enumerate((d0, d1)):
@@ -152,7 +157,13 @@
     back[...] = ((own[...] + received[...].astype(f32)) * slope[...]).astype(bf16)
 
 
-def last_kernel(back, received, n0, n1, n2, n3, up, up_in, terms):
+def last_kernel(back, received, n0, n1, n2, n3, up, up_in, terms, down_out, up_out, sems):
+    moves = [
+        pltpu.make_async_copy(source, terms.at[:, i], sems.at[i])
+        for i, source in enumerate((down_out, up_out))
+    ]
+    up_out[...] = (up[...] + up_in[...].astype(f32)).astype(bf16)
+    moves[1].start()
     block = n0.shape[0]
     down = 0.0
     for n, source, i in ((n0, back, 0), (n1, back, 1), (n3, received, 0), (n2, received, 1)):
@@ -162,8 +173,10 @@
             (((0,), (0,)), ((), ())),
             preferred_element_type=f32,
         )
-    terms[:, 0] = (down * down_scale).astype(bf16).reshape(up.shape)
-    terms[:, 1] = (up[...] + up_in[...].astype(f32)).astype(bf16)
+    down_out[...] = (down * down_scale).astype(bf16).reshape(up.shape)
+    moves[0].start()
+    moves[1].wait()
+    moves[0].wait()
 
 
 def total_kernel(received, losses, gradient, line):
@@ -201,11 +214,15 @@
     second,
     accumulated,
     perturbation,
+    weights_out,
+    first_out,
+    second_out,
+    own_loss,
+    outer,
     new_weights,
     new_first,
     new_second,
-    own_loss,
-    outer,
+    sems,
 ):
     total = jnp.sum(sums[...], axis=0)
     lane = lax.broadcasted_iota(jnp.int32, total.shape, 1)
@@ -221,6 +238,8 @@
         difference * (accumulated[...] + perturbation[...]), axis=0, keepdims=True
     ) / (2 * pairs)
     chunk = 32
+    buffers = (new_first, new_second, new_weights)
+    moves = []
     for half in range(2):
         square = jnp.sum(jnp.where(lane == mine + half, total, 0.0), axis=1, keepdims=True)
         factor = lax.rsqrt(square / elements + grad_eps)
@@ -247,6 +266,14 @@
                 out_a = out_a + act * learned[4 * HIDDEN + h]
                 out_b = out_b + act * learned[5 * HIDDEN + h]
             new_weights[at] = weight - step_size * (momentum + out_a) * jnp.exp(jnp.tanh(out_b))
+        for i, dest in enumerate((first_out, second_out, weights_out)):
+            move = pltpu.make_async_copy(
+                buffers[i].at[half], dest.at[half], sems.at[3 * half + i]
+            )
+            move.start()
+            moves.append(move)
+    for move in moves:
+        move.wait()
 
 
 def swap(array, axis, mask):
@@ -281,8 +308,9 @@
     shape = (weights.shape[1], rows, RANK)
     column = (nz, rows, RANK)
     full = (nz, 2 * rows, RANK)
-    up_size = nz * rows * RANK
-    (copies,) = call(copies_kernel, [((nz, *shape), bf16)], (weights[0],), weights.size)
+    (copies,) = call(
+        copies_kernel, [((nz, *shape), bf16)], (weights[0],), weights.size, [(shape, bf16)], 1, nz
+    )
     gathered = exchange(copies, "z")
     cuts = call(
         cut_kernel,
@@ -292,17 +320,19 @@
     )
     normed = [cuts[0]] + [swap(cuts[k], "x", k) for k in range(1, nx)]
     gaps = (cuts[nx], swap(cuts[nx + 1], "x", 1))
-    (up_w,) = call(split_kernel, [(column, bf16)], (gathered,), up_size)
-    up_w = (up_w, swap(up_w, "x", 3))
-
     wide, thin = ((tall, RANK), f32), ((tall, RANK), bf16)
     product = 2 * tall * width * RANK
-    pre, *sends = call(first_kernel, [wide] + [thin] * 3, (*normed, gathered), product)
+    pre, *sends = call(
+        first_kernel,
+        [wide, thin, thin, ((tall + nz * rows, RANK), bf16)],
+        (*normed, gathered),
+        product,
+    )
     sends = [swap(s, "x", k + 1) for k, s in enumerate(sends)]
     slope, active, upstream, loss, back, send = call(
         middle_kernel,
         [wide, thin, ((tall, width), bf16), ((1, 128), f32), wide, thin],
-        (pre, *sends, *gaps, *up_w),
+        (pre, *sends, *gaps, gathered),
         2 * product,
         [(full, bf16)],
     )
@@ -315,11 +345,25 @@
     loss = plus(loss, swap(loss, "y", 1))
     back_in, loss = lax.optimization_barrier((back_in, loss))
     (terms,) = call(
-        last_kernel, [((nz, *shape), bf16)], (back, back_in, *normed, up, up_in), product
+        last_kernel,
+        [((nz, *shape), bf16)],
+        (back, back_in, *normed, up, up_in),
+        product,
+        [(column, bf16)] * 2,
+        1,
+        2,
     )
     terms = exchange(terms, "z")
     loss = plus(loss, swap(loss, "y", 2))
-    loss = plus(loss, swap(loss, "y", 4))
+    loss = plus(loss, swap(loss, "y", 6))
+    (learned,) = call(
+        learned_kernel,
+        [((1, learned_params.shape[0]), f32)],
+        (learned_params[None], perturbation),
+        10 * perturbation.size,
+    )
+    loss, learned = lax.optimization_barrier((loss, learned))
+    learned = learned.reshape(-1)
     gradient, line = call(
         total_kernel,
         [(shape, f32), ((lax.axis_size("core") * nz * nx, 1, 128), f32)],
@@ -327,13 +371,6 @@
         10 * terms.size,
     )
     sums = exchange(line, ("core", "z", "x"))
-    (learned,) = call(
-        learned_kernel,
-        [((1, learned_params.shape[0]), f32)],
-        (learned_params[None], perturbation),
-        10 * perturbation.size,
-    )
-    learned = learned.reshape(-1)
     new_w, new_m, new_v, own_loss, outer = call(
         update_kernel,
         [(shape, f32)] * 3 + [((1, 1), f32), ((1, learned.shape[0]), f32)],
@@ -348,6 +385,9 @@
             perturbation,
         ),
         400 * weights.size,
+        [(shape, f32)] * 3,
+        3,
+        6,
     )
     return (new_w[None], new_m[None], new_v[None], own_loss.reshape(1), outer.reshape(-1))
 

time: 111 us -> 111 us (level)
  blocking collectives: 0 us -> 20.5 us
  starting transfers between devices: 75.1 us -> 59.1 us
  waiting for transfers between devices: 24.4 us -> 20.5 us
    all_to_all x0 -> x1, blocking collectives: none -> 20.5 us  [exchange(): return lax.all_to_all(array, axis, 0, 0, tiled=True)]
    all_to_all x3 -> x2, waiting for transfers between devices: 16.7 us -> 4.64 us  [exchange(): return lax.all_to_all(array, axis, 0, 0, tiled=True)]
    all_to_all x3 -> x2, starting transfers between devices: 23.5 us -> 14.5 us  [exchange(): return lax.all_to_all(array, axis, 0, 0, tiled=True)]
    ppermute x14 -> x13, waiting for transfers between devices: 7.66 us -> 15.9 us  [swap(): return lax.ppermute(array, axis, pairs)]
    ppermute x14 -> x13, starting transfers between devices: 51.6 us -> 44.6 us  [swap(): return lax.ppermute(array, axis, pairs)]
    pallas_call x14 -> x13, Pallas kernels: 8.35 us -> 8.43 us  [call(): pl.pallas_call(kernel, out_shape=[jax.ShapeDtypeStruct(s, d) for s, d in...]
  transfers between devices with their start and end apart: 17 -> 15, of which waited for: 8 -> 11; matrix products, arithmetic and copies ran while one was open for 0% -> 0% of each run, Pallas kernels for 1% -> 1%
where the time goes in v7:
time: 111 us; the launch traced here: 110 us
  starting transfers between devices  59.1 us (53%)
  waiting for transfers between devices  20.5 us (18%)
  blocking collectives  20.5 us (18%)
  Pallas kernels  8.43 us (8%)
    ppermute x13, starting transfers between devices, swap(): return lax.ppermute(array, axis, pairs)  44.6 us
    all_to_all x1, blocking collectives, exchange(): return lax.all_to_all(array, axis, 0, 0, tiled=True)  20.5 us
    ppermute x13, waiting for transfers between devices, swap(): return lax.ppermute(array, axis, pairs)  15.9 us
    all_to_all x2, starting transfers between devices, exchange(): return lax.all_to_all(array, axis, 0, 0, tiled=True)  14.5 us
    pallas_call x13, Pallas kernels, call(): pl.pallas_call(kernel, out_shape=[jax.ShapeDtypeStruct(s, d) for s, d in...  8.43 us
    all_to_all x2, waiting for transfers between devices, exchange(): return lax.all_to_all(array, axis, 0, 0, tiled=True)  4.64 us
  transfers between devices with their start and end apart: 15, of which 11 were waited for; matrix products, arithmetic and copies ran while one was open for 0% of the time, Pallas kernels for 1%

profile of v7, /device:TPU:1, one launch (start us, length us, event | category | flops | bytes accessed | tf_op | source)
XLA Modules:
  0.0 110.4 jit_solution(12938713732971337231)
XLA Ops:
  0.6 0.0 copy-start.2
  0.6 0.9 copy-done.2
  1.5 0.9 shard_map.129
  2.4 0.0 copy-start
  2.4 0.0 copy-start.1
  2.5 11.0 %all-to-all-start = ((bf16[8,2,64,256]{3,2,1,0:T(8,128)(2,1)}), bf16[8,2,64,256]{3,2,1,0:T(8,128)(2,1)S(1)}, u32[]{:S(2)}, u32[]{:S(2)}) async-start(bf16[8,2,64,256]{3,2,1,0:T(8,128)(2,1)} %shard_map.129), calls=%async_computation | async-start | bytes 1048576 | tf_op jit(solution)/shard_map/all_to_all | solution.py:285
  13.5 0.0 copy-done.7
  13.5 0.0 copy-done
  13.5 0.0 copy-done.1
  13.5 0.7 shard_map.128
  14.2 3.1 %collective-permute-start = (bf16[128,512]{1,0:T(8,128)(2,1)S(1)}, bf16[128,512]{1,0:T(8,128)(2,1)S(1)}, u32[]{:S(2)}, u32[]{:S(2)}) collective-permute-start(bf16[128,512]{1,0:T(8,128)(2,1)S(1)} %get-tuple-element.35), channel_id=1, source_target_pairs={{0,1},{1,0},{2,3},{3,2},{4,5},{5,4},{6,7},{7,6},{8,9},{9,8},{10,11... | collective-permute-start | bytes 393224 | tf_op jit(solution)/shard_map/ppermute | solution.py:281
  17.3 4.4 %collective-permute-start.1 = (bf16[128,512]{1,0:T(8,128)(2,1)S(1)}, bf16[128,512]{1,0:T(8,128)(2,1)S(1)}, u32[]{:S(2)}, u32[]{:S(2)}) collective-permute-start(bf16[128,512]{1,0:T(8,128)(2,1)S(1)} %get-tuple-element.36), channel_id=1, source_target_pairs={{0,2},{1,3},{2,0},{3,1},{4,6},{5,7},{6,4},{7,5},{8,10},{9,11},{10,... | collective-permute-start | bytes 393224 | tf_op jit(solution)/shard_map/ppermute | solution.py:281
  21.7 2.1 %collective-permute-start.2 = (bf16[128,512]{1,0:T(8,128)(2,1)S(1)}, bf16[128,512]{1,0:T(8,128)(2,1)S(1)}, u32[]{:S(2)}, u32[]{:S(2)}) collective-permute-start(bf16[128,512]{1,0:T(8,128)(2,1)S(1)} %get-tuple-element.37), channel_id=1, source_target_pairs={{0,3},{1,2},{2,1},{3,0},{4,7},{5,6},{6,5},{7,4},{8,11},{9,10},{10,... | collective-permute-start | bytes 393224 | tf_op jit(solution)/shard_map/ppermute | solution.py:281
  23.8 0.0 collective-permute-done.n1
  23.8 1.5 %collective-permute-done.1.n2 = bf16[128,512]{1,0:T(8,128)(2,1)S(1)} collective-permute-done((bf16[128,512]{1,0:T(8,128)(2,1)S(1)}, bf16[128,512]{1,0:T(8,128)(2,1)S(1)}, u32[]{:S(2)}, u32[]{:S(2)}) %collective-permute-start.1) | collective-permute-done | bytes 131104 | tf_op jit(solution)/shard_map/ppermute | solution.py:281
  25.3 3.3 %collective-permute-done.2.n3 = bf16[128,512]{1,0:T(8,128)(2,1)S(1)} collective-permute-done((bf16[128,512]{1,0:T(8,128)(2,1)S(1)}, bf16[128,512]{1,0:T(8,128)(2,1)S(1)}, u32[]{:S(2)}, u32[]{:S(2)}) %collective-permute-start.2) | collective-permute-done | bytes 131104 | tf_op jit(solution)/shard_map/ppermute | solution.py:281
  28.6 2.8 %all-to-all-done.gathered = bf16[8,2,64,256]{3,2,1,0:T(8,128)(2,1)S(1)} async-done(((bf16[8,2,64,256]{3,2,1,0:T(8,128)(2,1)}), bf16[8,2,64,256]{3,2,1,0:T(8,128)(2,1)S(1)}, u32[]{:S(2)}, u32[]{:S(2)}) %all-to-all-start) | async-done | bytes 524320 | tf_op jit(solution)/shard_map/all_to_all | solution.py:285
  31.4 0.3 shard_map.130
  31.7 4.4 %collective-permute-start.5 = (bf16[768,256]{1,0:T(8,128)(2,1)S(1)}, bf16[768,256]{1,0:T(8,128)(2,1)S(1)}, u32[]{:S(2)}, u32[]{:S(2)}) collective-permute-start(bf16[768,256]{1,0:T(8,128)(2,1)S(1)} %get-tuple-element.41), channel_id=1, source_target_pairs={{0,3},{1,2},{2,1},{3,0},{4,7},{5,6},{6,5},{7,4},{8,11},{9,10},{10,... | collective-permute-start | bytes 1179656 | tf_op jit(solution)/shard_map/ppermute | solution.py:281
  36.1 1.9 %collective-permute-start.6 = (bf16[128,1024]{1,0:T(8,128)(2,1)S(1)}, bf16[128,1024]{1,0:T(8,128)(2,1)S(1)}, u32[]{:S(2)}, u32[]{:S(2)}) collective-permute-start(bf16[128,1024]{1,0:T(8,128)(2,1)S(1)} %get-tuple-element.43), channel_id=1, source_target_pairs={{0,1},{1,0},{2,3},{3,2},{4,5},{5,4},{6,7},{7,6},{8,9},{9,8},{10,11... | collective-permute-start | bytes 786440 | tf_op jit(solution)/shard_map/ppermute | solution.py:281
  38.0 3.4 %collective-permute-start.3 = (bf16[256,256]{1,0:T(8,128)(2,1)S(1)}, bf16[256,256]{1,0:T(8,128)(2,1)S(1)}, u32[]{:S(2)}, u32[]{:S(2)}) collective-permute-start(bf16[256,256]{1,0:T(8,128)(2,1)S(1)} %get-tuple-element.39), channel_id=1, source_target_pairs={{0,1},{1,0},{2,3},{3,2},{4,5},{5,4},{6,7},{7,6},{8,9},{9,8},{10,11... | collective-permute-start | bytes 393224 | tf_op jit(solution)/shard_map/ppermute | solution.py:281
  41.4 2.4 %collective-permute-start.4 = (bf16[256,256]{1,0:T(8,128)(2,1)S(1)}, bf16[256,256]{1,0:T(8,128)(2,1)S(1)}, u32[]{:S(2)}, u32[]{:S(2)}) collective-permute-start(bf16[256,256]{1,0:T(8,128)(2,1)S(1)} %get-tuple-element.40), channel_id=1, source_target_pairs={{0,2},{1,3},{2,0},{3,1},{4,6},{5,7},{6,4},{7,5},{8,10},{9,11},{10,... | collective-permute-start | bytes 393224 | tf_op jit(solution)/shard_map/ppermute | solution.py:281
  43.9 1.2 %collective-permute-done.6.d1 = bf16[128,1024]{1,0:T(8,128)(2,1)S(1)} collective-permute-done((bf16[128,1024]{1,0:T(8,128)(2,1)S(1)}, bf16[128,1024]{1,0:T(8,128)(2,1)S(1)}, u32[]{:S(2)}, u32[]{:S(2)}) %collective-permute-start.6) | collective-permute-done | bytes 262176 | tf_op jit(solution)/shard_map/ppermute | solution.py:281
  45.1 2.8 %collective-permute-done.3.r1 = bf16[256,256]{1,0:T(8,128)(2,1)S(1)} collective-permute-done((bf16[256,256]{1,0:T(8,128)(2,1)S(1)}, bf16[256,256]{1,0:T(8,128)(2,1)S(1)}, u32[]{:S(2)}, u32[]{:S(2)}) %collective-permute-start.3) | collective-permute-done | bytes 131104 | tf_op jit(solution)/shard_map/ppermute | solution.py:281
  47.9 2.7 %collective-permute-done.4.r2 = bf16[256,256]{1,0:T(8,128)(2,1)S(1)} collective-permute-done((bf16[256,256]{1,0:T(8,128)(2,1)S(1)}, bf16[256,256]{1,0:T(8,128)(2,1)S(1)}, u32[]{:S(2)}, u32[]{:S(2)}) %collective-permute-start.4) | collective-permute-done | bytes 131104 | tf_op jit(solution)/shard_map/ppermute | solution.py:281
  50.6 0.0 collective-permute-done.5.r3
  50.6 0.8 shard_map.131
  51.5 1.9 %collective-permute-start.7 = (bf16[256,256]{1,0:T(8,128)(2,1)S(1)}, bf16[256,256]{1,0:T(8,128)(2,1)S(1)}, u32[]{:S(2)}, u32[]{:S(2)}) collective-permute-start(bf16[256,256]{1,0:T(8,128)(2,1)S(1)} %get-tuple-element.45), channel_id=1, source_target_pairs={{0,1},{1,0},{2,3},{3,2},{4,5},{5,4},{6,7},{7,6},{8,9},{9,8},{10,11... | collective-permute-start | bytes 393224 | tf_op jit(solution)/shard_map/ppermute | solution.py:281
  53.4 0.5 shard_map.137
  53.9 4.4 %collective-permute-start.12 = (bf16[8,64,256]{2,1,0:T(8,128)(2,1)S(1)}, bf16[8,64,256]{2,1,0:T(8,128)(2,1)S(1)}, u32[]{:S(2)}, u32[]{:S(2)}) collective-permute-start(bf16[8,64,256]{2,1,0:T(8,128)(2,1)S(1)} %get-tuple-element.54), channel_id=1, source_target_pairs={{0,3},{1,2},{2,1},{3,0},{4,7},{5,6},{6,5},{7,4},{8,11},{9,10},{10,... | collective-permute-start | bytes 786440 | tf_op jit(solution)/shard_map/ppermute | solution.py:281
  58.3 0.0 collective-permute-done.7.received
  58.3 3.2 %collective-permute-start.8 = (bf16[256,256]{1,0:T(8,128)(2,1)S(1)}, bf16[256,256]{1,0:T(8,128)(2,1)S(1)}, u32[]{:S(2)}, u32[]{:S(2)}) collective-permute-start(bf16[256,256]{1,0:T(8,128)(2,1)S(1)} %shard_map.132.back), channel_id=1, source_target_pairs={{0,3},{1,2},{2,1},{3,0},{4,7},{5,6},{6,5},{7,4},{8,11},{9,10},{10,... | collective-permute-start | bytes 393224 | tf_op jit(solution)/shard_map/ppermute | solution.py:281
  61.6 3.2 %collective-permute-start.9 = (f32[1,128]{1,0:T(1,128)S(1)}, f32[1,128]{1,0:T(1,128)S(1)}, u32[]{:S(2)}, u32[]{:S(2)}) collective-permute-start(f32[1,128]{1,0:T(1,128)S(1)} %get-tuple-element.47.a), channel_id=1, source_target_pairs={{0,64},{64,0},{128,192},{192,128},{256,320},{320,256},{384,448},{4... | collective-permute-start | bytes 1544 | tf_op jit(solution)/shard_map/ppermute | solution.py:281
  64.8 1.4 %collective-permute-done.9.b = f32[1,128]{1,0:T(1,128)S(1)} collective-permute-done((f32[1,128]{1,0:T(1,128)S(1)}, f32[1,128]{1,0:T(1,128)S(1)}, u32[]{:S(2)}, u32[]{:S(2)}) %collective-permute-start.9) | collective-permute-done | bytes 544 | tf_op jit(solution)/shard_map/ppermute | solution.py:281
  66.2 0.7 collective-permute-done.8.received
  66.9 0.0 collective-permute-done.12.up_in
  66.9 1.3 %shard_map.138 = bf16[8,2,64,256]{3,2,1,0:T(8,128)(2,1)} custom-call(bf16[256,256]{1,0:T(8,128)(2,1)S(1)} %shard_map.132.back, bf16[256,256]{1,0:T(8,128)(2,1)S(1)} %collective-permute-done.8.received, bf16[128,512]{1,0:T(8,128)(2,1)S(1)} %get-tuple-element.34.n0, bf16[128,512]{1,0:T(8,128)(2,1)S(1)} %collective-permute-done.n1, ...), custom_call_target="tpu_custom_call" | custom-call | flops 134217728 | bytes 1572864 | tf_op jit(solution)/shard_map/pallas_call | solution.py:30
  68.3 0.0 copy-start.6
  68.3 3.5 %all-to-all-start.1 = ((bf16[8,2,64,256]{3,2,1,0:T(8,128)(2,1)}), bf16[8,2,64,256]{3,2,1,0:T(8,128)(2,1)S(1)}, u32[]{:S(2)}, u32[]{:S(2)}) async-start(bf16[8,2,64,256]{3,2,1,0:T(8,128)(2,1)} %shard_map.138), calls=%async_computation.1 | async-start | bytes 1048576 | tf_op jit(solution)/shard_map/all_to_all | solution.py:285
  71.8 4.2 %collective-permute-start.10 = (f32[1,128]{1,0:T(1,128)S(1)}, f32[1,128]{1,0:T(1,128)S(1)}, u32[]{:S(2)}, u32[]{:S(2)}) collective-permute-start(f32[1,128]{1,0:T(1,128)S(1)} %shard_map.133.a), channel_id=1, source_target_pairs={{0,128},{64,192},{128,0},{192,64},{256,384},{320,448},{384,256},{4... | collective-permute-start | bytes 1544 | tf_op jit(solution)/shard_map/ppermute | solution.py:281
  76.0 1.0 collective-permute-done.10.b
  77.0 6.0 %collective-permute-start.11 = (f32[1,128]{1,0:T(1,128)S(1)}, f32[1,128]{1,0:T(1,128)S(1)}, u32[]{:S(2)}, u32[]{:S(2)}) collective-permute-start(f32[1,128]{1,0:T(1,128)S(1)} %shard_map.134.a), channel_id=1, source_target_pairs={{0,384},{64,448},{128,256},{192,320},{256,128},{320,192},{384,0},{... | collective-permute-start | bytes 1544 | tf_op jit(solution)/shard_map/ppermute | solution.py:281
  83.1 1.2 %collective-permute-done.11.b = f32[1,128]{1,0:T(1,128)S(1)} collective-permute-done((f32[1,128]{1,0:T(1,128)S(1)}, f32[1,128]{1,0:T(1,128)S(1)}, u32[]{:S(2)}, u32[]{:S(2)}) %collective-permute-start.11) | collective-permute-done | bytes 544 | tf_op jit(solution)/shard_map/ppermute | solution.py:281
  84.3 1.8 %all-to-all-done.1.received = bf16[8,2,64,256]{3,2,1,0:T(8,128)(2,1)S(1)} async-done(((bf16[8,2,64,256]{3,2,1,0:T(8,128)(2,1)}), bf16[8,2,64,256]{3,2,1,0:T(8,128)(2,1)S(1)}, u32[]{:S(2)}, u32[]{:S(2)}) %all-to-all-start.1) | async-done | bytes 524320 | tf_op jit(solution)/shard_map/all_to_all | solution.py:285
  86.1 0.2 shard_map.139
  86.3 0.0 copy-start.8
  86.3 20.5 %all_to_all.15.sums = f32[64,1,128]{2,1,0:T(1,128)S(1)} all-to-all(f32[64,1,128]{2,1,0:T(1,128)S(1)} %get-tuple-element.56), channel_id=1, replica_groups=mesh['y'=8,'core'=2,'z'=8,'x'=4] {'core','z','x'}, dimensions={0} | all-to-all | bytes 65536 | tf_op jit(solution)/shard_map/all_to_all | solution.py:285
  106.8 3.6 %shard_map.140 = (f32[2,64,256]{2,1,0:T(8,128)}, f32[2,64,256]{2,1,0:T(8,128)}, f32[2,64,256]{2,1,0:T(8,128)}, f32[1,1]{1,0:T(1,128)}, f32[1,192]{1,0:T(1,128)}) custom-call(f32[192]{0:T(256)S(1)} %bitcast.16, f32[64,1,128]{2,1,0:T(1,128)S(1)} %all_to_all.15.sums, f32[2,64,256]{2,1,0:T(8,128)S(1)} %get-tuple-element.57.gradient, f32[2,64,256]{2,1,0:T(8,128)S(1)} %bitcast.12, ...), custom_call_target="tpu_custom_call" | custom-call | flops 13107200 | bytes 570112 | tf_op jit(solution)/shard_map/pallas_call | solution.py:30
  (16 shorter events, 0.1 us)
Async XLA Ops:
  0.6 0.9 copy-start.2
  1.5 11.9 %copy-start.7 = (f32[2048]{0:T(1024)S(1)}, f32[2048]{0:T(1024)}, u32[]{:S(2)}) copy-start(f32[2048]{0:T(1024)} %param.11) | copy-start | bytes 24580
  2.4 11.0 %copy-start = (bf16[128,2048]{1,0:T(8,128)(2,1)S(1)}, bf16[128,2048]{1,0:T(8,128)(2,1)}, u32[]{:S(2)}) copy-start(bf16[128,2048]{1,0:T(8,128)(2,1)} %tokens.1) | copy-start | bytes 1572868
  2.4 11.0 %copy-start.1 = (bf16[128,2048]{1,0:T(8,128)(2,1)S(1)}, bf16[128,2048]{1,0:T(8,128)(2,1)}, u32[]{:S(2)}) copy-start(bf16[128,2048]{1,0:T(8,128)(2,1)} %targets.1) | copy-start | bytes 1572868
  2.5 29.0 %all-to-all-start = ((bf16[8,2,64,256]{3,2,1,0:T(8,128)(2,1)}), bf16[8,2,64,256]{3,2,1,0:T(8,128)(2,1)S(1)}, u32[]{:S(2)}, u32[]{:S(2)}) async-start(bf16[8,2,64,256]{3,2,1,0:T(8,128)(2,1)} %shard_map.129), calls=%async_computation | async-start | bytes 1048576 | tf_op jit(solution)/shard_map/all_to_all | solution.py:285
  14.2 9.6 %collective-permute-start = (bf16[128,512]{1,0:T(8,128)(2,1)S(1)}, bf16[128,512]{1,0:T(8,128)(2,1)S(1)}, u32[]{:S(2)}, u32[]{:S(2)}) collective-permute-start(bf16[128,512]{1,0:T(8,128)(2,1)S(1)} %get-tuple-element.35), channel_id=1, source_target_pairs={{0,1},{1,0},{2,3},{3,2},{4,5},{5,4},{6,7},{7,6},{8,9},{9,8},{10,11... | collective-permute-start | bytes 393224 | tf_op jit(solution)/shard_map/ppermute | solution.py:281
  17.3 8.0 %collective-permute-start.1 = (bf16[128,512]{1,0:T(8,128)(2,1)S(1)}, bf16[128,512]{1,0:T(8,128)(2,1)S(1)}, u32[]{:S(2)}, u32[]{:S(2)}) collective-permute-start(bf16[128,512]{1,0:T(8,128)(2,1)S(1)} %get-tuple-element.36), channel_id=1, source_target_pairs={{0,2},{1,3},{2,0},{3,1},{4,6},{5,7},{6,4},{7,5},{8,10},{9,11},{10,... | collective-permute-start | bytes 393224 | tf_op jit(solution)/shard_map/ppermute | solution.py:281
  21.7 6.9 %collective-permute-start.2 = (bf16[128,512]{1,0:T(8,128)(2,1)S(1)}, bf16[128,512]{1,0:T(8,128)(2,1)S(1)}, u32[]{:S(2)}, u32[]{:S(2)}) collective-permute-start(bf16[128,512]{1,0:T(8,128)(2,1)S(1)} %get-tuple-element.37), channel_id=1, source_target_pairs={{0,3},{1,2},{2,1},{3,0},{4,7},{5,6},{6,5},{7,4},{8,11},{9,10},{10,... | collective-permute-start | bytes 393224 | tf_op jit(solution)/shard_map/ppermute | solution.py:281
  31.7 18.9 %collective-permute-start.5 = (bf16[768,256]{1,0:T(8,128)(2,1)S(1)}, bf16[768,256]{1,0:T(8,128)(2,1)S(1)}, u32[]{:S(2)}, u32[]{:S(2)}) collective-permute-start(bf16[768,256]{1,0:T(8,128)(2,1)S(1)} %get-tuple-element.41), channel_id=1, source_target_pairs={{0,3},{1,2},{2,1},{3,0},{4,7},{5,6},{6,5},{7,4},{8,11},{9,10},{10,... | collective-permute-start | bytes 1179656 | tf_op jit(solution)/shard_map/ppermute | solution.py:281
  36.1 9.0 %collective-permute-start.6 = (bf16[128,1024]{1,0:T(8,128)(2,1)S(1)}, bf16[128,1024]{1,0:T(8,128)(2,1)S(1)}, u32[]{:S(2)}, u32[]{:S(2)}) collective-permute-start(bf16[128,1024]{1,0:T(8,128)(2,1)S(1)} %get-tuple-element.43), channel_id=1, source_target_pairs={{0,1},{1,0},{2,3},{3,2},{4,5},{5,4},{6,7},{7,6},{8,9},{9,8},{10,11... | collective-permute-start | bytes 786440 | tf_op jit(solution)/shard_map/ppermute | solution.py:281
  38.0 9.9 %collective-permute-start.3 = (bf16[256,256]{1,0:T(8,128)(2,1)S(1)}, bf16[256,256]{1,0:T(8,128)(2,1)S(1)}, u32[]{:S(2)}, u32[]{:S(2)}) collective-permute-start(bf16[256,256]{1,0:T(8,128)(2,1)S(1)} %get-tuple-element.39), channel_id=1, source_target_pairs={{0,1},{1,0},{2,3},{3,2},{4,5},{5,4},{6,7},{7,6},{8,9},{9,8},{10,11... | collective-permute-start | bytes 393224 | tf_op jit(solution)/shard_map/ppermute | solution.py:281
  41.4 9.2 %collective-permute-start.4 = (bf16[256,256]{1,0:T(8,128)(2,1)S(1)}, bf16[256,256]{1,0:T(8,128)(2,1)S(1)}, u32[]{:S(2)}, u32[]{:S(2)}) collective-permute-start(bf16[256,256]{1,0:T(8,128)(2,1)S(1)} %get-tuple-element.40), channel_id=1, source_target_pairs={{0,2},{1,3},{2,0},{3,1},{4,6},{5,7},{6,4},{7,5},{8,10},{9,11},{10,... | collective-permute-start | bytes 393224 | tf_op jit(solution)/shard_map/ppermute | solution.py:281
  51.5 6.8 %collective-permute-start.7 = (bf16[256,256]{1,0:T(8,128)(2,1)S(1)}, bf16[256,256]{1,0:T(8,128)(2,1)S(1)}, u32[]{:S(2)}, u32[]{:S(2)}) collective-permute-start(bf16[256,256]{1,0:T(8,128)(2,1)S(1)} %get-tuple-element.45), channel_id=1, source_target_pairs={{0,1},{1,0},{2,3},{3,2},{4,5},{5,4},{6,7},{7,6},{8,9},{9,8},{10,11... | collective-permute-start | bytes 393224 | tf_op jit(solution)/shard_map/ppermute | solution.py:281
  53.9 13.0 %collective-permute-start.12 = (bf16[8,64,256]{2,1,0:T(8,128)(2,1)S(1)}, bf16[8,64,256]{2,1,0:T(8,128)(2,1)S(1)}, u32[]{:S(2)}, u32[]{:S(2)}) collective-permute-start(bf16[8,64,256]{2,1,0:T(8,128)(2,1)S(1)} %get-tuple-element.54), channel_id=1, source_target_pairs={{0,3},{1,2},{2,1},{3,0},{4,7},{5,6},{6,5},{7,4},{8,11},{9,10},{10,... | collective-permute-start | bytes 786440 | tf_op jit(solution)/shard_map/ppermute | solution.py:281
  58.3 8.6 %collective-permute-start.8 = (bf16[256,256]{1,0:T(8,128)(2,1)S(1)}, bf16[256,256]{1,0:T(8,128)(2,1)S(1)}, u32[]{:S(2)}, u32[]{:S(2)}) collective-permute-start(bf16[256,256]{1,0:T(8,128)(2,1)S(1)} %shard_map.132.back), channel_id=1, source_target_pairs={{0,3},{1,2},{2,1},{3,0},{4,7},{5,6},{6,5},{7,4},{8,11},{9,10},{10,... | collective-permute-start | bytes 393224 | tf_op jit(solution)/shard_map/ppermute | solution.py:281
  61.6 4.6 %collective-permute-start.9 = (f32[1,128]{1,0:T(1,128)S(1)}, f32[1,128]{1,0:T(1,128)S(1)}, u32[]{:S(2)}, u32[]{:S(2)}) collective-permute-start(f32[1,128]{1,0:T(1,128)S(1)} %get-tuple-element.47.a), channel_id=1, source_target_pairs={{0,64},{64,0},{128,192},{192,128},{256,320},{320,256},{384,448},{4... | collective-permute-start | bytes 1544 | tf_op jit(solution)/shard_map/ppermute | solution.py:281
  68.3 14.7 %copy-start.6 = (f32[8,192]{1,0:T(8,128)S(1)}, f32[8,192]{1,0:T(8,128)}, u32[]{:S(2)}) copy-start(f32[8,192]{1,0:T(8,128)} %perturbation.3) | copy-start | bytes 18436
  68.3 17.8 %all-to-all-start.1 = ((bf16[8,2,64,256]{3,2,1,0:T(8,128)(2,1)}), bf16[8,2,64,256]{3,2,1,0:T(8,128)(2,1)S(1)}, u32[]{:S(2)}, u32[]{:S(2)}) async-start(bf16[8,2,64,256]{3,2,1,0:T(8,128)(2,1)} %shard_map.138), calls=%async_computation.1 | async-start | bytes 1048576 | tf_op jit(solution)/shard_map/all_to_all | solution.py:285
  71.8 5.2 %collective-permute-start.10 = (f32[1,128]{1,0:T(1,128)S(1)}, f32[1,128]{1,0:T(1,128)S(1)}, u32[]{:S(2)}, u32[]{:S(2)}) collective-permute-start(f32[1,128]{1,0:T(1,128)S(1)} %shard_map.133.a), channel_id=1, source_target_pairs={{0,128},{64,192},{128,0},{192,64},{256,384},{320,448},{384,256},{4... | collective-permute-start | bytes 1544 | tf_op jit(solution)/shard_map/ppermute | solution.py:281
  77.0 6.0 %copy-start.9 = (f32[192]{0:T(256)S(1)}, f32[192]{0:T(256)}, u32[]{:S(2)}) copy-start(f32[192]{0:T(256)} %param.15) | copy-start | bytes 2308
  77.0 7.2 %collective-permute-start.11 = (f32[1,128]{1,0:T(1,128)S(1)}, f32[1,128]{1,0:T(1,128)S(1)}, u32[]{:S(2)}, u32[]{:S(2)}) collective-permute-start(f32[1,128]{1,0:T(1,128)S(1)} %shard_map.134.a), channel_id=1, source_target_pairs={{0,384},{64,448},{128,256},{192,320},{256,128},{320,192},{384,0},{... | collective-permute-start | bytes 1544 | tf_op jit(solution)/shard_map/ppermute | solution.py:281
  86.1 20.7 %copy-start.3 = (f32[1,2,64,256]{3,2,1,0:T(8,128)S(1)}, f32[1,2,64,256]{3,2,1,0:T(8,128)}, u32[]{:S(2)}) copy-start(f32[1,2,64,256]{3,2,1,0:T(8,128)} %param.12) | copy-start | bytes 393220
  86.1 20.7 %copy-start.4 = (f32[1,2,64,256]{3,2,1,0:T(8,128)S(1)}, f32[1,2,64,256]{3,2,1,0:T(8,128)}, u32[]{:S(2)}) copy-start(f32[1,2,64,256]{3,2,1,0:T(8,128)} %param.13) | copy-start | bytes 393220
  86.1 20.7 %copy-start.5 = (f32[1,2,64,256]{3,2,1,0:T(8,128)S(1)}, f32[1,2,64,256]{3,2,1,0:T(8,128)}, u32[]{:S(2)}) copy-start(f32[1,2,64,256]{3,2,1,0:T(8,128)} %param.14) | copy-start | bytes 393220
  86.3 20.5 %copy-start.8 = (f32[8,192]{1,0:T(8,128)S(1)}, f32[8,192]{1,0:T(8,128)}, u32[]{:S(2)}) copy-start(f32[8,192]{1,0:T(8,128)} %accumulated.1) | copy-start | bytes 18436

commit v8 on v6

--- a/solution.py
+++ b/solution.py
@@ -74,10 +74,6 @@
             dest[:, q * tile : (q + 1) * tile] = jnp.where(keep, kept, moved).astype(bf16)
 
 
-def split_kernel(gathered, up_w):
-    up_w[...] = gathered[:, 1]
-
-
 def halves():
     half = lax.rem(lax.axis_index("x"), 2)
     rows = 64
@@ -90,8 +86,8 @@
 
 def joined(mine, theirs, full):
     own, other = halves()
-    full[:, own] = mine[...]
-    full[:, other] = theirs[...]
+    full[:, own] = mine
+    full[:, other] = theirs.reshape(mine.shape)
     return full[...].reshape(-1, full.shape[-1])
 
 
@@ -104,12 +100,13 @@
             j = i ^ k
             if j < 2:
                 dest[j * block : (j + 1) * block, :] = part.astype(dest.dtype)
+    s3[2 * block :, :] = gathered[:, 1].reshape(-1, RANK)
 
 
 def middle_kernel(
-    own, r1, r2, r3, d0, d1, mine, theirs, slope, active_out, upstream_out, loss, back, send, full
+    own, r1, r2, r3, d0, d1, gathered, slope, active_out, upstream_out, loss, back, send, full
 ):
-    up_w = joined(mine, theirs, full)
+    up_w = joined(gathered[:, 1], r3[own.shape[0] :, :], full)
     losses = 0.0
     block = d0.shape[0]
     for i, d in enumerate((d0, d1)):
@@ -281,7 +278,6 @@
     shape = (weights.shape[1], rows, RANK)
     column = (nz, rows, RANK)
     full = (nz, 2 * rows, RANK)
-    up_size = nz * rows * RANK
     (copies,) = call(copies_kernel, [((nz, *shape), bf16)], (weights[0],), weights.size)
     gathered = exchange(copies, "z")
     cuts = call(
@@ -292,17 +288,19 @@
     )
     normed = [cuts[0]] + [swap(cuts[k], "x", k) for k in range(1, nx)]
     gaps = (cuts[nx], swap(cuts[nx + 1], "x", 1))
-    (up_w,) = call(split_kernel, [(column, bf16)], (gathered,), up_size)
-    up_w = (up_w, swap(up_w, "x", 3))
-
     wide, thin = ((tall, RANK), f32), ((tall, RANK), bf16)
     product = 2 * tall * width * RANK
-    pre, *sends = call(first_kernel, [wide] + [thin] * 3, (*normed, gathered), product)
+    pre, *sends = call(
+        first_kernel,
+        [wide, thin, thin, ((tall + nz * rows, RANK), bf16)],
+        (*normed, gathered),
+        product,
+    )
     sends = [swap(s, "x", k + 1) for k, s in enumerate(sends)]
     slope, active, upstream, loss, back, send = call(
         middle_kernel,
         [wide, thin, ((tall, width), bf16), ((1, 128), f32), wide, thin],
-        (pre, *sends, *gaps, *up_w),
+        (pre, *sends, *gaps, gathered),
         2 * product,
         [(full, bf16)],
     )
@@ -319,7 +317,15 @@
     )
     terms = exchange(terms, "z")
     loss = plus(loss, swap(loss, "y", 2))
-    loss = plus(loss, swap(loss, "y", 4))
+    loss = plus(loss, swap(loss, "y", 6))
+    (learned,) = call(
+        learned_kernel,
+        [((1, learned_params.shape[0]), f32)],
+        (learned_params[None], perturbation),
+        10 * perturbation.size,
+    )
+    loss, learned = lax.optimization_barrier((loss, learned))
+    learned = learned.reshape(-1)
     gradient, line = call(
         total_kernel,
         [(shape, f32), ((lax.axis_size("core") * nz * nx, 1, 128), f32)],
@@ -327,13 +333,6 @@
         10 * terms.size,
     )
     sums = exchange(line, ("core", "z", "x"))
-    (learned,) = call(
-        learned_kernel,
-        [((1, learned_params.shape[0]), f32)],
-        (learned_params[None], perturbation),
-        10 * perturbation.size,
-    )
-    learned = learned.reshape(-1)
     new_w, new_m, new_v, own_loss, outer = call(
         update_kernel,
         [(shape, f32)] * 3 + [((1, 1), f32), ((1, learned.shape[0]), f32)],

time: 111 us -> 111 us (level)
  blocking collectives: 0 us -> 20.5 us
  starting transfers between devices: 75.1 us -> 59.3 us
  waiting for transfers between devices: 24.4 us -> 20.4 us
    all_to_all x0 -> x1, blocking collectives: none -> 20.5 us  [exchange(): return lax.all_to_all(array, axis, 0, 0, tiled=True)]
    all_to_all x3 -> x2, waiting for transfers between devices: 16.7 us -> 4.56 us  [exchange(): return lax.all_to_all(array, axis, 0, 0, tiled=True)]
    all_to_all x3 -> x2, starting transfers between devices: 23.5 us -> 14.6 us  [exchange(): return lax.all_to_all(array, axis, 0, 0, tiled=True)]
    ppermute x14 -> x13, waiting for transfers between devices: 7.66 us -> 15.8 us  [swap(): return lax.ppermute(array, axis, pairs)]
    ppermute x14 -> x13, starting transfers between devices: 51.6 us -> 44.7 us  [swap(): return lax.ppermute(array, axis, pairs)]
    pallas_call x14 -> x13, Pallas kernels: 8.35 us -> 7.78 us  [call(): pl.pallas_call(kernel, out_shape=[jax.ShapeDtypeStruct(s, d) for s, d in...]
  transfers between devices with their start and end apart: 17 -> 15, of which waited for: 8 -> 11; matrix products, arithmetic and copies ran while one was open for 0% -> 0% of each run, Pallas kernels for 1% -> 1%
where the time goes in v8:
time: 111 us; the launch traced here: 110 us
  starting transfers between devices  59.3 us (53%)
  blocking collectives  20.5 us (18%)
  waiting for transfers between devices  20.4 us (18%)
  Pallas kernels  7.78 us (7%)
    ppermute x13, starting transfers between devices, swap(): return lax.ppermute(array, axis, pairs)  44.7 us
    all_to_all x1, blocking collectives, exchange(): return lax.all_to_all(array, axis, 0, 0, tiled=True)  20.5 us
    ppermute x13, waiting for transfers between devices, swap(): return lax.ppermute(array, axis, pairs)  15.8 us
    all_to_all x2, starting transfers between devices, exchange(): return lax.all_to_all(array, axis, 0, 0, tiled=True)  14.6 us
    pallas_call x13, Pallas kernels, call(): pl.pallas_call(kernel, out_shape=[jax.ShapeDtypeStruct(s, d) for s, d in...  7.78 us
    all_to_all x2, waiting for transfers between devices, exchange(): return lax.all_to_all(array, axis, 0, 0, tiled=True)  4.56 us
  transfers between devices with their start and end apart: 15, of which 11 were waited for; matrix products, arithmetic and copies ran while one was open for 0% of the time, Pallas kernels for 1%

profile of v8, /device:TPU:1, one launch (start us, length us, event | category | flops | bytes accessed | tf_op | source)
XLA Modules:
  0.0 109.8 jit_solution(13002547133247849854)
XLA Ops:
  0.6 0.0 copy-start.2
  0.6 0.9 copy-done.2
  1.5 0.8 shard_map.129
  2.4 11.0 %all-to-all-start = ((bf16[8,2,64,256]{3,2,1,0:T(8,128)(2,1)}), bf16[8,2,64,256]{3,2,1,0:T(8,128)(2,1)S(1)}, u32[]{:S(2)}, u32[]{:S(2)}) async-start(bf16[8,2,64,256]{3,2,1,0:T(8,128)(2,1)} %shard_map.129), calls=%async_computation | async-start | bytes 1048576 | tf_op jit(solution)/shard_map/all_to_all | solution.py:255
  13.4 0.0 copy-done.7
  13.4 0.0 copy-done
  13.4 0.0 copy-done.1
  13.4 0.7 shard_map.128
  14.1 3.1 %collective-permute-start = (bf16[128,512]{1,0:T(8,128)(2,1)S(1)}, bf16[128,512]{1,0:T(8,128)(2,1)S(1)}, u32[]{:S(2)}, u32[]{:S(2)}) collective-permute-start(bf16[128,512]{1,0:T(8,128)(2,1)S(1)} %get-tuple-element.35), channel_id=1, source_target_pairs={{0,1},{1,0},{2,3},{3,2},{4,5},{5,4},{6,7},{7,6},{8,9},{9,8},{10,11... | collective-permute-start | bytes 393224 | tf_op jit(solution)/shard_map/ppermute | solution.py:251
  17.2 4.4 %collective-permute-start.1 = (bf16[128,512]{1,0:T(8,128)(2,1)S(1)}, bf16[128,512]{1,0:T(8,128)(2,1)S(1)}, u32[]{:S(2)}, u32[]{:S(2)}) collective-permute-start(bf16[128,512]{1,0:T(8,128)(2,1)S(1)} %get-tuple-element.36), channel_id=1, source_target_pairs={{0,2},{1,3},{2,0},{3,1},{4,6},{5,7},{6,4},{7,5},{8,10},{9,11},{10,... | collective-permute-start | bytes 393224 | tf_op jit(solution)/shard_map/ppermute | solution.py:251
  21.6 2.1 %collective-permute-start.2 = (bf16[128,512]{1,0:T(8,128)(2,1)S(1)}, bf16[128,512]{1,0:T(8,128)(2,1)S(1)}, u32[]{:S(2)}, u32[]{:S(2)}) collective-permute-start(bf16[128,512]{1,0:T(8,128)(2,1)S(1)} %get-tuple-element.37), channel_id=1, source_target_pairs={{0,3},{1,2},{2,1},{3,0},{4,7},{5,6},{6,5},{7,4},{8,11},{9,10},{10,... | collective-permute-start | bytes 393224 | tf_op jit(solution)/shard_map/ppermute | solution.py:251
  23.7 0.0 collective-permute-done.n1
  23.7 1.5 %collective-permute-done.1.n2 = bf16[128,512]{1,0:T(8,128)(2,1)S(1)} collective-permute-done((bf16[128,512]{1,0:T(8,128)(2,1)S(1)}, bf16[128,512]{1,0:T(8,128)(2,1)S(1)}, u32[]{:S(2)}, u32[]{:S(2)}) %collective-permute-start.1) | collective-permute-done | bytes 131104 | tf_op jit(solution)/shard_map/ppermute | solution.py:251
  25.2 3.3 %collective-permute-done.2.n3 = bf16[128,512]{1,0:T(8,128)(2,1)S(1)} collective-permute-done((bf16[128,512]{1,0:T(8,128)(2,1)S(1)}, bf16[128,512]{1,0:T(8,128)(2,1)S(1)}, u32[]{:S(2)}, u32[]{:S(2)}) %collective-permute-start.2) | collective-permute-done | bytes 131104 | tf_op jit(solution)/shard_map/ppermute | solution.py:251
  28.5 2.8 %all-to-all-done.gathered = bf16[8,2,64,256]{3,2,1,0:T(8,128)(2,1)S(1)} async-done(((bf16[8,2,64,256]{3,2,1,0:T(8,128)(2,1)}), bf16[8,2,64,256]{3,2,1,0:T(8,128)(2,1)S(1)}, u32[]{:S(2)}, u32[]{:S(2)}) %all-to-all-start) | async-done | bytes 524320 | tf_op jit(solution)/shard_map/all_to_all | solution.py:255
  31.3 0.3 shard_map.130
  31.6 4.4 %collective-permute-start.5 = (bf16[768,256]{1,0:T(8,128)(2,1)S(1)}, bf16[768,256]{1,0:T(8,128)(2,1)S(1)}, u32[]{:S(2)}, u32[]{:S(2)}) collective-permute-start(bf16[768,256]{1,0:T(8,128)(2,1)S(1)} %get-tuple-element.41), channel_id=1, source_target_pairs={{0,3},{1,2},{2,1},{3,0},{4,7},{5,6},{6,5},{7,4},{8,11},{9,10},{10,... | collective-permute-start | bytes 1179656 | tf_op jit(solution)/shard_map/ppermute | solution.py:251
  36.0 1.9 %collective-permute-start.6 = (bf16[128,1024]{1,0:T(8,128)(2,1)S(1)}, bf16[128,1024]{1,0:T(8,128)(2,1)S(1)}, u32[]{:S(2)}, u32[]{:S(2)}) collective-permute-start(bf16[128,1024]{1,0:T(8,128)(2,1)S(1)} %get-tuple-element.43), channel_id=1, source_target_pairs={{0,1},{1,0},{2,3},{3,2},{4,5},{5,4},{6,7},{7,6},{8,9},{9,8},{10,11... | collective-permute-start | bytes 786440 | tf_op jit(solution)/shard_map/ppermute | solution.py:251
  38.0 3.4 %collective-permute-start.3 = (bf16[256,256]{1,0:T(8,128)(2,1)S(1)}, bf16[256,256]{1,0:T(8,128)(2,1)S(1)}, u32[]{:S(2)}, u32[]{:S(2)}) collective-permute-start(bf16[256,256]{1,0:T(8,128)(2,1)S(1)} %get-tuple-element.39), channel_id=1, source_target_pairs={{0,1},{1,0},{2,3},{3,2},{4,5},{5,4},{6,7},{7,6},{8,9},{9,8},{10,11... | collective-permute-start | bytes 393224 | tf_op jit(solution)/shard_map/ppermute | solution.py:251
  41.3 2.4 %collective-permute-start.4 = (bf16[256,256]{1,0:T(8,128)(2,1)S(1)}, bf16[256,256]{1,0:T(8,128)(2,1)S(1)}, u32[]{:S(2)}, u32[]{:S(2)}) collective-permute-start(bf16[256,256]{1,0:T(8,128)(2,1)S(1)} %get-tuple-element.40), channel_id=1, source_target_pairs={{0,2},{1,3},{2,0},{3,1},{4,6},{5,7},{6,4},{7,5},{8,10},{9,11},{10,... | collective-permute-start | bytes 393224 | tf_op jit(solution)/shard_map/ppermute | solution.py:251
  43.8 1.2 %collective-permute-done.6.d1 = bf16[128,1024]{1,0:T(8,128)(2,1)S(1)} collective-permute-done((bf16[128,1024]{1,0:T(8,128)(2,1)S(1)}, bf16[128,1024]{1,0:T(8,128)(2,1)S(1)}, u32[]{:S(2)}, u32[]{:S(2)}) %collective-permute-start.6) | collective-permute-done | bytes 262176 | tf_op jit(solution)/shard_map/ppermute | solution.py:251
  45.0 2.8 %collective-permute-done.3.r1 = bf16[256,256]{1,0:T(8,128)(2,1)S(1)} collective-permute-done((bf16[256,256]{1,0:T(8,128)(2,1)S(1)}, bf16[256,256]{1,0:T(8,128)(2,1)S(1)}, u32[]{:S(2)}, u32[]{:S(2)}) %collective-permute-start.3) | collective-permute-done | bytes 131104 | tf_op jit(solution)/shard_map/ppermute | solution.py:251
  47.8 2.7 %collective-permute-done.4.r2 = bf16[256,256]{1,0:T(8,128)(2,1)S(1)} collective-permute-done((bf16[256,256]{1,0:T(8,128)(2,1)S(1)}, bf16[256,256]{1,0:T(8,128)(2,1)S(1)}, u32[]{:S(2)}, u32[]{:S(2)}) %collective-permute-start.4) | collective-permute-done | bytes 131104 | tf_op jit(solution)/shard_map/ppermute | solution.py:251
  50.6 0.0 collective-permute-done.5.r3
  50.6 0.8 shard_map.131
  51.4 1.9 %collective-permute-start.7 = (bf16[256,256]{1,0:T(8,128)(2,1)S(1)}, bf16[256,256]{1,0:T(8,128)(2,1)S(1)}, u32[]{:S(2)}, u32[]{:S(2)}) collective-permute-start(bf16[256,256]{1,0:T(8,128)(2,1)S(1)} %get-tuple-element.45), channel_id=1, source_target_pairs={{0,1},{1,0},{2,3},{3,2},{4,5},{5,4},{6,7},{7,6},{8,9},{9,8},{10,11... | collective-permute-start | bytes 393224 | tf_op jit(solution)/shard_map/ppermute | solution.py:251
  53.3 0.5 shard_map.137
  53.8 4.4 %collective-permute-start.12 = (bf16[8,64,256]{2,1,0:T(8,128)(2,1)S(1)}, bf16[8,64,256]{2,1,0:T(8,128)(2,1)S(1)}, u32[]{:S(2)}, u32[]{:S(2)}) collective-permute-start(bf16[8,64,256]{2,1,0:T(8,128)(2,1)S(1)} %get-tuple-element.54), channel_id=1, source_target_pairs={{0,3},{1,2},{2,1},{3,0},{4,7},{5,6},{6,5},{7,4},{8,11},{9,10},{10,... | collective-permute-start | bytes 786440 | tf_op jit(solution)/shard_map/ppermute | solution.py:251
  58.2 0.0 collective-permute-done.7.received
  58.3 3.2 %collective-permute-start.8 = (bf16[256,256]{1,0:T(8,128)(2,1)S(1)}, bf16[256,256]{1,0:T(8,128)(2,1)S(1)}, u32[]{:S(2)}, u32[]{:S(2)}) collective-permute-start(bf16[256,256]{1,0:T(8,128)(2,1)S(1)} %shard_map.132.back), channel_id=1, source_target_pairs={{0,3},{1,2},{2,1},{3,0},{4,7},{5,6},{6,5},{7,4},{8,11},{9,10},{10,... | collective-permute-start | bytes 393224 | tf_op jit(solution)/shard_map/ppermute | solution.py:251
  61.5 3.2 %collective-permute-start.9 = (f32[1,128]{1,0:T(1,128)S(1)}, f32[1,128]{1,0:T(1,128)S(1)}, u32[]{:S(2)}, u32[]{:S(2)}) collective-permute-start(f32[1,128]{1,0:T(1,128)S(1)} %get-tuple-element.47.a), channel_id=1, source_target_pairs={{0,64},{64,0},{128,192},{192,128},{256,320},{320,256},{384,448},{4... | collective-permute-start | bytes 1544 | tf_op jit(solution)/shard_map/ppermute | solution.py:251
  64.7 1.4 %collective-permute-done.9.b = f32[1,128]{1,0:T(1,128)S(1)} collective-permute-done((f32[1,128]{1,0:T(1,128)S(1)}, f32[1,128]{1,0:T(1,128)S(1)}, u32[]{:S(2)}, u32[]{:S(2)}) %collective-permute-start.9) | collective-permute-done | bytes 544 | tf_op jit(solution)/shard_map/ppermute | solution.py:251
  66.1 0.7 collective-permute-done.8.received
  66.8 0.0 collective-permute-done.12.up_in
  66.8 1.3 %shard_map.138 = bf16[8,2,64,256]{3,2,1,0:T(8,128)(2,1)} custom-call(bf16[256,256]{1,0:T(8,128)(2,1)S(1)} %shard_map.132.back, bf16[256,256]{1,0:T(8,128)(2,1)S(1)} %collective-permute-done.8.received, bf16[128,512]{1,0:T(8,128)(2,1)S(1)} %get-tuple-element.34.n0, bf16[128,512]{1,0:T(8,128)(2,1)S(1)} %collective-permute-done.n1, ...), custom_call_target="tpu_custom_call" | custom-call | flops 134217728 | bytes 1572864 | tf_op jit(solution)/shard_map/pallas_call | solution.py:29
  68.2 3.6 %all-to-all-start.1 = ((bf16[8,2,64,256]{3,2,1,0:T(8,128)(2,1)}), bf16[8,2,64,256]{3,2,1,0:T(8,128)(2,1)S(1)}, u32[]{:S(2)}, u32[]{:S(2)}) async-start(bf16[8,2,64,256]{3,2,1,0:T(8,128)(2,1)} %shard_map.138), calls=%async_computation.1 | async-start | bytes 1048576 | tf_op jit(solution)/shard_map/all_to_all | solution.py:255
  71.8 4.2 %collective-permute-start.10 = (f32[1,128]{1,0:T(1,128)S(1)}, f32[1,128]{1,0:T(1,128)S(1)}, u32[]{:S(2)}, u32[]{:S(2)}) collective-permute-start(f32[1,128]{1,0:T(1,128)S(1)} %shard_map.133.a), channel_id=1, source_target_pairs={{0,128},{64,192},{128,0},{192,64},{256,384},{320,448},{384,256},{4... | collective-permute-start | bytes 1544 | tf_op jit(solution)/shard_map/ppermute | solution.py:251
  76.0 1.0 collective-permute-done.10.b
  77.0 6.0 %collective-permute-start.11 = (f32[1,128]{1,0:T(1,128)S(1)}, f32[1,128]{1,0:T(1,128)S(1)}, u32[]{:S(2)}, u32[]{:S(2)}) collective-permute-start(f32[1,128]{1,0:T(1,128)S(1)} %shard_map.134.a), channel_id=1, source_target_pairs={{0,384},{64,448},{128,256},{192,320},{256,128},{320,192},{384,0},{... | collective-permute-start | bytes 1544 | tf_op jit(solution)/shard_map/ppermute | solution.py:251
  83.0 0.0 copy-done.6
  83.1 1.2 %collective-permute-done.11.b = f32[1,128]{1,0:T(1,128)S(1)} collective-permute-done((f32[1,128]{1,0:T(1,128)S(1)}, f32[1,128]{1,0:T(1,128)S(1)}, u32[]{:S(2)}, u32[]{:S(2)}) %collective-permute-start.11) | collective-permute-done | bytes 544 | tf_op jit(solution)/shard_map/ppermute | solution.py:251
  84.3 1.7 %all-to-all-done.1.received = bf16[8,2,64,256]{3,2,1,0:T(8,128)(2,1)S(1)} async-done(((bf16[8,2,64,256]{3,2,1,0:T(8,128)(2,1)}), bf16[8,2,64,256]{3,2,1,0:T(8,128)(2,1)S(1)}, u32[]{:S(2)}, u32[]{:S(2)}) %all-to-all-start.1) | async-done | bytes 524320 | tf_op jit(solution)/shard_map/all_to_all | solution.py:255
  86.0 0.2 shard_map.139
  86.2 0.0 copy-start.8
  86.2 20.5 %all_to_all.15.sums = f32[64,1,128]{2,1,0:T(1,128)S(1)} all-to-all(f32[64,1,128]{2,1,0:T(1,128)S(1)} %get-tuple-element.56), channel_id=1, replica_groups=mesh['y'=8,'core'=2,'z'=8,'x'=4] {'core','z','x'}, dimensions={0} | all-to-all | bytes 65536 | tf_op jit(solution)/shard_map/all_to_all | solution.py:255
  106.7 0.0 copy-done.5
  106.8 0.0 copy-done.8
  106.8 3.0 %shard_map.140 = (f32[2,64,256]{2,1,0:T(8,128)}, f32[2,64,256]{2,1,0:T(8,128)}, f32[2,64,256]{2,1,0:T(8,128)}, f32[1,1]{1,0:T(1,128)}, f32[1,192]{1,0:T(1,128)}) custom-call(f32[192]{0:T(256)S(1)} %bitcast.16, f32[64,1,128]{2,1,0:T(1,128)S(1)} %all_to_all.15.sums, f32[2,64,256]{2,1,0:T(8,128)S(1)} %get-tuple-element.57.gradient, f32[2,64,256]{2,1,0:T(8,128)S(1)} %bitcast.12, ...), custom_call_target="tpu_custom_call" | custom-call | flops 13107200 | bytes 570112 | tf_op jit(solution)/shard_map/pallas_call | solution.py:29
  (16 shorter events, 0.1 us)
Async XLA Ops:
  0.6 0.9 copy-start.2
  1.5 11.8 %copy-start.7 = (f32[2048]{0:T(1024)S(1)}, f32[2048]{0:T(1024)}, u32[]{:S(2)}) copy-start(f32[2048]{0:T(1024)} %param.11) | copy-start | bytes 24580
  2.4 11.0 %copy-start = (bf16[128,2048]{1,0:T(8,128)(2,1)S(1)}, bf16[128,2048]{1,0:T(8,128)(2,1)}, u32[]{:S(2)}) copy-start(bf16[128,2048]{1,0:T(8,128)(2,1)} %tokens.1) | copy-start | bytes 1572868
  2.4 11.0 %copy-start.1 = (bf16[128,2048]{1,0:T(8,128)(2,1)S(1)}, bf16[128,2048]{1,0:T(8,128)(2,1)}, u32[]{:S(2)}) copy-start(bf16[128,2048]{1,0:T(8,128)(2,1)} %targets.1) | copy-start | bytes 1572868
  2.4 28.9 %all-to-all-start = ((bf16[8,2,64,256]{3,2,1,0:T(8,128)(2,1)}), bf16[8,2,64,256]{3,2,1,0:T(8,128)(2,1)S(1)}, u32[]{:S(2)}, u32[]{:S(2)}) async-start(bf16[8,2,64,256]{3,2,1,0:T(8,128)(2,1)} %shard_map.129), calls=%async_computation | async-start | bytes 1048576 | tf_op jit(solution)/shard_map/all_to_all | solution.py:255
  14.1 9.6 %collective-permute-start = (bf16[128,512]{1,0:T(8,128)(2,1)S(1)}, bf16[128,512]{1,0:T(8,128)(2,1)S(1)}, u32[]{:S(2)}, u32[]{:S(2)}) collective-permute-start(bf16[128,512]{1,0:T(8,128)(2,1)S(1)} %get-tuple-element.35), channel_id=1, source_target_pairs={{0,1},{1,0},{2,3},{3,2},{4,5},{5,4},{6,7},{7,6},{8,9},{9,8},{10,11... | collective-permute-start | bytes 393224 | tf_op jit(solution)/shard_map/ppermute | solution.py:251
  17.2 8.0 %collective-permute-start.1 = (bf16[128,512]{1,0:T(8,128)(2,1)S(1)}, bf16[128,512]{1,0:T(8,128)(2,1)S(1)}, u32[]{:S(2)}, u32[]{:S(2)}) collective-permute-start(bf16[128,512]{1,0:T(8,128)(2,1)S(1)} %get-tuple-element.36), channel_id=1, source_target_pairs={{0,2},{1,3},{2,0},{3,1},{4,6},{5,7},{6,4},{7,5},{8,10},{9,11},{10,... | collective-permute-start | bytes 393224 | tf_op jit(solution)/shard_map/ppermute | solution.py:251
  21.6 6.9 %collective-permute-start.2 = (bf16[128,512]{1,0:T(8,128)(2,1)S(1)}, bf16[128,512]{1,0:T(8,128)(2,1)S(1)}, u32[]{:S(2)}, u32[]{:S(2)}) collective-permute-start(bf16[128,512]{1,0:T(8,128)(2,1)S(1)} %get-tuple-element.37), channel_id=1, source_target_pairs={{0,3},{1,2},{2,1},{3,0},{4,7},{5,6},{6,5},{7,4},{8,11},{9,10},{10,... | collective-permute-start | bytes 393224 | tf_op jit(solution)/shard_map/ppermute | solution.py:251
  31.6 18.9 %collective-permute-start.5 = (bf16[768,256]{1,0:T(8,128)(2,1)S(1)}, bf16[768,256]{1,0:T(8,128)(2,1)S(1)}, u32[]{:S(2)}, u32[]{:S(2)}) collective-permute-start(bf16[768,256]{1,0:T(8,128)(2,1)S(1)} %get-tuple-element.41), channel_id=1, source_target_pairs={{0,3},{1,2},{2,1},{3,0},{4,7},{5,6},{6,5},{7,4},{8,11},{9,10},{10,... | collective-permute-start | bytes 1179656 | tf_op jit(solution)/shard_map/ppermute | solution.py:251
  36.0 9.0 %collective-permute-start.6 = (bf16[128,1024]{1,0:T(8,128)(2,1)S(1)}, bf16[128,1024]{1,0:T(8,128)(2,1)S(1)}, u32[]{:S(2)}, u32[]{:S(2)}) collective-permute-start(bf16[128,1024]{1,0:T(8,128)(2,1)S(1)} %get-tuple-element.43), channel_id=1, source_target_pairs={{0,1},{1,0},{2,3},{3,2},{4,5},{5,4},{6,7},{7,6},{8,9},{9,8},{10,11... | collective-permute-start | bytes 786440 | tf_op jit(solution)/shard_map/ppermute | solution.py:251
  38.0 9.9 %collective-permute-start.3 = (bf16[256,256]{1,0:T(8,128)(2,1)S(1)}, bf16[256,256]{1,0:T(8,128)(2,1)S(1)}, u32[]{:S(2)}, u32[]{:S(2)}) collective-permute-start(bf16[256,256]{1,0:T(8,128)(2,1)S(1)} %get-tuple-element.39), channel_id=1, source_target_pairs={{0,1},{1,0},{2,3},{3,2},{4,5},{5,4},{6,7},{7,6},{8,9},{9,8},{10,11... | collective-permute-start | bytes 393224 | tf_op jit(solution)/shard_map/ppermute | solution.py:251
  41.3 9.2 %collective-permute-start.4 = (bf16[256,256]{1,0:T(8,128)(2,1)S(1)}, bf16[256,256]{1,0:T(8,128)(2,1)S(1)}, u32[]{:S(2)}, u32[]{:S(2)}) collective-permute-start(bf16[256,256]{1,0:T(8,128)(2,1)S(1)} %get-tuple-element.40), channel_id=1, source_target_pairs={{0,2},{1,3},{2,0},{3,1},{4,6},{5,7},{6,4},{7,5},{8,10},{9,11},{10,... | collective-permute-start | bytes 393224 | tf_op jit(solution)/shard_map/ppermute | solution.py:251
  51.4 6.8 %collective-permute-start.7 = (bf16[256,256]{1,0:T(8,128)(2,1)S(1)}, bf16[256,256]{1,0:T(8,128)(2,1)S(1)}, u32[]{:S(2)}, u32[]{:S(2)}) collective-permute-start(bf16[256,256]{1,0:T(8,128)(2,1)S(1)} %get-tuple-element.45), channel_id=1, source_target_pairs={{0,1},{1,0},{2,3},{3,2},{4,5},{5,4},{6,7},{7,6},{8,9},{9,8},{10,11... | collective-permute-start | bytes 393224 | tf_op jit(solution)/shard_map/ppermute | solution.py:251
  53.8 13.0 %collective-permute-start.12 = (bf16[8,64,256]{2,1,0:T(8,128)(2,1)S(1)}, bf16[8,64,256]{2,1,0:T(8,128)(2,1)S(1)}, u32[]{:S(2)}, u32[]{:S(2)}) collective-permute-start(bf16[8,64,256]{2,1,0:T(8,128)(2,1)S(1)} %get-tuple-element.54), channel_id=1, source_target_pairs={{0,3},{1,2},{2,1},{3,0},{4,7},{5,6},{6,5},{7,4},{8,11},{9,10},{10,... | collective-permute-start | bytes 786440 | tf_op jit(solution)/shard_map/ppermute | solution.py:251
  58.3 8.6 %collective-permute-start.8 = (bf16[256,256]{1,0:T(8,128)(2,1)S(1)}, bf16[256,256]{1,0:T(8,128)(2,1)S(1)}, u32[]{:S(2)}, u32[]{:S(2)}) collective-permute-start(bf16[256,256]{1,0:T(8,128)(2,1)S(1)} %shard_map.132.back), channel_id=1, source_target_pairs={{0,3},{1,2},{2,1},{3,0},{4,7},{5,6},{6,5},{7,4},{8,11},{9,10},{10,... | collective-permute-start | bytes 393224 | tf_op jit(solution)/shard_map/ppermute | solution.py:251
  61.5 4.6 %collective-permute-start.9 = (f32[1,128]{1,0:T(1,128)S(1)}, f32[1,128]{1,0:T(1,128)S(1)}, u32[]{:S(2)}, u32[]{:S(2)}) collective-permute-start(f32[1,128]{1,0:T(1,128)S(1)} %get-tuple-element.47.a), channel_id=1, source_target_pairs={{0,64},{64,0},{128,192},{192,128},{256,320},{320,256},{384,448},{4... | collective-permute-start | bytes 1544 | tf_op jit(solution)/shard_map/ppermute | solution.py:251
  68.2 14.9 %copy-start.6 = (f32[8,192]{1,0:T(8,128)S(1)}, f32[8,192]{1,0:T(8,128)}, u32[]{:S(2)}) copy-start(f32[8,192]{1,0:T(8,128)} %perturbation.3) | copy-start | bytes 18436
  68.2 17.8 %all-to-all-start.1 = ((bf16[8,2,64,256]{3,2,1,0:T(8,128)(2,1)}), bf16[8,2,64,256]{3,2,1,0:T(8,128)(2,1)S(1)}, u32[]{:S(2)}, u32[]{:S(2)}) async-start(bf16[8,2,64,256]{3,2,1,0:T(8,128)(2,1)} %shard_map.138), calls=%async_computation.1 | async-start | bytes 1048576 | tf_op jit(solution)/shard_map/all_to_all | solution.py:255
  71.8 5.2 %collective-permute-start.10 = (f32[1,128]{1,0:T(1,128)S(1)}, f32[1,128]{1,0:T(1,128)S(1)}, u32[]{:S(2)}, u32[]{:S(2)}) collective-permute-start(f32[1,128]{1,0:T(1,128)S(1)} %shard_map.133.a), channel_id=1, source_target_pairs={{0,128},{64,192},{128,0},{192,64},{256,384},{320,448},{384,256},{4... | collective-permute-start | bytes 1544 | tf_op jit(solution)/shard_map/ppermute | solution.py:251
  77.0 6.0 %copy-start.9 = (f32[192]{0:T(256)S(1)}, f32[192]{0:T(256)}, u32[]{:S(2)}) copy-start(f32[192]{0:T(256)} %param.15) | copy-start | bytes 2308
  77.0 7.3 %collective-permute-start.11 = (f32[1,128]{1,0:T(1,128)S(1)}, f32[1,128]{1,0:T(1,128)S(1)}, u32[]{:S(2)}, u32[]{:S(2)}) collective-permute-start(f32[1,128]{1,0:T(1,128)S(1)} %shard_map.134.a), channel_id=1, source_target_pairs={{0,384},{64,448},{128,256},{192,320},{256,128},{320,192},{384,0},{... | collective-permute-start | bytes 1544 | tf_op jit(solution)/shard_map/ppermute | solution.py:251
  86.0 20.7 %copy-start.3 = (f32[1,2,64,256]{3,2,1,0:T(8,128)S(1)}, f32[1,2,64,256]{3,2,1,0:T(8,128)}, u32[]{:S(2)}) copy-start(f32[1,2,64,256]{3,2,1,0:T(8,128)} %param.12) | copy-start | bytes 393220
  86.0 20.7 %copy-start.4 = (f32[1,2,64,256]{3,2,1,0:T(8,128)S(1)}, f32[1,2,64,256]{3,2,1,0:T(8,128)}, u32[]{:S(2)}) copy-start(f32[1,2,64,256]{3,2,1,0:T(8,128)} %param.13) | copy-start | bytes 393220
  86.0 20.7 %copy-start.5 = (f32[1,2,64,256]{3,2,1,0:T(8,128)S(1)}, f32[1,2,64,256]{3,2,1,0:T(8,128)}, u32[]{:S(2)}) copy-start(f32[1,2,64,256]{3,2,1,0:T(8,128)} %param.14) | copy-start | bytes 393220
  86.2 20.6 %copy-start.8 = (f32[8,192]{1,0:T(8,128)S(1)}, f32[8,192]{1,0:T(8,128)}, u32[]{:S(2)}) copy-start(f32[8,192]{1,0:T(8,128)} %accumulated.1) | copy-start | bytes 18436

commit v9 on v8

--- a/solution.py
+++ b/solution.py
@@ -81,7 +81,8 @@
 
 
 def particle_index():
-    return lax.axis_index("y") * lax.axis_size("core") + lax.axis_index("core")
+    y = lax.axis_index("y_high") * lax.axis_size("y_low") + lax.axis_index("y_low")
+    return y * lax.axis_size("core") + lax.axis_index("core")
 
 
 def joined(mine, theirs, full):
@@ -165,7 +166,7 @@
 
 def total_kernel(received, losses, gradient, line):
     full = losses[...]
-    lane = lax.broadcasted_iota(jnp.int32, full.shape, 1) - 2 * lax.axis_index("core")
+    lane = lax.broadcasted_iota(jnp.int32, full.shape, 1) - 2 * lax.axis_index("y_low")
     for half in range(gradient.shape[0]):
         total = received[0, half].astype(f32)
         for i in range(1, received.shape[0]):
@@ -207,7 +208,7 @@
     total = jnp.sum(sums[...], axis=0)
     lane = lax.broadcasted_iota(jnp.int32, total.shape, 1)
     elements = D * RANK
-    mine = 2 * lax.axis_index("core")
+    mine = 2 * lax.axis_index("y_low")
     pairs = accumulated.shape[0]
     own_loss[...] = jnp.sum(jnp.where(lane == 4 + particle_index(), total, 0.0), axis=1, keepdims=True)
     row = lax.broadcasted_iota(jnp.int32, (pairs, total.shape[1]), 0)
@@ -310,14 +311,14 @@
     up_in = swap(send, "x", 3)
     (back,) = call(back_kernel, [thin], (back, received, slope), 2 * back.size)
     back_in = swap(back, "x", 3)
-    loss = plus(loss, swap(loss, "y", 1))
+    loss = plus(loss, swap(loss, "core", 1))
     back_in, loss = lax.optimization_barrier((back_in, loss))
     (terms,) = call(
         last_kernel, [((nz, *shape), bf16)], (back, back_in, *normed, up, up_in), product
     )
     terms = exchange(terms, "z")
-    loss = plus(loss, swap(loss, "y", 2))
-    loss = plus(loss, swap(loss, "y", 6))
+    loss = plus(loss, swap(loss, "y_high", 1))
+    loss = plus(loss, swap(loss, "y_high", 3))
     (learned,) = call(
         learned_kernel,
         [((1, learned_params.shape[0]), f32)],
@@ -328,11 +329,11 @@
     learned = learned.reshape(-1)
     gradient, line = call(
         total_kernel,
-        [(shape, f32), ((lax.axis_size("core") * nz * nx, 1, 128), f32)],
+        [(shape, f32), ((lax.axis_size("y_low") * nz * nx, 1, 128), f32)],
         (terms, loss),
         10 * terms.size,
     )
-    sums = exchange(line, ("core", "z", "x"))
+    sums = exchange(line, ("y_low", "z", "x"))
     new_w, new_m, new_v, own_loss, outer = call(
         update_kernel,
         [(shape, f32)] * 3 + [((1, 1), f32), ((1, learned.shape[0]), f32)],
@@ -352,8 +353,8 @@
 
 
 def solution(mesh):
-    grid = Mesh(mesh.devices.reshape(8, 2, 8, 4), ("y", "core", "z", "x"))
-    pop, shard = ("y", "core"), ("z", "x")
+    grid = Mesh(mesh.devices.reshape(4, 2, 2, 8, 4), ("y_high", "y_low", "core", "z", "x"))
+    pop, shard = ("y_high", "y_low", "core"), ("z", "x")
     return jax.shard_map(
         local,
         mesh=grid,

time: 111 us -> 112 us (level)
  the two profiles are of different devices: /device:TPU:1 before, /device:TPU:16 now
where the time goes in v9:
time: 112 us; the launch traced here: 111 us
  starting transfers between devices  58.8 us (52%)
  waiting for transfers between devices  24 us (21%)
  blocking collectives  18.5 us (17%)
  Pallas kernels  7.78 us (7%)
    ppermute x13, starting transfers between devices, swap(): return lax.ppermute(array, axis, pairs)  44.6 us
    ppermute x13, waiting for transfers between devices, swap(): return lax.ppermute(array, axis, pairs)  20.3 us
    all_to_all x1, blocking collectives, exchange(): return lax.all_to_all(array, axis, 0, 0, tiled=True)  18.5 us
    all_to_all x2, starting transfers between devices, exchange(): return lax.all_to_all(array, axis, 0, 0, tiled=True)  14.2 us
    pallas_call x13, Pallas kernels, call(): pl.pallas_call(kernel, out_shape=[jax.ShapeDtypeStruct(s, d) for s, d in...  7.78 us
    all_to_all x2, waiting for transfers between devices, exchange(): return lax.all_to_all(array, axis, 0, 0, tiled=True)  3.7 us
  transfers between devices with their start and end apart: 15, of which 11 were waited for; matrix products, arithmetic and copies ran while one was open for 0% of the time, Pallas kernels for 1%

profile of v9, /device:TPU:16, one launch (start us, length us, event | category | flops | bytes accessed | tf_op | source)
XLA Modules:
  0.0 110.9 jit_solution(17349815830918019837)
XLA Ops:
  0.6 0.0 copy-start.2
  0.6 0.9 copy-done.2
  1.5 0.8 shard_map.129
  2.4 10.4 %all-to-all-start = ((bf16[8,2,64,256]{3,2,1,0:T(8,128)(2,1)}), bf16[8,2,64,256]{3,2,1,0:T(8,128)(2,1)S(1)}, u32[]{:S(2)}, u32[]{:S(2)}) async-start(bf16[8,2,64,256]{3,2,1,0:T(8,128)(2,1)} %shard_map.129), calls=%async_computation | async-start | bytes 1048576 | tf_op jit(solution)/shard_map/all_to_all | solution.py:256
  12.8 0.0 copy-done.7
  12.8 0.0 copy-done
  12.9 0.0 copy-done.1
  12.9 0.7 shard_map.128
  13.5 3.4 %collective-permute-start = (bf16[128,512]{1,0:T(8,128)(2,1)S(1)}, bf16[128,512]{1,0:T(8,128)(2,1)S(1)}, u32[]{:S(2)}, u32[]{:S(2)}) collective-permute-start(bf16[128,512]{1,0:T(8,128)(2,1)S(1)} %get-tuple-element.35), channel_id=1, source_target_pairs={{0,1},{1,0},{2,3},{3,2},{4,5},{5,4},{6,7},{7,6},{8,9},{9,8},{10,11... | collective-permute-start | bytes 393224 | tf_op jit(solution)/shard_map/ppermute | solution.py:252
  17.0 4.6 %collective-permute-start.1 = (bf16[128,512]{1,0:T(8,128)(2,1)S(1)}, bf16[128,512]{1,0:T(8,128)(2,1)S(1)}, u32[]{:S(2)}, u32[]{:S(2)}) collective-permute-start(bf16[128,512]{1,0:T(8,128)(2,1)S(1)} %get-tuple-element.36), channel_id=1, source_target_pairs={{0,2},{1,3},{2,0},{3,1},{4,6},{5,7},{6,4},{7,5},{8,10},{9,11},{10,... | collective-permute-start | bytes 393224 | tf_op jit(solution)/shard_map/ppermute | solution.py:252
  21.6 2.4 %collective-permute-start.2 = (bf16[128,512]{1,0:T(8,128)(2,1)S(1)}, bf16[128,512]{1,0:T(8,128)(2,1)S(1)}, u32[]{:S(2)}, u32[]{:S(2)}) collective-permute-start(bf16[128,512]{1,0:T(8,128)(2,1)S(1)} %get-tuple-element.37), channel_id=1, source_target_pairs={{0,3},{1,2},{2,1},{3,0},{4,7},{5,6},{6,5},{7,4},{8,11},{9,10},{10,... | collective-permute-start | bytes 393224 | tf_op jit(solution)/shard_map/ppermute | solution.py:252
  24.0 0.0 collective-permute-done.n1
  24.0 1.4 %collective-permute-done.1.n2 = bf16[128,512]{1,0:T(8,128)(2,1)S(1)} collective-permute-done((bf16[128,512]{1,0:T(8,128)(2,1)S(1)}, bf16[128,512]{1,0:T(8,128)(2,1)S(1)}, u32[]{:S(2)}, u32[]{:S(2)}) %collective-permute-start.1) | collective-permute-done | bytes 131104 | tf_op jit(solution)/shard_map/ppermute | solution.py:252
  25.4 4.3 %collective-permute-done.2.n3 = bf16[128,512]{1,0:T(8,128)(2,1)S(1)} collective-permute-done((bf16[128,512]{1,0:T(8,128)(2,1)S(1)}, bf16[128,512]{1,0:T(8,128)(2,1)S(1)}, u32[]{:S(2)}, u32[]{:S(2)}) %collective-permute-start.2) | collective-permute-done | bytes 131104 | tf_op jit(solution)/shard_map/ppermute | solution.py:252
  29.7 0.7 all-to-all-done.gathered
  30.3 0.3 shard_map.130
  30.7 4.7 %collective-permute-start.5 = (bf16[768,256]{1,0:T(8,128)(2,1)S(1)}, bf16[768,256]{1,0:T(8,128)(2,1)S(1)}, u32[]{:S(2)}, u32[]{:S(2)}) collective-permute-start(bf16[768,256]{1,0:T(8,128)(2,1)S(1)} %get-tuple-element.41), channel_id=1, source_target_pairs={{0,3},{1,2},{2,1},{3,0},{4,7},{5,6},{6,5},{7,4},{8,11},{9,10},{10,... | collective-permute-start | bytes 1179656 | tf_op jit(solution)/shard_map/ppermute | solution.py:252
  35.3 2.1 %collective-permute-start.6 = (bf16[128,1024]{1,0:T(8,128)(2,1)S(1)}, bf16[128,1024]{1,0:T(8,128)(2,1)S(1)}, u32[]{:S(2)}, u32[]{:S(2)}) collective-permute-start(bf16[128,1024]{1,0:T(8,128)(2,1)S(1)} %get-tuple-element.43), channel_id=1, source_target_pairs={{0,1},{1,0},{2,3},{3,2},{4,5},{5,4},{6,7},{7,6},{8,9},{9,8},{10,11... | collective-permute-start | bytes 786440 | tf_op jit(solution)/shard_map/ppermute | solution.py:252
  37.5 3.7 %collective-permute-start.3 = (bf16[256,256]{1,0:T(8,128)(2,1)S(1)}, bf16[256,256]{1,0:T(8,128)(2,1)S(1)}, u32[]{:S(2)}, u32[]{:S(2)}) collective-permute-start(bf16[256,256]{1,0:T(8,128)(2,1)S(1)} %get-tuple-element.39), channel_id=1, source_target_pairs={{0,1},{1,0},{2,3},{3,2},{4,5},{5,4},{6,7},{7,6},{8,9},{9,8},{10,11... | collective-permute-start | bytes 393224 | tf_op jit(solution)/shard_map/ppermute | solution.py:252
  41.2 2.7 %collective-permute-start.4 = (bf16[256,256]{1,0:T(8,128)(2,1)S(1)}, bf16[256,256]{1,0:T(8,128)(2,1)S(1)}, u32[]{:S(2)}, u32[]{:S(2)}) collective-permute-start(bf16[256,256]{1,0:T(8,128)(2,1)S(1)} %get-tuple-element.40), channel_id=1, source_target_pairs={{0,2},{1,3},{2,0},{3,1},{4,6},{5,7},{6,4},{7,5},{8,10},{9,11},{10,... | collective-permute-start | bytes 393224 | tf_op jit(solution)/shard_map/ppermute | solution.py:252
  43.9 2.5 %collective-permute-done.6.d1 = bf16[128,1024]{1,0:T(8,128)(2,1)S(1)} collective-permute-done((bf16[128,1024]{1,0:T(8,128)(2,1)S(1)}, bf16[128,1024]{1,0:T(8,128)(2,1)S(1)}, u32[]{:S(2)}, u32[]{:S(2)}) %collective-permute-start.6) | collective-permute-done | bytes 262176 | tf_op jit(solution)/shard_map/ppermute | solution.py:252
  46.4 2.8 %collective-permute-done.3.r1 = bf16[256,256]{1,0:T(8,128)(2,1)S(1)} collective-permute-done((bf16[256,256]{1,0:T(8,128)(2,1)S(1)}, bf16[256,256]{1,0:T(8,128)(2,1)S(1)}, u32[]{:S(2)}, u32[]{:S(2)}) %collective-permute-start.3) | collective-permute-done | bytes 131104 | tf_op jit(solution)/shard_map/ppermute | solution.py:252
  49.2 1.5 %collective-permute-done.4.r2 = bf16[256,256]{1,0:T(8,128)(2,1)S(1)} collective-permute-done((bf16[256,256]{1,0:T(8,128)(2,1)S(1)}, bf16[256,256]{1,0:T(8,128)(2,1)S(1)}, u32[]{:S(2)}, u32[]{:S(2)}) %collective-permute-start.4) | collective-permute-done | bytes 131104 | tf_op jit(solution)/shard_map/ppermute | solution.py:252
  50.7 0.0 collective-permute-done.5.r3
  50.7 0.8 shard_map.131
  51.5 2.2 %collective-permute-start.7 = (bf16[256,256]{1,0:T(8,128)(2,1)S(1)}, bf16[256,256]{1,0:T(8,128)(2,1)S(1)}, u32[]{:S(2)}, u32[]{:S(2)}) collective-permute-start(bf16[256,256]{1,0:T(8,128)(2,1)S(1)} %get-tuple-element.45), channel_id=1, source_target_pairs={{0,1},{1,0},{2,3},{3,2},{4,5},{5,4},{6,7},{7,6},{8,9},{9,8},{10,11... | collective-permute-start | bytes 393224 | tf_op jit(solution)/shard_map/ppermute | solution.py:252
  53.7 0.5 shard_map.137
  54.2 4.4 %collective-permute-start.12 = (bf16[8,64,256]{2,1,0:T(8,128)(2,1)S(1)}, bf16[8,64,256]{2,1,0:T(8,128)(2,1)S(1)}, u32[]{:S(2)}, u32[]{:S(2)}) collective-permute-start(bf16[8,64,256]{2,1,0:T(8,128)(2,1)S(1)} %get-tuple-element.54), channel_id=1, source_target_pairs={{0,3},{1,2},{2,1},{3,0},{4,7},{5,6},{6,5},{7,4},{8,11},{9,10},{10,... | collective-permute-start | bytes 786440 | tf_op jit(solution)/shard_map/ppermute | solution.py:252
  58.6 0.0 collective-permute-done.7.received
  58.7 4.4 %collective-permute-start.8 = (bf16[256,256]{1,0:T(8,128)(2,1)S(1)}, bf16[256,256]{1,0:T(8,128)(2,1)S(1)}, u32[]{:S(2)}, u32[]{:S(2)}) collective-permute-start(bf16[256,256]{1,0:T(8,128)(2,1)S(1)} %shard_map.132.back), channel_id=1, source_target_pairs={{0,3},{1,2},{2,1},{3,0},{4,7},{5,6},{6,5},{7,4},{8,11},{9,10},{10,... | collective-permute-start | bytes 393224 | tf_op jit(solution)/shard_map/ppermute | solution.py:252
  63.1 1.9 %collective-permute-start.9 = (f32[1,128]{1,0:T(1,128)S(1)}, f32[1,128]{1,0:T(1,128)S(1)}, u32[]{:S(2)}, u32[]{:S(2)}) collective-permute-start(f32[1,128]{1,0:T(1,128)S(1)} %get-tuple-element.47.a), channel_id=1, source_target_pairs={{0,32},{32,0},{1,33},{33,1},{2,34},{34,2},{3,35},{35,3},{4,36},{36... | collective-permute-start | bytes 1544 | tf_op jit(solution)/shard_map/ppermute | solution.py:252
  65.0 1.1 %collective-permute-done.9.b = f32[1,128]{1,0:T(1,128)S(1)} collective-permute-done((f32[1,128]{1,0:T(1,128)S(1)}, f32[1,128]{1,0:T(1,128)S(1)}, u32[]{:S(2)}, u32[]{:S(2)}) %collective-permute-start.9) | collective-permute-done | bytes 544 | tf_op jit(solution)/shard_map/ppermute | solution.py:252
  66.2 0.8 collective-permute-done.8.received
  67.0 0.0 collective-permute-done.12.up_in
  67.0 1.3 %shard_map.138 = bf16[8,2,64,256]{3,2,1,0:T(8,128)(2,1)} custom-call(bf16[256,256]{1,0:T(8,128)(2,1)S(1)} %shard_map.132.back, bf16[256,256]{1,0:T(8,128)(2,1)S(1)} %collective-permute-done.8.received, bf16[128,512]{1,0:T(8,128)(2,1)S(1)} %get-tuple-element.34.n0, bf16[128,512]{1,0:T(8,128)(2,1)S(1)} %collective-permute-done.n1, ...), custom_call_target="tpu_custom_call" | custom-call | flops 134217728 | bytes 1572864 | tf_op jit(solution)/shard_map/pallas_call | solution.py:29
  68.3 3.8 %all-to-all-start.1 = ((bf16[8,2,64,256]{3,2,1,0:T(8,128)(2,1)}), bf16[8,2,64,256]{3,2,1,0:T(8,128)(2,1)S(1)}, u32[]{:S(2)}, u32[]{:S(2)}) async-start(bf16[8,2,64,256]{3,2,1,0:T(8,128)(2,1)} %shard_map.138), calls=%async_computation.1 | async-start | bytes 1048576 | tf_op jit(solution)/shard_map/all_to_all | solution.py:256
  72.1 2.2 %collective-permute-start.10 = (f32[1,128]{1,0:T(1,128)S(1)}, f32[1,128]{1,0:T(1,128)S(1)}, u32[]{:S(2)}, u32[]{:S(2)}) collective-permute-start(f32[1,128]{1,0:T(1,128)S(1)} %shard_map.133.a), channel_id=1, source_target_pairs={{0,128},{128,0},{256,384},{384,256},{1,129},{129,1},{257,385},{385... | collective-permute-start | bytes 1544 | tf_op jit(solution)/shard_map/ppermute | solution.py:252
  74.3 4.1 %collective-permute-done.10.b = f32[1,128]{1,0:T(1,128)S(1)} collective-permute-done((f32[1,128]{1,0:T(1,128)S(1)}, f32[1,128]{1,0:T(1,128)S(1)}, u32[]{:S(2)}, u32[]{:S(2)}) %collective-permute-start.10) | collective-permute-done | bytes 544 | tf_op jit(solution)/shard_map/ppermute | solution.py:252
  78.4 5.8 %collective-permute-start.11 = (f32[1,128]{1,0:T(1,128)S(1)}, f32[1,128]{1,0:T(1,128)S(1)}, u32[]{:S(2)}, u32[]{:S(2)}) collective-permute-start(f32[1,128]{1,0:T(1,128)S(1)} %shard_map.134.a), channel_id=1, source_target_pairs={{0,384},{128,256},{256,128},{384,0},{1,385},{129,257},{257,129},{3... | collective-permute-start | bytes 1544 | tf_op jit(solution)/shard_map/ppermute | solution.py:252
  84.2 0.0 copy-done.6
  84.3 1.8 %collective-permute-done.11.b = f32[1,128]{1,0:T(1,128)S(1)} collective-permute-done((f32[1,128]{1,0:T(1,128)S(1)}, f32[1,128]{1,0:T(1,128)S(1)}, u32[]{:S(2)}, u32[]{:S(2)}) %collective-permute-start.11) | collective-permute-done | bytes 544 | tf_op jit(solution)/shard_map/ppermute | solution.py:252
  86.1 3.0 %all-to-all-done.1.received = bf16[8,2,64,256]{3,2,1,0:T(8,128)(2,1)S(1)} async-done(((bf16[8,2,64,256]{3,2,1,0:T(8,128)(2,1)}), bf16[8,2,64,256]{3,2,1,0:T(8,128)(2,1)S(1)}, u32[]{:S(2)}, u32[]{:S(2)}) %all-to-all-start.1) | async-done | bytes 524320 | tf_op jit(solution)/shard_map/all_to_all | solution.py:256
  89.2 0.2 shard_map.139
  89.3 0.0 copy-start.8
  89.3 18.5 %all_to_all.15.sums = f32[64,1,128]{2,1,0:T(1,128)S(1)} all-to-all(f32[64,1,128]{2,1,0:T(1,128)S(1)} %get-tuple-element.56), channel_id=1, replica_groups=mesh['y_high'=4,'y_low'=2,'core'=2,'z'=8,'x'=4] {'y_low','z','x'}, dimensions={0} | all-to-all | bytes 65536 | tf_op jit(solution)/shard_map/all_to_all | solution.py:256
  107.9 0.0 copy-done.5
  107.9 0.0 copy-done.8
  107.9 3.0 %shard_map.140 = (f32[2,64,256]{2,1,0:T(8,128)}, f32[2,64,256]{2,1,0:T(8,128)}, f32[2,64,256]{2,1,0:T(8,128)}, f32[1,1]{1,0:T(1,128)}, f32[1,192]{1,0:T(1,128)}) custom-call(f32[192]{0:T(256)S(1)} %bitcast.16, f32[64,1,128]{2,1,0:T(1,128)S(1)} %all_to_all.15.sums, f32[2,64,256]{2,1,0:T(8,128)S(1)} %get-tuple-element.57.gradient, f32[2,64,256]{2,1,0:T(8,128)S(1)} %bitcast.12, ...), custom_call_target="tpu_custom_call" | custom-call | flops 13107200 | bytes 570112 | tf_op jit(solution)/shard_map/pallas_call | solution.py:29
  (16 shorter events, 0.1 us)
Async XLA Ops:
  0.6 0.9 copy-start.2
  1.5 11.3 %copy-start.7 = (f32[2048]{0:T(1024)S(1)}, f32[2048]{0:T(1024)}, u32[]{:S(2)}) copy-start(f32[2048]{0:T(1024)} %param.11) | copy-start | bytes 24580
  2.4 10.5 %copy-start = (bf16[128,2048]{1,0:T(8,128)(2,1)S(1)}, bf16[128,2048]{1,0:T(8,128)(2,1)}, u32[]{:S(2)}) copy-start(bf16[128,2048]{1,0:T(8,128)(2,1)} %tokens.1) | copy-start | bytes 1572868
  2.4 10.5 %copy-start.1 = (bf16[128,2048]{1,0:T(8,128)(2,1)S(1)}, bf16[128,2048]{1,0:T(8,128)(2,1)}, u32[]{:S(2)}) copy-start(bf16[128,2048]{1,0:T(8,128)(2,1)} %targets.1) | copy-start | bytes 1572868
  2.4 27.9 %all-to-all-start = ((bf16[8,2,64,256]{3,2,1,0:T(8,128)(2,1)}), bf16[8,2,64,256]{3,2,1,0:T(8,128)(2,1)S(1)}, u32[]{:S(2)}, u32[]{:S(2)}) async-start(bf16[8,2,64,256]{3,2,1,0:T(8,128)(2,1)} %shard_map.129), calls=%async_computation | async-start | bytes 1048576 | tf_op jit(solution)/shard_map/all_to_all | solution.py:256
  13.5 10.4 %collective-permute-start = (bf16[128,512]{1,0:T(8,128)(2,1)S(1)}, bf16[128,512]{1,0:T(8,128)(2,1)S(1)}, u32[]{:S(2)}, u32[]{:S(2)}) collective-permute-start(bf16[128,512]{1,0:T(8,128)(2,1)S(1)} %get-tuple-element.35), channel_id=1, source_target_pairs={{0,1},{1,0},{2,3},{3,2},{4,5},{5,4},{6,7},{7,6},{8,9},{9,8},{10,11... | collective-permute-start | bytes 393224 | tf_op jit(solution)/shard_map/ppermute | solution.py:252
  17.0 8.5 %collective-permute-start.1 = (bf16[128,512]{1,0:T(8,128)(2,1)S(1)}, bf16[128,512]{1,0:T(8,128)(2,1)S(1)}, u32[]{:S(2)}, u32[]{:S(2)}) collective-permute-start(bf16[128,512]{1,0:T(8,128)(2,1)S(1)} %get-tuple-element.36), channel_id=1, source_target_pairs={{0,2},{1,3},{2,0},{3,1},{4,6},{5,7},{6,4},{7,5},{8,10},{9,11},{10,... | collective-permute-start | bytes 393224 | tf_op jit(solution)/shard_map/ppermute | solution.py:252
  21.6 8.1 %collective-permute-start.2 = (bf16[128,512]{1,0:T(8,128)(2,1)S(1)}, bf16[128,512]{1,0:T(8,128)(2,1)S(1)}, u32[]{:S(2)}, u32[]{:S(2)}) collective-permute-start(bf16[128,512]{1,0:T(8,128)(2,1)S(1)} %get-tuple-element.37), channel_id=1, source_target_pairs={{0,3},{1,2},{2,1},{3,0},{4,7},{5,6},{6,5},{7,4},{8,11},{9,10},{10,... | collective-permute-start | bytes 393224 | tf_op jit(solution)/shard_map/ppermute | solution.py:252
  30.7 20.1 %collective-permute-start.5 = (bf16[768,256]{1,0:T(8,128)(2,1)S(1)}, bf16[768,256]{1,0:T(8,128)(2,1)S(1)}, u32[]{:S(2)}, u32[]{:S(2)}) collective-permute-start(bf16[768,256]{1,0:T(8,128)(2,1)S(1)} %get-tuple-element.41), channel_id=1, source_target_pairs={{0,3},{1,2},{2,1},{3,0},{4,7},{5,6},{6,5},{7,4},{8,11},{9,10},{10,... | collective-permute-start | bytes 1179656 | tf_op jit(solution)/shard_map/ppermute | solution.py:252
  35.3 11.1 %collective-permute-start.6 = (bf16[128,1024]{1,0:T(8,128)(2,1)S(1)}, bf16[128,1024]{1,0:T(8,128)(2,1)S(1)}, u32[]{:S(2)}, u32[]{:S(2)}) collective-permute-start(bf16[128,1024]{1,0:T(8,128)(2,1)S(1)} %get-tuple-element.43), channel_id=1, source_target_pairs={{0,1},{1,0},{2,3},{3,2},{4,5},{5,4},{6,7},{7,6},{8,9},{9,8},{10,11... | collective-permute-start | bytes 786440 | tf_op jit(solution)/shard_map/ppermute | solution.py:252
  37.5 11.7 %collective-permute-start.3 = (bf16[256,256]{1,0:T(8,128)(2,1)S(1)}, bf16[256,256]{1,0:T(8,128)(2,1)S(1)}, u32[]{:S(2)}, u32[]{:S(2)}) collective-permute-start(bf16[256,256]{1,0:T(8,128)(2,1)S(1)} %get-tuple-element.39), channel_id=1, source_target_pairs={{0,1},{1,0},{2,3},{3,2},{4,5},{5,4},{6,7},{7,6},{8,9},{9,8},{10,11... | collective-permute-start | bytes 393224 | tf_op jit(solution)/shard_map/ppermute | solution.py:252
  41.2 9.5 %collective-permute-start.4 = (bf16[256,256]{1,0:T(8,128)(2,1)S(1)}, bf16[256,256]{1,0:T(8,128)(2,1)S(1)}, u32[]{:S(2)}, u32[]{:S(2)}) collective-permute-start(bf16[256,256]{1,0:T(8,128)(2,1)S(1)} %get-tuple-element.40), channel_id=1, source_target_pairs={{0,2},{1,3},{2,0},{3,1},{4,6},{5,7},{6,4},{7,5},{8,10},{9,11},{10,... | collective-permute-start | bytes 393224 | tf_op jit(solution)/shard_map/ppermute | solution.py:252
  51.5 7.1 %collective-permute-start.7 = (bf16[256,256]{1,0:T(8,128)(2,1)S(1)}, bf16[256,256]{1,0:T(8,128)(2,1)S(1)}, u32[]{:S(2)}, u32[]{:S(2)}) collective-permute-start(bf16[256,256]{1,0:T(8,128)(2,1)S(1)} %get-tuple-element.45), channel_id=1, source_target_pairs={{0,1},{1,0},{2,3},{3,2},{4,5},{5,4},{6,7},{7,6},{8,9},{9,8},{10,11... | collective-permute-start | bytes 393224 | tf_op jit(solution)/shard_map/ppermute | solution.py:252
  54.2 12.7 %collective-permute-start.12 = (bf16[8,64,256]{2,1,0:T(8,128)(2,1)S(1)}, bf16[8,64,256]{2,1,0:T(8,128)(2,1)S(1)}, u32[]{:S(2)}, u32[]{:S(2)}) collective-permute-start(bf16[8,64,256]{2,1,0:T(8,128)(2,1)S(1)} %get-tuple-element.54), channel_id=1, source_target_pairs={{0,3},{1,2},{2,1},{3,0},{4,7},{5,6},{6,5},{7,4},{8,11},{9,10},{10,... | collective-permute-start | bytes 786440 | tf_op jit(solution)/shard_map/ppermute | solution.py:252
  58.7 8.3 %collective-permute-start.8 = (bf16[256,256]{1,0:T(8,128)(2,1)S(1)}, bf16[256,256]{1,0:T(8,128)(2,1)S(1)}, u32[]{:S(2)}, u32[]{:S(2)}) collective-permute-start(bf16[256,256]{1,0:T(8,128)(2,1)S(1)} %shard_map.132.back), channel_id=1, source_target_pairs={{0,3},{1,2},{2,1},{3,0},{4,7},{5,6},{6,5},{7,4},{8,11},{9,10},{10,... | collective-permute-start | bytes 393224 | tf_op jit(solution)/shard_map/ppermute | solution.py:252
  63.1 3.1 %collective-permute-start.9 = (f32[1,128]{1,0:T(1,128)S(1)}, f32[1,128]{1,0:T(1,128)S(1)}, u32[]{:S(2)}, u32[]{:S(2)}) collective-permute-start(f32[1,128]{1,0:T(1,128)S(1)} %get-tuple-element.47.a), channel_id=1, source_target_pairs={{0,32},{32,0},{1,33},{33,1},{2,34},{34,2},{3,35},{35,3},{4,36},{36... | collective-permute-start | bytes 1544 | tf_op jit(solution)/shard_map/ppermute | solution.py:252
  68.3 16.0 %copy-start.6 = (f32[8,192]{1,0:T(8,128)S(1)}, f32[8,192]{1,0:T(8,128)}, u32[]{:S(2)}) copy-start(f32[8,192]{1,0:T(8,128)} %perturbation.3) | copy-start | bytes 18436
  68.3 20.9 %all-to-all-start.1 = ((bf16[8,2,64,256]{3,2,1,0:T(8,128)(2,1)}), bf16[8,2,64,256]{3,2,1,0:T(8,128)(2,1)S(1)}, u32[]{:S(2)}, u32[]{:S(2)}) async-start(bf16[8,2,64,256]{3,2,1,0:T(8,128)(2,1)} %shard_map.138), calls=%async_computation.1 | async-start | bytes 1048576 | tf_op jit(solution)/shard_map/all_to_all | solution.py:256
  72.1 6.3 %collective-permute-start.10 = (f32[1,128]{1,0:T(1,128)S(1)}, f32[1,128]{1,0:T(1,128)S(1)}, u32[]{:S(2)}, u32[]{:S(2)}) collective-permute-start(f32[1,128]{1,0:T(1,128)S(1)} %shard_map.133.a), channel_id=1, source_target_pairs={{0,128},{128,0},{256,384},{384,256},{1,129},{129,1},{257,385},{385... | collective-permute-start | bytes 1544 | tf_op jit(solution)/shard_map/ppermute | solution.py:252
  78.4 5.8 %copy-start.9 = (f32[192]{0:T(256)S(1)}, f32[192]{0:T(256)}, u32[]{:S(2)}) copy-start(f32[192]{0:T(256)} %param.15) | copy-start | bytes 2308
  78.4 7.7 %collective-permute-start.11 = (f32[1,128]{1,0:T(1,128)S(1)}, f32[1,128]{1,0:T(1,128)S(1)}, u32[]{:S(2)}, u32[]{:S(2)}) collective-permute-start(f32[1,128]{1,0:T(1,128)S(1)} %shard_map.134.a), channel_id=1, source_target_pairs={{0,384},{128,256},{256,128},{384,0},{1,385},{129,257},{257,129},{3... | collective-permute-start | bytes 1544 | tf_op jit(solution)/shard_map/ppermute | solution.py:252
  89.1 18.7 %copy-start.3 = (f32[1,2,64,256]{3,2,1,0:T(8,128)S(1)}, f32[1,2,64,256]{3,2,1,0:T(8,128)}, u32[]{:S(2)}) copy-start(f32[1,2,64,256]{3,2,1,0:T(8,128)} %param.12) | copy-start | bytes 393220
  89.1 18.7 %copy-start.4 = (f32[1,2,64,256]{3,2,1,0:T(8,128)S(1)}, f32[1,2,64,256]{3,2,1,0:T(8,128)}, u32[]{:S(2)}) copy-start(f32[1,2,64,256]{3,2,1,0:T(8,128)} %param.13) | copy-start | bytes 393220
  89.1 18.7 %copy-start.5 = (f32[1,2,64,256]{3,2,1,0:T(8,128)S(1)}, f32[1,2,64,256]{3,2,1,0:T(8,128)}, u32[]{:S(2)}) copy-start(f32[1,2,64,256]{3,2,1,0:T(8,128)} %param.14) | copy-start | bytes 393220
  89.3 18.6 %copy-start.8 = (f32[8,192]{1,0:T(8,128)S(1)}, f32[8,192]{1,0:T(8,128)}, u32[]{:S(2)}) copy-start(f32[8,192]{1,0:T(8,128)} %accumulated.1) | copy-start | bytes 18436
